TPU v7x, 128 devices: a whole 4x4x4 slice. The times are simulated.
128 devices in a mesh: row: 64 (over z, y, x), col: 2 (over core).
Axes of the slice: x: 4, y: 4, z: 4, core: 2. Of those that a mesh axis runs over, the one named last changes fastest.
Arguments:
- pencil_left: bfloat16 [1, 64, 256, 4, 2, 256], P(None, 'row', None, None, 'col'), may hold values from -0.09375 to 0.09375
- pencil_right: bfloat16 [1, 64, 256, 4, 2, 256], P(None, 'row', None, None, 'col'), may hold values from -0.09375 to 0.09375
- basis_panel: bfloat16 [1, 64, 256, 4, 2, 256], P(None, 'row', None, None, 'col'), may hold values from -0.125 to 0.125
- block_inverses: float32 [4, 2, 256, 256], replicated, may hold values from -0.2 to 2.3
- pencil_shift: float32 [], replicated, may hold values from 0.5 to 1.5
- start_vectors: float32 [1, 64, 256, 512], P(None, 'row', None, 'col'), may hold values from -6 to 6
Outputs:
- pending: float32 [1, 64, 256, 512], P(None, 'row', None, 'col')
- image: float32 [1, 64, 256, 512], P(None, 'row', None, 'col')
All inputs are finite; a program needn't handle non-finite values.
Results may differ from a plain program's by a relative error of at most 0.0043.
Values may be sent and summed in bfloat16 or wider, within the bound.
No kernel may reach another device: no remote copies, remote signals or barrier semaphores. Data moves between devices by JAX's collectives and lax.ppermute only.
A program may use at most 64 MiB of HBM per device.

v0:
```python
import functools

import jax
import jax.numpy as jnp
from jax import lax
from jax.experimental import pallas as pl
from jax.experimental.pallas import tpu as pltpu
from jax.sharding import Mesh, PartitionSpec as P


STEPS = 8
HALF = STEPS // 2
NB = 256
WIDE = NB // 2
GROUPS = 8
ROWS = ("z", "yh", "yl", "xp", "xq")
FLIP = [(0, 1), (1, 0)]


def dot(a, b):
    return jnp.dot(a, b, preferred_element_type=jnp.float32)


def halves(a):
    high = a.astype(jnp.bfloat16)
    return high, (a - high.astype(jnp.float32)).astype(jnp.bfloat16)


def precise(a, b):
    (a1, a2), (b1, b2) = halves(a), halves(b)
    return dot(a1, b1) + (dot(a2, b1) + dot(a1, b2))


def pair_kernel(
    turn, arriving, where_ref, inv_ref, rhs_ref, mate_rhs_ref, own_ref, other_ref,
    mate3_ref, mate3_other_ref, mate_ref, mate_other_ref, *rest,
):
    *arrived, prev_ref, out_ref, x_ref = rest
    pair, odd, half, parity = (where_ref[i] for i in range(4))

    def less(accs, b, x):
        own, mate = accs
        mine, theirs = x[parity], x[1 - parity]
        near = (mate3_ref[0], mate3_other_ref[0]) if b == HALF - 1 else (mate_ref[b], mate_other_ref[b])
        own = own - (dot(own_ref[b], mine) + dot(other_ref[b], theirs))
        return own, mate - (dot(near[0], mine) + dot(near[1], theirs))

    @pl.when(pair == turn)
    def _():
        accs = rhs_ref[:, pl.ds(pl.multiple_of(half * WIDE, WIDE), WIDE)], mate_rhs_ref[...]
        for b, x in zip(arriving, arrived):
            accs = less(accs, b, x)
        high = jnp.where(odd == 1, *accs)
        x_high = precise(inv_ref[2 * turn + 1], high).astype(jnp.bfloat16)
        x_ref[0] = jnp.zeros_like(x_high)
        x_ref[1] = x_high
        accs = less(accs, turn, x_ref)
        low = jnp.where(odd == 0, *accs)
        out_ref[0] = precise(inv_ref[2 * turn], low).astype(jnp.bfloat16)
        out_ref[1] = x_high

    @pl.when(pair != turn)
    def _():
        out_ref[...] = prev_ref[...]


def final_kernel(
    where_ref, x_ref, w_own_ref, w_other_ref, z_own_ref, z_other_ref, rhs_ref, pending_ref, image_ref
):
    parity = where_ref[3]
    pending = rhs_ref[...]
    image = jnp.zeros_like(pending)
    for b in range(HALF):
        yl, xp = b // 2, b % 2
        for w, z, p in ((w_own_ref, z_own_ref, parity), (w_other_ref, z_other_ref, 1 - parity)):
            columns = []
            for half in range(2):
                at = [(((4 * p + i) * 2 + yl) * 2 + xp) * 2 + (half ^ xp) for i in range(4)]
                columns.append(jnp.concatenate([x_ref[n] for n in at], 0))
            x = jnp.concatenate(columns, 1)
            pending = pending - dot(w[b], x)
            image = image + dot(z[b], x)
    pending_ref[...] = pending
    image_ref[...] = image


def call(kernel, outs, scratch, *args, limit=24 << 20):
    vmem = pl.BlockSpec(memory_space=pltpu.VMEM)
    smem = pl.BlockSpec(memory_space=pltpu.SMEM)
    return pl.pallas_call(
        kernel,
        out_shape=outs,
        in_specs=[smem if a.dtype == jnp.int32 else vmem for a in args],
        out_specs=jax.tree.map(lambda _: vmem, outs),
        scratch_shapes=scratch,
        compiler_params=pltpu.CompilerParams(vmem_limit_bytes=limit),
    )(*args)


def to_pairs(a, moves):
    sends = []
    for src, dst in moves:
        for half in range(2):
            sends.append(tuple(2 * m + (half ^ (m % 2)) for m in (src, dst)))
    return lax.ppermute(a, ("yl", "xp", "xq"), sends)


def local(pencil_left, pencil_right, basis_panel, block_inverses, pencil_shift, start_vectors):
    row = lax.axis_index(ROWS)
    parity = lax.axis_index("col")
    pair = lax.axis_index(("yl", "xp"))
    odd = lax.axis_index("xq")
    half = odd ^ lax.axis_index("xp")
    where = jnp.stack([pair, odd, half, parity]).astype(jnp.int32)
    first = lax.axis_size(ROWS) - STEPS

    left = pencil_left.reshape(NB, HALF, NB)
    right = pencil_right.reshape(NB, HALF, NB)
    own_z = jnp.transpose(basis_panel.reshape(NB, HALF, NB), (1, 0, 2))
    rhs = start_vectors.reshape(NB, NB)
    inverses = block_inverses.reshape(STEPS, NB, NB)

    their_half = lax.dynamic_slice_in_dim(rhs, (1 - half) * WIDE, WIDE, 1)
    mate_rhs = lax.ppermute(their_half, "xq", FLIP)

    cols = 2 * jnp.arange(HALF) + parity
    live = (row < first + cols)[None, :, None]
    both = left.astype(jnp.float32) - pencil_shift * right.astype(jnp.float32)
    own_w = jnp.transpose(jnp.where(live, both, 0.0).astype(jnp.bfloat16), (1, 0, 2))

    mate3 = lax.ppermute(own_w[HALF - 1 :], "xq", FLIP)
    other_w = lax.ppermute(own_w, "col", FLIP)
    mate = lax.ppermute(own_w[: HALF - 1], "xq", FLIP)
    mate3_other = lax.ppermute(mate3, "col", FLIP)
    mate_other = lax.ppermute(mate, "col", FLIP)
    other_z = lax.ppermute(own_z, "col", FLIP)

    shape = jax.ShapeDtypeStruct((2, NB, WIDE), jnp.bfloat16)
    scratch = [pltpu.VMEM((2, NB, WIDE), jnp.bfloat16)]

    def solve(turn, arrivals, prev):
        return call(
            functools.partial(pair_kernel, turn, [b for b, _ in arrivals]), shape, scratch,
            where, inverses, rhs, mate_rhs, own_w, other_w, mate3, mate3_other,
            *((mate, mate_other) if turn < 3 else (mate3, mate3_other)),
            *[x for _, x in arrivals], prev,
        )

    x3 = solve(3, [], jnp.zeros(shape.shape, shape.dtype))
    a = to_pairs(x3, [(3, 2)])
    b = to_pairs(x3, [(3, 1)])
    x2 = solve(2, [(3, a)], x3)
    c = to_pairs(x2, [(2, 1), (3, 0)])
    d = to_pairs(x2, [(2, 0)])
    x1 = solve(1, [(3, b), (2, c)], x2)
    e = to_pairs(x1, [(1, 0)])
    x0 = solve(0, [(3, c), (2, d), (1, e)], x1)

    spread = lax.all_to_all(
        x0.reshape(GROUPS, 2 * NB // GROUPS, WIDE), ("z", "yh"), 0, 0, tiled=True
    )[GROUPS - 1]
    count = lax.axis_size(ROWS)
    every = lax.all_to_all(
        jnp.broadcast_to(spread[None], (count, *spread.shape)), ROWS, 0, 0, tiled=True
    )

    out = jax.ShapeDtypeStruct((NB, NB), jnp.float32)
    pending, image = call(
        final_kernel, (out, out), [],
        where, every, own_w, other_w, own_z, other_z, rhs,
    )
    return pending.reshape(1, 1, NB, NB), image.reshape(1, 1, NB, NB)


def solution(mesh):
    fine = Mesh(mesh.devices.reshape(4, 2, 2, 2, 2, 2), (*ROWS, "col"))
    wide = P(None, ROWS, None, None, "col", None)
    tall = P(None, ROWS, None, "col")
    return jax.shard_map(
        local, mesh=fine, in_specs=(wide, wide, wide, P(), P(), tall),
        out_specs=(tall, tall), check_vma=False,
    )
```

profile of v0, /device:TPU:0, one launch (start us, length us, event | category | flops | bytes accessed | tf_op | source)
XLA Modules:
  0.0 90.5 jit_solution(3678076207183622229)
XLA Ops:
  0.6 0.0 copy-start.1
  0.6 0.0 copy-start
  1.5 1.5 %fusion.1.own_ref.w_own_ref = bf16[4,256,256]{2,1,0:T(8,128)(2,1)S(1)} fusion(bf16[1,1,256,4,1,256]{5,3,4,2,1,0:T(4,128)(2,1)} %param.7, bf16[1,1,256,4,1,256]{5,3,4,2,1,0:T(4,128)(2,1)} %param.6, f32[]{:T(128)S(6)} %copy.15, pred[4]{0:T(512)(128)(4,1)S(1)} %add_compare_fusion), kind=kLoop, calls=%fused_computation.2 | loop fusion | flops 1572864 | bytes 1572872 | tf_op jit(solution)/shard_map/transpose | solution.py:129
  3.0 1.7 %collective-permute-start.4 = (bf16[3,256,256]{2,1,0:T(8,128)(2,1)S(1)}, bf16[3,256,256]{2,1,0:T(8,128)(2,1)}, u32[]{:S(2)}, u32[]{:S(2)}) collective-permute-start(bf16[3,256,256]{2,1,0:T(8,128)(2,1)S(1)} %slice.13), channel_id=1, source_target_pairs={{0,2},{2,0},{1,3},{3,1},{4,6},{6,4},{5,7},{7,5},{8,10},{10,8},{9,1... | collective-permute-start | bytes 1179656 | tf_op jit(solution)/shard_map/ppermute | solution.py:133
  4.7 0.0 collective-permute-start.1
  4.7 0.7 slice.12
  5.3 0.4 collective-permute-start.2
  5.7 9.4 %collective-permute-done.4.mate_ref = bf16[3,256,256]{2,1,0:T(8,128)(2,1)} collective-permute-done((bf16[3,256,256]{2,1,0:T(8,128)(2,1)S(1)}, bf16[3,256,256]{2,1,0:T(8,128)(2,1)}, u32[]{:S(2)}, u32[]{:S(2)}) %collective-permute-start.4) | collective-permute-done | bytes 393248 | tf_op jit(solution)/shard_map/ppermute | solution.py:133
  15.1 0.0 collective-permute-start.5
  15.1 0.0 copy-done.1
  15.2 0.7 dynamic-slice_bitcast_fusion
  15.8 1.6 %collective-permute-start = (f32[256,128]{1,0:T(8,128)}, f32[256,128]{1,0:T(8,128)}, u32[]{:S(2)}, u32[]{:S(2)}) collective-permute-start(f32[256,128]{1,0:T(8,128)} %dynamic-slice_bitcast_fusion), channel_id=1, source_target_pairs={{0,2},{2,0},{1,3},{3,1},{4,6},{6,4},{5,7},{7,5},{8,10},{10,8},{9,1... | collective-permute-start | bytes 393224 | tf_op jit(solution)/shard_map/ppermute | solution.py:124
  17.4 0.0 collective-permute-done.2.mate3_ref.mate_ref
  17.4 0.2 collective-permute-start.3
  17.6 0.1 pad_add_fusion.where_ref
  17.7 4.3 %collective-permute-done.mate_rhs_ref = f32[256,128]{1,0:T(8,128)} collective-permute-done((f32[256,128]{1,0:T(8,128)}, f32[256,128]{1,0:T(8,128)}, u32[]{:S(2)}, u32[]{:S(2)}) %collective-permute-start) | collective-permute-done | bytes 131104 | tf_op jit(solution)/shard_map/ppermute | solution.py:124
  22.0 0.0 collective-permute-done.3.mate3_other_ref.mate_other_ref
  22.0 0.0 collective-permute-done.1.other_ref.w_other_ref
  22.1 0.0 copy-done
  22.1 1.1 %shard_map.77.rest_1_ = bf16[2,256,128]{2,1,0:T(8,128)(2,1)S(1)} custom-call(s32[4]{0:T(128)S(1)} %pad_add_fusion.where_ref, f32[8,256,256]{2,1,0:T(8,128)S(1)} %bitcast.26, f32[256,256]{1,0:T(8,128)S(1)} %bitcast.30, f32[256,128]{1,0:T(8,128)} %collective-permute-done.mate_rhs_ref, bf16[4,256,256]{2,1,0:T(8,128)(2,1)S(1)} %fusion.1.own_ref.w_own_ref, ...), custom_call_target="tpu_custom_call" | custom-call | tf_op jit(solution)/shard_map/pallas_call | solution.py:90
  23.2 0.7 collective-permute-start.6
  23.8 0.7 collective-permute-start.9
  24.5 0.0 collective-permute-done.6.rest_0_
  24.5 0.0 collective-permute-done.5.mate_other_ref
  24.5 1.3 %shard_map.78.rest_2_ = bf16[2,256,128]{2,1,0:T(8,128)(2,1)S(1)} custom-call(s32[4]{0:T(128)S(1)} %pad_add_fusion.where_ref, f32[8,256,256]{2,1,0:T(8,128)S(1)} %bitcast.27, f32[256,256]{1,0:T(8,128)S(1)} %bitcast.31, f32[256,128]{1,0:T(8,128)} %collective-permute-done.mate_rhs_ref, bf16[4,256,256]{2,1,0:T(8,128)(2,1)S(1)} %fusion.1.own_ref.w_own_ref, ...), custom_call_target="tpu_custom_call" | custom-call | tf_op jit(solution)/shard_map/pallas_call | solution.py:90
  25.8 1.3 %collective-permute-start.7 = (bf16[2,256,128]{2,1,0:T(8,128)(2,1)S(1)}, bf16[2,256,128]{2,1,0:T(8,128)(2,1)S(1)}, u32[]{:S(2)}, u32[]{:S(2)}) collective-permute-start(bf16[2,256,128]{2,1,0:T(8,128)(2,1)S(1)} %shard_map.78.rest_2_), channel_id=1, source_target_pairs={{8,6},{10,4},{14,0},{12,2},{9,7},{11,5},{15,1},{13,3},{24,22},{26,... | collective-permute-start | bytes 393224 | tf_op jit(solution)/shard_map/ppermute | solution.py:105
  27.1 1.3 %collective-permute-start.8 = (bf16[2,256,128]{2,1,0:T(8,128)(2,1)S(1)}, bf16[2,256,128]{2,1,0:T(8,128)(2,1)S(1)}, u32[]{:S(2)}, u32[]{:S(2)}) collective-permute-start(bf16[2,256,128]{2,1,0:T(8,128)(2,1)S(1)} %shard_map.78.rest_2_), channel_id=1, source_target_pairs={{8,0},{10,2},{9,1},{11,3},{24,16},{26,18},{25,17},{27,19},{40,32},... | collective-permute-start | bytes 393224 | tf_op jit(solution)/shard_map/ppermute | solution.py:105
  28.4 0.0 collective-permute-done.9.rest_0_
  28.4 9.1 %collective-permute-done.7.rest_1_.rest_0_ = bf16[2,256,128]{2,1,0:T(8,128)(2,1)S(1)} collective-permute-done((bf16[2,256,128]{2,1,0:T(8,128)(2,1)S(1)}, bf16[2,256,128]{2,1,0:T(8,128)(2,1)S(1)}, u32[]{:S(2)}, u32[]{:S(2)}) %collective-permute-start.7) | collective-permute-done | bytes 131104 | tf_op jit(solution)/shard_map/ppermute | solution.py:105
  37.5 1.3 %shard_map.79.rest_3_ = bf16[2,256,128]{2,1,0:T(8,128)(2,1)S(1)} custom-call(s32[4]{0:T(128)S(1)} %pad_add_fusion.where_ref, f32[8,256,256]{2,1,0:T(8,128)S(1)} %bitcast.28, f32[256,256]{1,0:T(8,128)S(1)} %bitcast.32, f32[256,128]{1,0:T(8,128)} %collective-permute-done.mate_rhs_ref, bf16[4,256,256]{2,1,0:T(8,128)(2,1)S(1)} %fusion.1.own_ref.w_own_ref, ...), custom_call_target="tpu_custom_call" | custom-call | tf_op jit(solution)/shard_map/pallas_call | solution.py:90
  38.8 1.3 %collective-permute-start.10 = (bf16[2,256,128]{2,1,0:T(8,128)(2,1)S(1)}, bf16[2,256,128]{2,1,0:T(8,128)(2,1)S(1)}, u32[]{:S(2)}, u32[]{:S(2)}) collective-permute-start(bf16[2,256,128]{2,1,0:T(8,128)(2,1)S(1)} %shard_map.79.rest_3_), channel_id=1, source_target_pairs={{6,0},{4,2},{7,1},{5,3},{22,16},{20,18},{23,17},{21,19},{38,32},{3... | collective-permute-start | bytes 393224 | tf_op jit(solution)/shard_map/ppermute | solution.py:105
  40.1 0.9 collective-permute-done.8.rest_1_
  41.0 8.1 %collective-permute-done.10.rest_2_ = bf16[2,256,128]{2,1,0:T(8,128)(2,1)S(1)} collective-permute-done((bf16[2,256,128]{2,1,0:T(8,128)(2,1)S(1)}, bf16[2,256,128]{2,1,0:T(8,128)(2,1)S(1)}, u32[]{:S(2)}, u32[]{:S(2)}) %collective-permute-start.10) | collective-permute-done | bytes 131104 | tf_op jit(solution)/shard_map/ppermute | solution.py:105
  49.1 2.7 %shard_map.80 = bf16[2,256,128]{2,1,0:T(8,128)(2,1)S(1)} custom-call(s32[4]{0:T(128)S(1)} %pad_add_fusion.where_ref, f32[8,256,256]{2,1,0:T(8,128)S(1)} %bitcast.29, f32[256,256]{1,0:T(8,128)S(1)} %bitcast.33, f32[256,128]{1,0:T(8,128)} %collective-permute-done.mate_rhs_ref, bf16[4,256,256]{2,1,0:T(8,128)(2,1)S(1)} %fusion.1.own_ref.w_own_ref, ...), custom_call_target="tpu_custom_call" | custom-call | tf_op jit(solution)/shard_map/pallas_call | solution.py:90
  51.8 0.0 copy-start.2
  51.8 15.8 %all_to_all.10 = bf16[8,64,128]{2,1,0:T(8,128)(2,1)S(1)} all-to-all(bf16[8,64,128]{2,1,0:T(8,128)(2,1)S(1)} %bitcast.37), channel_id=1, replica_groups=mesh['z'=4,'yh'=2,'yl'=2,'xp'=2,'xq'=2,'col'=2] {'z','yh'}, dimensions={0} | all-to-all | bytes 262144 | tf_op jit(solution)/shard_map/all_to_all | solution.py:159
  67.6 1.2 %broadcast_in_dim.27 = bf16[64,64,128]{2,1,0:T(8,128)(2,1)} broadcast(bf16[64,128]{1,0:T(8,128)(2,1)S(1)} %slice_bitcast_fusion), dimensions={1,2} | broadcast | bytes 1064960 | tf_op jit(solution)/shard_map/broadcast_in_dim | solution.py:164
  68.8 4.7 %all-to-all-start.1 = ((bf16[64,64,128]{2,1,0:T(8,128)(2,1)}), bf16[64,64,128]{2,1,0:T(8,128)(2,1)S(1)}, u32[]{:S(2)}, u32[]{:S(2)}) async-start(bf16[64,64,128]{2,1,0:T(8,128)(2,1)} %broadcast_in_dim.27), calls=%async_computation.1 | async-start | bytes 2097152 | tf_op jit(solution)/shard_map/all_to_all | solution.py:163
  73.5 0.0 copy-done.2
  73.5 0.1 copy.14
  73.6 0.1 collective-permute-start.11
  73.7 1.9 %collective-permute-done.11.z_other_ref = bf16[4,256,256]{2,1,0:T(8,128)(2,1)S(1)} collective-permute-done((bf16[4,256,256]{2,1,0:T(8,128)(2,1)S(1)}, bf16[4,256,256]{2,1,0:T(8,128)(2,1)S(1)}, u32[]{:S(2)}, u32[]{:S(2)}) %collective-permute-start.11) | collective-permute-done | bytes 524320 | tf_op jit(solution)/shard_map/ppermute | solution.py:136
  75.5 12.9 %all-to-all-done.1.x_ref = bf16[64,64,128]{2,1,0:T(8,128)(2,1)S(1)} async-done(((bf16[64,64,128]{2,1,0:T(8,128)(2,1)}), bf16[64,64,128]{2,1,0:T(8,128)(2,1)S(1)}, u32[]{:S(2)}, u32[]{:S(2)}) %all-to-all-start.1) | async-done | bytes 1048608 | tf_op jit(solution)/shard_map/all_to_all | solution.py:163
  88.5 2.1 %shard_map.81 = (f32[256,256]{1,0:T(8,128)}, f32[256,256]{1,0:T(8,128)}) custom-call(s32[4]{0:T(128)S(1)} %pad_add_fusion.where_ref, bf16[64,64,128]{2,1,0:T(8,128)(2,1)S(1)} %all-to-all-done.1.x_ref, bf16[4,256,256]{2,1,0:T(8,128)(2,1)S(1)} %fusion.1.own_ref.w_own_ref, bf16[4,256,256]{2,1,0:T(8,128)(2,1)S(1)} %collective-permute-done.1.other_ref.w_other_ref, ...), custom_call_target="tpu_custom_call" | custom-call | tf_op jit(solution)/shard_map/pallas_call | solution.py:90
  (4 shorter events, 0.1 us)
Async XLA Ops:
  0.6 14.5 %copy-start.1 = (f32[1,1,256,256]{3,2,1,0:T(8,128)S(1)}, f32[1,1,256,256]{3,2,1,0:T(8,128)}, u32[]{:S(2)}) copy-start(f32[1,1,256,256]{3,2,1,0:T(8,128)} %param.11) | copy-start | bytes 786436
  0.6 21.4 %copy-start = (f32[4,2,256,256]{3,2,1,0:T(8,128)S(1)}, f32[4,2,256,256]{3,2,1,0:T(8,128)}, u32[]{:S(2)}) copy-start(f32[4,2,256,256]{3,2,1,0:T(8,128)} %param.9) | copy-start | bytes 6291460
  3.0 12.2 %collective-permute-start.4 = (bf16[3,256,256]{2,1,0:T(8,128)(2,1)S(1)}, bf16[3,256,256]{2,1,0:T(8,128)(2,1)}, u32[]{:S(2)}, u32[]{:S(2)}) collective-permute-start(bf16[3,256,256]{2,1,0:T(8,128)(2,1)S(1)} %slice.13), channel_id=1, source_target_pairs={{0,2},{2,0},{1,3},{3,1},{4,6},{6,4},{5,7},{7,5},{8,10},{10,8},{9,1... | collective-permute-start | bytes 1179656 | tf_op jit(solution)/shard_map/ppermute | solution.py:133
  4.7 17.4 %collective-permute-start.1 = (bf16[4,256,256]{2,1,0:T(8,128)(2,1)S(1)}, bf16[4,256,256]{2,1,0:T(8,128)(2,1)S(1)}, u32[]{:S(2)}, u32[]{:S(2)}) collective-permute-start(bf16[4,256,256]{2,1,0:T(8,128)(2,1)S(1)} %fusion.1.own_ref.w_own_ref), channel_id=1, source_target_pairs={{0,1},{1,0},{2,3},{3,2},{4,5},{5,4},{6,7},{7,6},{8,9},{9,8},{10,11... | collective-permute-start | bytes 1572872 | tf_op jit(solution)/shard_map/ppermute | solution.py:132
  5.3 12.1 %collective-permute-start.2 = (bf16[1,256,256]{2,1,0:T(8,128)(2,1)}, bf16[1,256,256]{2,1,0:T(8,128)(2,1)S(1)}, u32[]{:S(2)}, u32[]{:S(2)}) collective-permute-start(bf16[1,256,256]{2,1,0:T(8,128)(2,1)} %slice.12), channel_id=1, source_target_pairs={{0,2},{2,0},{1,3},{3,1},{4,6},{6,4},{5,7},{7,5},{8,10},{10,8},{9,1... | collective-permute-start | bytes 393224 | tf_op jit(solution)/shard_map/ppermute | solution.py:131
  15.1 9.4 %collective-permute-start.5 = (bf16[3,256,256]{2,1,0:T(8,128)(2,1)}, bf16[3,256,256]{2,1,0:T(8,128)(2,1)}, u32[]{:S(2)}, u32[]{:S(2)}) collective-permute-start(bf16[3,256,256]{2,1,0:T(8,128)(2,1)} %collective-permute-done.4.mate_ref), channel_id=1, source_target_pairs={{0,1},{1,0},{2,3},{3,2},{4,5},{5,4},{6,7},{7,6},{8,9},{9,8},{10,11... | collective-permute-start | bytes 1179656 | tf_op jit(solution)/shard_map/ppermute | solution.py:135
  15.8 6.2 %collective-permute-start = (f32[256,128]{1,0:T(8,128)}, f32[256,128]{1,0:T(8,128)}, u32[]{:S(2)}, u32[]{:S(2)}) collective-permute-start(f32[256,128]{1,0:T(8,128)} %dynamic-slice_bitcast_fusion), channel_id=1, source_target_pairs={{0,2},{2,0},{1,3},{3,1},{4,6},{6,4},{5,7},{7,5},{8,10},{10,8},{9,1... | collective-permute-start | bytes 393224 | tf_op jit(solution)/shard_map/ppermute | solution.py:124
  17.4 4.6 %collective-permute-start.3 = (bf16[1,256,256]{2,1,0:T(8,128)(2,1)S(1)}, bf16[1,256,256]{2,1,0:T(8,128)(2,1)}, u32[]{:S(2)}, u32[]{:S(2)}) collective-permute-start(bf16[1,256,256]{2,1,0:T(8,128)(2,1)S(1)} %collective-permute-done.2.mate3_ref.mate_ref), channel_id=1, source_target_pairs={{0,1},{1,0},{2,3},{3,2},{4,5},{5,4},{6,7},{7,6},{8,9},{9,8},{10,11... | collective-permute-start | bytes 393224 | tf_op jit(solution)/shard_map/ppermute | solution.py:134
  23.2 1.4 %collective-permute-start.6 = (bf16[2,256,128]{2,1,0:T(8,128)(2,1)S(1)}, bf16[2,256,128]{2,1,0:T(8,128)(2,1)S(1)}, u32[]{:S(2)}, u32[]{:S(2)}) collective-permute-start(bf16[2,256,128]{2,1,0:T(8,128)(2,1)S(1)} %shard_map.77.rest_1_), channel_id=1, source_target_pairs={{14,8},{12,10},{15,9},{13,11},{30,24},{28,26},{31,25},{29,27},{46,... | collective-permute-start | bytes 393224 | tf_op jit(solution)/shard_map/ppermute | solution.py:105
  23.8 4.6 %collective-permute-start.9 = (bf16[2,256,128]{2,1,0:T(8,128)(2,1)S(1)}, bf16[2,256,128]{2,1,0:T(8,128)(2,1)S(1)}, u32[]{:S(2)}, u32[]{:S(2)}) collective-permute-start(bf16[2,256,128]{2,1,0:T(8,128)(2,1)S(1)} %shard_map.77.rest_1_), channel_id=1, source_target_pairs={{14,6},{12,4},{15,7},{13,5},{30,22},{28,20},{31,23},{29,21},{46,38... | collective-permute-start | bytes 393224 | tf_op jit(solution)/shard_map/ppermute | solution.py:105
  25.8 11.7 %collective-permute-start.7 = (bf16[2,256,128]{2,1,0:T(8,128)(2,1)S(1)}, bf16[2,256,128]{2,1,0:T(8,128)(2,1)S(1)}, u32[]{:S(2)}, u32[]{:S(2)}) collective-permute-start(bf16[2,256,128]{2,1,0:T(8,128)(2,1)S(1)} %shard_map.78.rest_2_), channel_id=1, source_target_pairs={{8,6},{10,4},{14,0},{12,2},{9,7},{11,5},{15,1},{13,3},{24,22},{26,... | collective-permute-start | bytes 393224 | tf_op jit(solution)/shard_map/ppermute | solution.py:105
  27.1 13.8 %collective-permute-start.8 = (bf16[2,256,128]{2,1,0:T(8,128)(2,1)S(1)}, bf16[2,256,128]{2,1,0:T(8,128)(2,1)S(1)}, u32[]{:S(2)}, u32[]{:S(2)}) collective-permute-start(bf16[2,256,128]{2,1,0:T(8,128)(2,1)S(1)} %shard_map.78.rest_2_), channel_id=1, source_target_pairs={{8,0},{10,2},{9,1},{11,3},{24,16},{26,18},{25,17},{27,19},{40,32},... | collective-permute-start | bytes 393224 | tf_op jit(solution)/shard_map/ppermute | solution.py:105
  38.8 10.3 %collective-permute-start.10 = (bf16[2,256,128]{2,1,0:T(8,128)(2,1)S(1)}, bf16[2,256,128]{2,1,0:T(8,128)(2,1)S(1)}, u32[]{:S(2)}, u32[]{:S(2)}) collective-permute-start(bf16[2,256,128]{2,1,0:T(8,128)(2,1)S(1)} %shard_map.79.rest_3_), channel_id=1, source_target_pairs={{6,0},{4,2},{7,1},{5,3},{22,16},{20,18},{23,17},{21,19},{38,32},{3... | collective-permute-start | bytes 393224 | tf_op jit(solution)/shard_map/ppermute | solution.py:105
  51.8 21.7 %copy-start.2 = (bf16[1,1,256,4,1,256]{5,3,4,2,1,0:T(4,128)(2,1)S(1)}, bf16[1,1,256,4,1,256]{5,3,4,2,1,0:T(4,128)(2,1)}, u32[]{:S(2)}) copy-start(bf16[1,1,256,4,1,256]{5,3,4,2,1,0:T(4,128)(2,1)} %param.8) | copy-start | bytes 1572868
  68.8 19.7 %all-to-all-start.1 = ((bf16[64,64,128]{2,1,0:T(8,128)(2,1)}), bf16[64,64,128]{2,1,0:T(8,128)(2,1)S(1)}, u32[]{:S(2)}, u32[]{:S(2)}) async-start(bf16[64,64,128]{2,1,0:T(8,128)(2,1)} %broadcast_in_dim.27), calls=%async_computation.1 | async-start | bytes 2097152 | tf_op jit(solution)/shard_map/all_to_all | solution.py:163
  73.6 2.0 %collective-permute-start.11 = (bf16[4,256,256]{2,1,0:T(8,128)(2,1)S(1)}, bf16[4,256,256]{2,1,0:T(8,128)(2,1)S(1)}, u32[]{:S(2)}, u32[]{:S(2)}) collective-permute-start(bf16[4,256,256]{2,1,0:T(8,128)(2,1)S(1)} %bitcast.35), channel_id=1, source_target_pairs={{0,1},{1,0},{2,3},{3,2},{4,5},{5,4},{6,7},{7,6},{8,9},{9,8},{10,11... | collective-permute-start | bytes 1572872 | tf_op jit(solution)/shard_map/ppermute | solution.py:136
where the time goes:
time: 91 us; the launch traced here: 90.5 us
  waiting for transfers between devices  46.6 us (51%)
  blocking collectives  15.8 us (17%)
  starting transfers between devices  13.9 us (15%)
  Pallas kernels  8.35 us (9%)
  local copies, waits for them, and re-layouts  2.71 us (3%)
  between operations  1.64 us (2%)
  other arithmetic  1.54 us (2%)
    ppermute x5, waiting for transfers between devices, to_pairs(): return lax.ppermute(a, ('yl', 'xp', 'xq'), sends)  18.1 us
    all_to_all x1, blocking collectives, local(): lax.all_to_all(x0.reshape(GROUPS, 2 * NB // GROUPS, WIDE), ('z', 'yh'), 0...  15.8 us
    all_to_all x1, waiting for transfers between devices, local(): lax.all_to_all(jnp.broadcast_to(spread[None], (count, *spread.shape)), RO...  12.9 us
    ppermute x1, waiting for transfers between devices, local(): mate = lax.ppermute(own_w[:HALF - 1], 'xq', FLIP)  9.4 us
    pallas_call x5, Pallas kernels, call(): pl.pallas_call(kernel, out_shape=outs, in_specs=[smem if a.dtype == jnp.i...  8.35 us
    ppermute x5, starting transfers between devices, to_pairs(): return lax.ppermute(a, ('yl', 'xp', 'xq'), sends)  5.21 us
    all_to_all x1, starting transfers between devices, local(): lax.all_to_all(jnp.broadcast_to(spread[None], (count, *spread.shape)), RO...  4.65 us
    ppermute x1, waiting for transfers between devices, local(): mate_rhs = lax.ppermute(their_half, 'xq', FLIP)  4.31 us
  transfers between devices with their start and end apart: 13, of which 7 were waited for; matrix products, arithmetic and copies ran while one was open for 2% of the time, Pallas kernels for 4%

commit v1 on v0

v1 whole, which is shorter than its diff:
```python
import functools

import jax
import jax.numpy as jnp
from jax import lax
from jax.experimental import pallas as pl
from jax.experimental.pallas import tpu as pltpu
from jax.sharding import Mesh, PartitionSpec as P


STEPS = 8
HALF = STEPS // 2
NB = 256
WIDE = NB // 2
GROUPS = 8
ROWS = ("z", "yh", "yl", "xp", "xq")
FLIP = [(0, 1), (1, 0)]


def dot(a, b):
    return jnp.dot(a, b, preferred_element_type=jnp.float32)


def halves(a):
    high = a.astype(jnp.bfloat16)
    return high, (a - high.astype(jnp.float32)).astype(jnp.bfloat16)


def lead_kernel(where_ref, inv_ref, rhs_ref, inv_out_ref, rhs_out_ref):
    pair, half = where_ref[0], where_ref[2]
    rhs_out_ref[...] = jnp.where(half == 0, rhs_ref[:, WIDE:], rhs_ref[:, :WIDE])
    for e in range(2):
        inv_out_ref[e, 0], inv_out_ref[e, 1] = halves(inv_ref[pair, e])


def precise(inv_ref, e, b):
    high, low = halves(b)
    return dot(inv_ref[e, 0], high) + (dot(inv_ref[e, 1], high) + dot(inv_ref[e, 0], low))


def pair_kernel(
    turn, arriving, early, where_ref, inv_ref, rhs_ref, mate_rhs_ref,
    own_ref, other3_ref, mate3_ref, mate3_other_ref, *rest,
):
    if turn < HALF - 1:
        other_ref, mate_ref, mate_other_ref, *rest = rest
    *seen, acc_ref, prev_ref, out_ref, sum_ref = rest
    pair, odd, half, parity = (where_ref[i] for i in range(4))

    def blocks(b):
        if b == HALF - 1:
            return own_ref[b], other3_ref[0], mate3_ref[0], mate3_other_ref[0]
        return own_ref[b], other_ref[b], mate_ref[b], mate_other_ref[b]

    def less(accs, b, x):
        own, other, mate, mate_other = blocks(b)
        mine, theirs = x[parity], x[1 - parity]
        return (
            accs[0] - (dot(own, mine) + dot(other, theirs)),
            accs[1] - (dot(mate, mine) + dot(mate_other, theirs)),
        )

    def fresh():
        return rhs_ref[:, pl.ds(pl.multiple_of(half * WIDE, WIDE), WIDE)], mate_rhs_ref[...]

    @pl.when(pair == turn)
    def _():
        accs = fresh() if turn >= HALF - 2 else (acc_ref[0], acc_ref[1])
        for b, x in zip(arriving, seen):
            accs = less(accs, b, x)
        high = jnp.where(odd == 1, *accs)
        own, other, mate, mate_other = blocks(turn)
        between = jnp.where(
            odd == 0, jnp.where(parity == 1, own, other), jnp.where(parity == 1, mate, mate_other)
        )
        x_high = precise(inv_ref, 1, high).astype(jnp.bfloat16)
        low = jnp.where(odd == 0, *accs) - dot(between, x_high)
        out_ref[0] = precise(inv_ref, 0, low).astype(jnp.bfloat16)
        out_ref[1] = x_high

    @pl.when(pair != turn)
    def _():
        out_ref[...] = prev_ref[...]

    @pl.when(pair == turn - 1)
    def _():
        accs = fresh()
        for b, x in zip(early, seen[len(arriving) :]):
            accs = less(accs, b, x)
        sum_ref[0], sum_ref[1] = accs


def final_kernel(
    where_ref, x_ref, w_own_ref, w3_other_ref, w_other_ref, z_own_ref, z_other_ref,
    rhs_ref, pending_ref, image_ref,
):
    parity = where_ref[3]
    pending = rhs_ref[...]
    image = jnp.zeros_like(pending)
    for b in range(HALF):
        yl, xp = b // 2, b % 2
        own, other = w_own_ref[b], w3_other_ref[0] if b == HALF - 1 else w_other_ref[b]
        for w, z, p in ((own, z_own_ref, parity), (other, z_other_ref, 1 - parity)):
            columns = []
            for half in range(2):
                at = [(((4 * p + i) * 2 + yl) * 2 + xp) * 2 + (half ^ xp) for i in range(4)]
                columns.append(jnp.concatenate([x_ref[n] for n in at], 0))
            x = jnp.concatenate(columns, 1)
            pending = pending - dot(w, x)
            image = image + dot(z[b], x)
    pending_ref[...] = pending
    image_ref[...] = image


def call(kernel, outs, scratch, *args, limit=12 << 20):
    vmem = pl.BlockSpec(memory_space=pltpu.VMEM)
    smem = pl.BlockSpec(memory_space=pltpu.SMEM)
    return pl.pallas_call(
        kernel,
        out_shape=outs,
        in_specs=[smem if a.dtype == jnp.int32 else vmem for a in args],
        out_specs=jax.tree.map(lambda _: vmem, outs),
        scratch_shapes=scratch,
        compiler_params=pltpu.CompilerParams(vmem_limit_bytes=limit),
    )(*args)


def to_pairs(a, moves):
    sends = []
    for src, dst in moves:
        for half in range(2):
            sends.append(tuple(2 * m + (half ^ (m % 2)) for m in (src, dst)))
    return lax.ppermute(a, ("yl", "xp", "xq"), sends)


def local(pencil_left, pencil_right, basis_panel, block_inverses, pencil_shift, start_vectors):
    row = lax.axis_index(ROWS)
    parity = lax.axis_index("col")
    pair = lax.axis_index(("yl", "xp"))
    odd = lax.axis_index("xq")
    half = odd ^ lax.axis_index("xp")
    where = jnp.stack([pair, odd, half, parity]).astype(jnp.int32)
    where, pencil_shift = lax.optimization_barrier((where, pencil_shift))
    first = lax.axis_size(ROWS) - STEPS

    left = pencil_left.reshape(NB, HALF, NB)
    right = pencil_right.reshape(NB, HALF, NB)
    own_z = jnp.transpose(basis_panel.reshape(NB, HALF, NB), (1, 0, 2))
    rhs = start_vectors.reshape(NB, NB)

    cols = 2 * jnp.arange(HALF) + parity
    live = (row < first + cols)[None, :, None]
    both = left.astype(jnp.float32) - pencil_shift * right.astype(jnp.float32)
    own = jnp.transpose(jnp.where(live, both, 0.0).astype(jnp.bfloat16), (1, 0, 2))
    own3 = own[HALF - 1 :]
    mate3 = lax.ppermute(own3, "xq", FLIP)
    other3 = lax.ppermute(own3, "col", FLIP)
    lead_shapes = (
        jax.ShapeDtypeStruct((2, 2, NB, NB), jnp.bfloat16), jax.ShapeDtypeStruct((NB, WIDE), jnp.float32)
    )
    inverses, their_rhs = call(lead_kernel, lead_shapes, [], where, block_inverses, rhs)
    mate_rhs = lax.ppermute(their_rhs, "xq", FLIP)
    mate3_other = lax.ppermute(mate3, "col", FLIP)
    lower = own[: HALF - 1]
    mate = lax.ppermute(lower, "xq", FLIP)
    other = lax.ppermute(lower, "col", FLIP)
    mate_other = lax.ppermute(mate, "col", FLIP)
    other_z = lax.ppermute(own_z, "col", FLIP)

    shape = jax.ShapeDtypeStruct((2, NB, WIDE), jnp.bfloat16)
    sums = jax.ShapeDtypeStruct((2, NB, WIDE), jnp.float32)

    def solve(turn, arriving, early, acc, prev):
        return call(
            functools.partial(pair_kernel, turn, [b for b, _ in arriving], [b for b, _ in early]),
            (shape, sums), [],
            where, inverses, rhs, mate_rhs, own, other3, mate3, mate3_other,
            *((other, mate, mate_other) if turn < HALF - 1 else ()),
            *[x for _, x in arriving + early], acc, prev,
        )

    x3, acc = solve(3, [], [], jnp.zeros(sums.shape, sums.dtype), jnp.zeros(shape.shape, shape.dtype))
    a = to_pairs(x3, [(3, 2)])
    b = to_pairs(x3, [(3, 1)])
    x2, acc = solve(2, [(3, a)], [(3, b)], acc, x3)
    c = to_pairs(x2, [(2, 1), (3, 0)])
    d = to_pairs(x2, [(2, 0)])
    x1, acc = solve(1, [(2, c)], [(3, c), (2, d)], acc, x2)
    e = to_pairs(x1, [(1, 0)])
    x0, _ = solve(0, [(1, e)], [], acc, x1)

    spread = lax.all_to_all(
        x0.reshape(GROUPS, 2 * NB // GROUPS, WIDE), ("z", "yh"), 0, 0, tiled=True
    )[GROUPS - 1]
    spread, other_z, other, other3, own_z = lax.optimization_barrier((spread, other_z, other, other3, own_z))
    count = lax.axis_size(ROWS)
    every = lax.all_to_all(
        jnp.broadcast_to(spread[None], (count, *spread.shape)), ROWS, 0, 0, tiled=True
    )

    out = jax.ShapeDtypeStruct((NB, NB), jnp.float32)
    pending, image = call(
        final_kernel, (out, out), [],
        where, every, own, other3, other, own_z, other_z, rhs,
    )
    return pending.reshape(1, 1, NB, NB), image.reshape(1, 1, NB, NB)


def solution(mesh):
    fine = Mesh(mesh.devices.reshape(4, 2, 2, 2, 2, 2), (*ROWS, "col"))
    wide = P(None, ROWS, None, None, "col", None)
    tall = P(None, ROWS, None, "col")
    return jax.shard_map(
        local, mesh=fine, in_specs=(wide, wide, wide, P(), P(), tall),
        out_specs=(tall, tall), check_vma=False,
    )
```

time: 91 us -> 90.5 us (level)
  blocking collectives: 15.8 us -> 34.2 us
  waiting for transfers between devices: 46.6 us -> 34.1 us
  starting transfers between devices: 13.9 us -> 9.81 us
  Pallas kernels: 8.35 us -> 7.14 us
    all_to_all x0 -> x1, blocking collectives: none -> 18.5 us  [local(): lax.all_to_all(jnp.broadcast_to(spread[None], (count, *spread.shape)), RO...]
    all_to_all x1 -> x0, waiting for transfers between devices: 12.9 us -> none  [local(): lax.all_to_all(jnp.broadcast_to(spread[None], (count, *spread.shape)), RO...]
    all_to_all x1 -> x0, starting transfers between devices: 4.65 us -> none  [local(): lax.all_to_all(jnp.broadcast_to(spread[None], (count, *spread.shape)), RO...]
    ppermute x5, waiting for transfers between devices: 18.1 us -> 20.4 us  [to_pairs(): return lax.ppermute(a, ('yl', 'xp', 'xq'), sends)]
    ppermute x1, waiting for transfers between devices: 1.9 us -> 0.01 us  [local(): other_z = lax.ppermute(own_z, 'col', FLIP)]
    unnamed x7, local copies, waits for them, and re-layouts: 0.09 us -> 1.68 us
    pallas_call x5 -> x6, Pallas kernels: 8.35 us -> 7.14 us  [call(): pl.pallas_call(kernel, out_shape=outs, in_specs=[smem if a.dtype == jnp.i...]
    broadcast_in_dim x2 -> x1, local copies, waits for them, and re-layouts: 1.24 us -> 0.24 us  [local(): jnp.broadcast_to(spread[None], (count, *spread.shape))]
  transfers between devices with their start and end apart: 13 -> 13, of which waited for: 7 -> 4; matrix products, arithmetic and copies ran while one was open for 2% -> 0% of each run, Pallas kernels for 4% -> 5%
where the time goes in v1:
time: 90.5 us; the launch traced here: 90.2 us
  blocking collectives  34.2 us (38%)
  waiting for transfers between devices  34.1 us (38%)
  starting transfers between devices  9.81 us (11%)
  Pallas kernels  7.14 us (8%)
  local copies, waits for them, and re-layouts  1.99 us (2%)
  other arithmetic  1.54 us (2%)
  between operations  1.52 us (2%)
    ppermute x5, waiting for transfers between devices, to_pairs(): return lax.ppermute(a, ('yl', 'xp', 'xq'), sends)  20.4 us
    all_to_all x1, blocking collectives, local(): lax.all_to_all(jnp.broadcast_to(spread[None], (count, *spread.shape)), RO...  18.5 us
    all_to_all x1, blocking collectives, local(): lax.all_to_all(x0.reshape(GROUPS, 2 * NB // GROUPS, WIDE), ('z', 'yh'), 0...  15.6 us
    ppermute x1, waiting for transfers between devices, local(): mate = lax.ppermute(lower, 'xq', FLIP)  9.86 us
    pallas_call x6, Pallas kernels, call(): pl.pallas_call(kernel, out_shape=outs, in_specs=[smem if a.dtype == jnp.i...  7.14 us
    ppermute x5, starting transfers between devices, to_pairs(): return lax.ppermute(a, ('yl', 'xp', 'xq'), sends)  5.35 us
    ppermute x1, waiting for transfers between devices, local(): mate_rhs = lax.ppermute(their_rhs, 'xq', FLIP)  3.8 us
  transfers between devices with their start and end apart: 13, of which 4 were waited for; matrix products, arithmetic and copies ran while one was open for 0% of the time, Pallas kernels for 5%

profile of v1, /device:TPU:0, one launch (start us, length us, event | category | flops | bytes accessed | tf_op | source)
XLA Modules:
  0.0 90.2 jit_solution(3918894214190658722)
XLA Ops:
  0.6 0.0 copy-start
  1.4 1.5 %fusion.1.own_ref.w_own_ref = bf16[4,256,256]{2,1,0:T(8,128)(2,1)S(1)} fusion(bf16[1,1,256,4,1,256]{5,3,4,2,1,0:T(4,128)(2,1)} %param.7, bf16[1,1,256,4,1,256]{5,3,4,2,1,0:T(4,128)(2,1)} %param.6, f32[]{:T(128)S(6)} %copy.15, pred[4]{0:T(512)(128)(4,1)S(1)} %add_compare_fusion), kind=kLoop, calls=%fused_computation.2 | loop fusion | flops 1572864 | bytes 1572872 | tf_op jit(solution)/shard_map/transpose | solution.py:154
  2.9 1.7 %collective-permute-start.5 = (bf16[3,256,256]{2,1,0:T(8,128)(2,1)S(1)}, bf16[3,256,256]{2,1,0:T(8,128)(2,1)S(1)}, u32[]{:S(2)}, u32[]{:S(2)}) collective-permute-start(bf16[3,256,256]{2,1,0:T(8,128)(2,1)S(1)} %slice.13), channel_id=1, source_target_pairs={{0,2},{2,0},{1,3},{3,1},{4,6},{6,4},{5,7},{7,5},{8,10},{10,8},{9,1... | collective-permute-start | bytes 1179656 | tf_op jit(solution)/shard_map/ppermute | solution.py:165
  4.5 0.5 collective-permute-start.2
  5.1 0.0 collective-permute-start.4
  5.1 9.9 %collective-permute-done.5.rest_1_ = bf16[3,256,256]{2,1,0:T(8,128)(2,1)S(1)} collective-permute-done((bf16[3,256,256]{2,1,0:T(8,128)(2,1)S(1)}, bf16[3,256,256]{2,1,0:T(8,128)(2,1)S(1)}, u32[]{:S(2)}, u32[]{:S(2)}) %collective-permute-start.5) | collective-permute-done | bytes 393248 | tf_op jit(solution)/shard_map/ppermute | solution.py:165
  14.9 0.0 collective-permute-start.6
  14.9 0.5 collective-permute-start.1
  15.4 0.1 pad_add_fusion.where_ref
  15.5 0.0 copy-done
  15.5 0.0 copy-start.1
  15.5 1.6 %copy-done.1 = f32[4,2,256,256]{3,2,1,0:T(8,128)S(1)} copy-done((f32[4,2,256,256]{3,2,1,0:T(8,128)S(1)}, f32[4,2,256,256]{3,2,1,0:T(8,128)}, u32[]{:S(2)}) %copy-start.1) | copy-done | bytes 2097176
  17.1 0.6 shard_map.77
  17.7 1.7 %collective-permute-start = (f32[256,128]{1,0:T(8,128)S(1)}, f32[256,128]{1,0:T(8,128)S(1)}, u32[]{:S(2)}, u32[]{:S(2)}) collective-permute-start(f32[256,128]{1,0:T(8,128)S(1)} %get-tuple-element.22), channel_id=1, source_target_pairs={{0,2},{2,0},{1,3},{3,1},{4,6},{6,4},{5,7},{7,5},{8,10},{10,8},{9,1... | collective-permute-start | bytes 393224 | tf_op jit(solution)/shard_map/ppermute | solution.py:162
  19.4 0.0 collective-permute-done.2.mate3_ref
  19.4 0.0 collective-permute-start.3
  19.4 3.8 %collective-permute-done.mate_rhs_ref = f32[256,128]{1,0:T(8,128)S(1)} collective-permute-done((f32[256,128]{1,0:T(8,128)S(1)}, f32[256,128]{1,0:T(8,128)S(1)}, u32[]{:S(2)}, u32[]{:S(2)}) %collective-permute-start) | collective-permute-done | bytes 131104 | tf_op jit(solution)/shard_map/ppermute | solution.py:162
  23.2 0.0 collective-permute-done.1.other3_ref.w3_other_ref
  23.2 0.0 collective-permute-done.3.mate3_other_ref
  23.3 0.6 shard_map.78
  23.9 0.0 copy-start.2
  23.9 0.8 collective-permute-start.7
  24.7 0.7 collective-permute-start.8
  25.4 0.0 collective-permute-done.7.rest_3_
  25.4 0.0 collective-permute-done.8.rest_4_
  25.4 0.0 collective-permute-done.4.rest_0_.w_other_ref
  25.4 0.0 collective-permute-done.6.rest_2_
  25.4 0.6 shard_map.79
  26.0 1.3 %collective-permute-start.10 = (bf16[2,256,128]{2,1,0:T(8,128)(2,1)S(1)}, bf16[2,256,128]{2,1,0:T(8,128)(2,1)S(1)}, u32[]{:S(2)}, u32[]{:S(2)}) collective-permute-start(bf16[2,256,128]{2,1,0:T(8,128)(2,1)S(1)} %get-tuple-element.26.rest_7_), channel_id=1, source_target_pairs={{8,0},{10,2},{9,1},{11,3},{24,16},{26,18},{25,17},{27,19},{40,32},... | collective-permute-start | bytes 393224 | tf_op jit(solution)/shard_map/ppermute | solution.py:133
  27.3 1.3 %collective-permute-start.9 = (bf16[2,256,128]{2,1,0:T(8,128)(2,1)S(1)}, bf16[2,256,128]{2,1,0:T(8,128)(2,1)S(1)}, u32[]{:S(2)}, u32[]{:S(2)}) collective-permute-start(bf16[2,256,128]{2,1,0:T(8,128)(2,1)S(1)} %get-tuple-element.26.rest_7_), channel_id=1, source_target_pairs={{8,6},{10,4},{14,0},{12,2},{9,7},{11,5},{15,1},{13,3},{24,22},{26,... | collective-permute-start | bytes 393224 | tf_op jit(solution)/shard_map/ppermute | solution.py:133
  28.6 0.0 copy-done.2
  28.6 0.1 copy.14
  28.7 0.1 collective-permute-start.12
  28.8 12.4 %collective-permute-done.10.rest_5_ = bf16[2,256,128]{2,1,0:T(8,128)(2,1)S(1)} collective-permute-done((bf16[2,256,128]{2,1,0:T(8,128)(2,1)S(1)}, bf16[2,256,128]{2,1,0:T(8,128)(2,1)S(1)}, u32[]{:S(2)}, u32[]{:S(2)}) %collective-permute-start.10) | collective-permute-done | bytes 131104 | tf_op jit(solution)/shard_map/ppermute | solution.py:133
  41.2 0.0 collective-permute-done.9.rest_3_.rest_4_
  41.2 1.0 %shard_map.80 = (bf16[2,256,128]{2,1,0:T(8,128)(2,1)S(1)}, f32[2,256,128]{2,1,0:T(8,128)S(1)}) custom-call(s32[4]{0:T(128)S(1)} %pad_add_fusion.where_ref, bf16[2,2,256,256]{3,2,1,0:T(8,128)(2,1)S(1)} %get-tuple-element.21.inv_ref, f32[256,256]{1,0:T(8,128)S(1)} %bitcast.26, f32[256,128]{1,0:T(8,128)S(1)} %collective-permute-done.mate_rhs_ref, ...), custom_call_target="tpu_custom_call" | custom-call | tf_op jit(solution)/shard_map/pallas_call | solution.py:118
  42.1 1.3 %collective-permute-start.11 = (bf16[2,256,128]{2,1,0:T(8,128)(2,1)S(1)}, bf16[2,256,128]{2,1,0:T(8,128)(2,1)S(1)}, u32[]{:S(2)}, u32[]{:S(2)}) collective-permute-start(bf16[2,256,128]{2,1,0:T(8,128)(2,1)S(1)} %get-tuple-element.28.rest_5_), channel_id=1, source_target_pairs={{6,0},{4,2},{7,1},{5,3},{22,16},{20,18},{23,17},{21,19},{38,32},{3... | collective-permute-start | bytes 393224 | tf_op jit(solution)/shard_map/ppermute | solution.py:133
  43.4 8.0 %collective-permute-done.11.rest_3_ = bf16[2,256,128]{2,1,0:T(8,128)(2,1)S(1)} collective-permute-done((bf16[2,256,128]{2,1,0:T(8,128)(2,1)S(1)}, bf16[2,256,128]{2,1,0:T(8,128)(2,1)S(1)}, u32[]{:S(2)}, u32[]{:S(2)}) %collective-permute-start.11) | collective-permute-done | bytes 131104 | tf_op jit(solution)/shard_map/ppermute | solution.py:133
  51.4 2.3 %shard_map.81 = (bf16[2,256,128]{2,1,0:T(8,128)(2,1)S(1)}, f32[2,256,128]{2,1,0:T(8,128)}) custom-call(s32[4]{0:T(128)S(1)} %pad_add_fusion.where_ref, bf16[2,2,256,256]{3,2,1,0:T(8,128)(2,1)S(1)} %get-tuple-element.21.inv_ref, f32[256,256]{1,0:T(8,128)S(1)} %bitcast.27, f32[256,128]{1,0:T(8,128)S(1)} %collective-permute-done.mate_rhs_ref, ...), custom_call_target="tpu_custom_call" | custom-call | tf_op jit(solution)/shard_map/pallas_call | solution.py:118
  53.7 15.6 %all_to_all.10 = bf16[8,64,128]{2,1,0:T(8,128)(2,1)S(1)} all-to-all(bf16[8,64,128]{2,1,0:T(8,128)(2,1)S(1)} %bitcast.31), channel_id=1, replica_groups=mesh['z'=4,'yh'=2,'yl'=2,'xp'=2,'xq'=2,'col'=2] {'z','yh'}, dimensions={0} | all-to-all | bytes 262144 | tf_op jit(solution)/shard_map/all_to_all | solution.py:192
  69.4 0.0 collective-permute-done.12.z_other_ref
  69.4 0.2 broadcast_in_dim.29
  69.6 18.5 %all_to_all.11.x_ref = bf16[64,64,128]{2,1,0:T(8,128)(2,1)S(1)} all-to-all(bf16[64,64,128]{2,1,0:T(8,128)(2,1)S(1)} %broadcast_in_dim.29), channel_id=1, replica_groups=mesh['z'=4,'yh'=2,'yl'=2,'xp'=2,'xq'=2,'col'=2] {'z','yh','yl','xp','xq'}, dimensions={0} | all-to-all | bytes 2097152 | tf_op jit(solution)/shard_map/all_to_all | solution.py:197
  88.1 2.1 %shard_map.82 = (f32[256,256]{1,0:T(8,128)}, f32[256,256]{1,0:T(8,128)}) custom-call(s32[4]{0:T(128)S(1)} %pad_add_fusion.where_ref, bf16[64,64,128]{2,1,0:T(8,128)(2,1)S(1)} %all_to_all.11.x_ref, bf16[4,256,256]{2,1,0:T(8,128)(2,1)S(1)} %fusion.1.own_ref.w_own_ref, bf16[1,256,256]{2,1,0:T(8,128)(2,1)S(1)} %collective-permute-done.1.other3_ref.w3_other_ref, ...), custom_call_target="tpu_custom_call" | custom-call | tf_op jit(solution)/shard_map/pallas_call | solution.py:118
  (6 shorter events, 0.1 us)
Async XLA Ops:
  0.6 14.9 %copy-start = (f32[1,1,256,256]{3,2,1,0:T(8,128)S(1)}, f32[1,1,256,256]{3,2,1,0:T(8,128)}, u32[]{:S(2)}) copy-start(f32[1,1,256,256]{3,2,1,0:T(8,128)} %param.11) | copy-start | bytes 786436
  2.9 12.1 %collective-permute-start.5 = (bf16[3,256,256]{2,1,0:T(8,128)(2,1)S(1)}, bf16[3,256,256]{2,1,0:T(8,128)(2,1)S(1)}, u32[]{:S(2)}, u32[]{:S(2)}) collective-permute-start(bf16[3,256,256]{2,1,0:T(8,128)(2,1)S(1)} %slice.13), channel_id=1, source_target_pairs={{0,2},{2,0},{1,3},{3,1},{4,6},{6,4},{5,7},{7,5},{8,10},{10,8},{9,1... | collective-permute-start | bytes 1179656 | tf_op jit(solution)/shard_map/ppermute | solution.py:165
  4.5 14.9 %collective-permute-start.2 = (bf16[1,256,256]{2,1,0:T(8,128)(2,1)S(1)}, bf16[1,256,256]{2,1,0:T(8,128)(2,1)S(1)}, u32[]{:S(2)}, u32[]{:S(2)}) collective-permute-start(bf16[1,256,256]{2,1,0:T(8,128)(2,1)S(1)} %slice.12), channel_id=1, source_target_pairs={{0,2},{2,0},{1,3},{3,1},{4,6},{6,4},{5,7},{7,5},{8,10},{10,8},{9,1... | collective-permute-start | bytes 393224 | tf_op jit(solution)/shard_map/ppermute | solution.py:156
  5.1 20.3 %collective-permute-start.4 = (bf16[3,256,256]{2,1,0:T(8,128)(2,1)S(1)}, bf16[3,256,256]{2,1,0:T(8,128)(2,1)S(1)}, u32[]{:S(2)}, u32[]{:S(2)}) collective-permute-start(bf16[3,256,256]{2,1,0:T(8,128)(2,1)S(1)} %slice.13), channel_id=1, source_target_pairs={{0,1},{1,0},{2,3},{3,2},{4,5},{5,4},{6,7},{7,6},{8,9},{9,8},{10,11... | collective-permute-start | bytes 1179656 | tf_op jit(solution)/shard_map/ppermute | solution.py:166
  14.9 10.5 %collective-permute-start.6 = (bf16[3,256,256]{2,1,0:T(8,128)(2,1)S(1)}, bf16[3,256,256]{2,1,0:T(8,128)(2,1)S(1)}, u32[]{:S(2)}, u32[]{:S(2)}) collective-permute-start(bf16[3,256,256]{2,1,0:T(8,128)(2,1)S(1)} %collective-permute-done.5.rest_1_), channel_id=1, source_target_pairs={{0,1},{1,0},{2,3},{3,2},{4,5},{5,4},{6,7},{7,6},{8,9},{9,8},{10,11... | collective-permute-start | bytes 1179656 | tf_op jit(solution)/shard_map/ppermute | solution.py:167
  14.9 8.3 %collective-permute-start.1 = (bf16[1,256,256]{2,1,0:T(8,128)(2,1)S(1)}, bf16[1,256,256]{2,1,0:T(8,128)(2,1)S(1)}, u32[]{:S(2)}, u32[]{:S(2)}) collective-permute-start(bf16[1,256,256]{2,1,0:T(8,128)(2,1)S(1)} %slice.12), channel_id=1, source_target_pairs={{0,1},{1,0},{2,3},{3,2},{4,5},{5,4},{6,7},{7,6},{8,9},{9,8},{10,11... | collective-permute-start | bytes 393224 | tf_op jit(solution)/shard_map/ppermute | solution.py:157
  15.5 1.6 %copy-start.1 = (f32[4,2,256,256]{3,2,1,0:T(8,128)S(1)}, f32[4,2,256,256]{3,2,1,0:T(8,128)}, u32[]{:S(2)}) copy-start(f32[4,2,256,256]{3,2,1,0:T(8,128)} %inv_ref.1) | copy-start | bytes 6291460
  17.7 5.5 %collective-permute-start = (f32[256,128]{1,0:T(8,128)S(1)}, f32[256,128]{1,0:T(8,128)S(1)}, u32[]{:S(2)}, u32[]{:S(2)}) collective-permute-start(f32[256,128]{1,0:T(8,128)S(1)} %get-tuple-element.22), channel_id=1, source_target_pairs={{0,2},{2,0},{1,3},{3,1},{4,6},{6,4},{5,7},{7,5},{8,10},{10,8},{9,1... | collective-permute-start | bytes 393224 | tf_op jit(solution)/shard_map/ppermute | solution.py:162
  19.4 3.8 %collective-permute-start.3 = (bf16[1,256,256]{2,1,0:T(8,128)(2,1)S(1)}, bf16[1,256,256]{2,1,0:T(8,128)(2,1)S(1)}, u32[]{:S(2)}, u32[]{:S(2)}) collective-permute-start(bf16[1,256,256]{2,1,0:T(8,128)(2,1)S(1)} %collective-permute-done.2.mate3_ref), channel_id=1, source_target_pairs={{0,1},{1,0},{2,3},{3,2},{4,5},{5,4},{6,7},{7,6},{8,9},{9,8},{10,11... | collective-permute-start | bytes 393224 | tf_op jit(solution)/shard_map/ppermute | solution.py:163
  23.9 4.7 %copy-start.2 = (bf16[1,1,256,4,1,256]{5,3,4,2,1,0:T(4,128)(2,1)S(1)}, bf16[1,1,256,4,1,256]{5,3,4,2,1,0:T(4,128)(2,1)}, u32[]{:S(2)}) copy-start(bf16[1,1,256,4,1,256]{5,3,4,2,1,0:T(4,128)(2,1)} %param.8) | copy-start | bytes 1572868
  23.9 1.5 %collective-permute-start.7 = (bf16[2,256,128]{2,1,0:T(8,128)(2,1)S(1)}, bf16[2,256,128]{2,1,0:T(8,128)(2,1)S(1)}, u32[]{:S(2)}, u32[]{:S(2)}) collective-permute-start(bf16[2,256,128]{2,1,0:T(8,128)(2,1)S(1)} %get-tuple-element.24.rest_6_), channel_id=1, source_target_pairs={{14,8},{12,10},{15,9},{13,11},{30,24},{28,26},{31,25},{29,27},{46,... | collective-permute-start | bytes 393224 | tf_op jit(solution)/shard_map/ppermute | solution.py:133
  24.7 0.7 collective-permute-start.8
  26.0 15.2 %collective-permute-start.10 = (bf16[2,256,128]{2,1,0:T(8,128)(2,1)S(1)}, bf16[2,256,128]{2,1,0:T(8,128)(2,1)S(1)}, u32[]{:S(2)}, u32[]{:S(2)}) collective-permute-start(bf16[2,256,128]{2,1,0:T(8,128)(2,1)S(1)} %get-tuple-element.26.rest_7_), channel_id=1, source_target_pairs={{8,0},{10,2},{9,1},{11,3},{24,16},{26,18},{25,17},{27,19},{40,32},... | collective-permute-start | bytes 393224 | tf_op jit(solution)/shard_map/ppermute | solution.py:133
  27.3 13.9 %collective-permute-start.9 = (bf16[2,256,128]{2,1,0:T(8,128)(2,1)S(1)}, bf16[2,256,128]{2,1,0:T(8,128)(2,1)S(1)}, u32[]{:S(2)}, u32[]{:S(2)}) collective-permute-start(bf16[2,256,128]{2,1,0:T(8,128)(2,1)S(1)} %get-tuple-element.26.rest_7_), channel_id=1, source_target_pairs={{8,6},{10,4},{14,0},{12,2},{9,7},{11,5},{15,1},{13,3},{24,22},{26,... | collective-permute-start | bytes 393224 | tf_op jit(solution)/shard_map/ppermute | solution.py:133
  28.7 40.7 %collective-permute-start.12 = (bf16[4,256,256]{2,1,0:T(8,128)(2,1)S(1)}, bf16[4,256,256]{2,1,0:T(8,128)(2,1)S(1)}, u32[]{:S(2)}, u32[]{:S(2)}) collective-permute-start(bf16[4,256,256]{2,1,0:T(8,128)(2,1)S(1)} %bitcast.29), channel_id=1, source_target_pairs={{0,1},{1,0},{2,3},{3,2},{4,5},{5,4},{6,7},{7,6},{8,9},{9,8},{10,11... | collective-permute-start | bytes 1572872 | tf_op jit(solution)/shard_map/ppermute | solution.py:168
  42.1 9.3 %collective-permute-start.11 = (bf16[2,256,128]{2,1,0:T(8,128)(2,1)S(1)}, bf16[2,256,128]{2,1,0:T(8,128)(2,1)S(1)}, u32[]{:S(2)}, u32[]{:S(2)}) collective-permute-start(bf16[2,256,128]{2,1,0:T(8,128)(2,1)S(1)} %get-tuple-element.28.rest_5_), channel_id=1, source_target_pairs={{6,0},{4,2},{7,1},{5,3},{22,16},{20,18},{23,17},{21,19},{38,32},{3... | collective-permute-start | bytes 393224 | tf_op jit(solution)/shard_map/ppermute | solution.py:133

commit v2 on v1

--- a/solution.py
+++ b/solution.py
@@ -26,11 +26,9 @@
     return high, (a - high.astype(jnp.float32)).astype(jnp.bfloat16)
 
 
-def lead_kernel(where_ref, inv_ref, rhs_ref, inv_out_ref, rhs_out_ref):
-    pair, half = where_ref[0], where_ref[2]
-    rhs_out_ref[...] = jnp.where(half == 0, rhs_ref[:, WIDE:], rhs_ref[:, :WIDE])
+def split_kernel(where_ref, inv_ref, out_ref):
     for e in range(2):
-        inv_out_ref[e, 0], inv_out_ref[e, 1] = halves(inv_ref[pair, e])
+        out_ref[e, 0], out_ref[e, 1] = halves(inv_ref[where_ref[0], e])
 
 
 def precise(inv_ref, e, b):
@@ -39,18 +37,21 @@
 
 
 def pair_kernel(
-    turn, arriving, early, where_ref, inv_ref, rhs_ref, mate_rhs_ref,
-    own_ref, other3_ref, mate3_ref, mate3_other_ref, *rest,
+    turn, arriving, early, where_ref, inv_ref, rhs_ref, mate_rhs_ref, own_ref, *rest,
 ):
-    if turn < HALF - 1:
-        other_ref, mate_ref, mate_other_ref, *rest = rest
-    *seen, acc_ref, prev_ref, out_ref, sum_ref = rest
+    groups = min(HALF - turn, 3)
+    foreign, rest = rest[: 3 * groups], rest[3 * groups :]
+    if turn:
+        *seen, acc_ref, prev_ref, out_ref, sum_ref = rest
+    else:
+        *seen, acc_ref, prev_ref, out_ref = rest
     pair, odd, half, parity = (where_ref[i] for i in range(4))
 
     def blocks(b):
-        if b == HALF - 1:
-            return own_ref[b], other3_ref[0], mate3_ref[0], mate3_other_ref[0]
-        return own_ref[b], other_ref[b], mate_ref[b], mate_other_ref[b]
+        n, at = max(HALF - 1 - b, 0), 0
+        if n >= 2:
+            n, at = 2, b
+        return own_ref[b], *(ref[at] for ref in foreign[3 * n : 3 * n + 3])
 
     def less(accs, b, x):
         own, other, mate, mate_other = blocks(b)
@@ -82,16 +83,17 @@
     def _():
         out_ref[...] = prev_ref[...]
 
-    @pl.when(pair == turn - 1)
-    def _():
-        accs = fresh()
-        for b, x in zip(early, seen[len(arriving) :]):
-            accs = less(accs, b, x)
-        sum_ref[0], sum_ref[1] = accs
+    if turn:
+        @pl.when(pair == turn - 1)
+        def _():
+            accs = fresh()
+            for b, x in zip(early, seen[len(arriving) :]):
+                accs = less(accs, b, x)
+            sum_ref[0], sum_ref[1] = accs
 
 
 def final_kernel(
-    where_ref, x_ref, w_own_ref, w3_other_ref, w_other_ref, z_own_ref, z_other_ref,
+    where_ref, x_ref, w_own_ref, other3_ref, other2_ref, other01_ref, z_own_ref, z_other_ref,
     rhs_ref, pending_ref, image_ref,
 ):
     parity = where_ref[3]
@@ -99,7 +101,7 @@
     image = jnp.zeros_like(pending)
     for b in range(HALF):
         yl, xp = b // 2, b % 2
-        own, other = w_own_ref[b], w3_other_ref[0] if b == HALF - 1 else w_other_ref[b]
+        own, other = w_own_ref[b], (other01_ref[b] if b < 2 else (other2_ref, other3_ref)[b - 2][0])
         for w, z, p in ((own, z_own_ref, parity), (other, z_other_ref, 1 - parity)):
             columns = []
             for half in range(2):
@@ -140,7 +142,7 @@
     odd = lax.axis_index("xq")
     half = odd ^ lax.axis_index("xp")
     where = jnp.stack([pair, odd, half, parity]).astype(jnp.int32)
-    where, pencil_shift = lax.optimization_barrier((where, pencil_shift))
+    where, pencil_shift, lower_half = lax.optimization_barrier((where, pencil_shift, half == 0))
     first = lax.axis_size(ROWS) - STEPS
 
     left = pencil_left.reshape(NB, HALF, NB)
@@ -155,27 +157,31 @@
     own3 = own[HALF - 1 :]
     mate3 = lax.ppermute(own3, "xq", FLIP)
     other3 = lax.ppermute(own3, "col", FLIP)
-    lead_shapes = (
-        jax.ShapeDtypeStruct((2, 2, NB, NB), jnp.bfloat16), jax.ShapeDtypeStruct((NB, WIDE), jnp.float32)
-    )
-    inverses, their_rhs = call(lead_kernel, lead_shapes, [], where, block_inverses, rhs)
-    mate_rhs = lax.ppermute(their_rhs, "xq", FLIP)
+    mate_rhs = lax.ppermute(jnp.where(lower_half, rhs[:, WIDE:], rhs[:, :WIDE]), "xq", FLIP)
     mate3_other = lax.ppermute(mate3, "col", FLIP)
-    lower = own[: HALF - 1]
-    mate = lax.ppermute(lower, "xq", FLIP)
-    other = lax.ppermute(lower, "col", FLIP)
-    mate_other = lax.ppermute(mate, "col", FLIP)
+    mate2 = lax.ppermute(own[2:3], "xq", FLIP)
+    other2 = lax.ppermute(own[2:3], "col", FLIP)
+    inverses = call(
+        split_kernel, jax.ShapeDtypeStruct((2, 2, NB, NB), jnp.bfloat16), [], where, block_inverses
+    )
+    mate01 = lax.ppermute(own[:2], "xq", FLIP)
+    other01 = lax.ppermute(own[:2], "col", FLIP)
+    mate2_other = lax.ppermute(mate2, "col", FLIP)
+    mate01_other = lax.ppermute(mate01, "col", FLIP)
     other_z = lax.ppermute(own_z, "col", FLIP)
 
     shape = jax.ShapeDtypeStruct((2, NB, WIDE), jnp.bfloat16)
     sums = jax.ShapeDtypeStruct((2, NB, WIDE), jnp.float32)
+
+    foreign = (
+        (other3, mate3, mate3_other), (other2, mate2, mate2_other), (other01, mate01, mate01_other)
+    )
 
     def solve(turn, arriving, early, acc, prev):
         return call(
             functools.partial(pair_kernel, turn, [b for b, _ in arriving], [b for b, _ in early]),
-            (shape, sums), [],
-            where, inverses, rhs, mate_rhs, own, other3, mate3, mate3_other,
-            *((other, mate, mate_other) if turn < HALF - 1 else ()),
+            (shape, sums) if turn else shape, [],
+            where, inverses, rhs, mate_rhs, own, *sum(foreign[: HALF - turn], ()),
             *[x for _, x in arriving + early], acc, prev,
         )
 
@@ -187,12 +193,12 @@
     d = to_pairs(x2, [(2, 0)])
     x1, acc = solve(1, [(2, c)], [(3, c), (2, d)], acc, x2)
     e = to_pairs(x1, [(1, 0)])
-    x0, _ = solve(0, [(1, e)], [], acc, x1)
+    x0 = solve(0, [(1, e)], [], acc, x1)
 
     spread = lax.all_to_all(
         x0.reshape(GROUPS, 2 * NB // GROUPS, WIDE), ("z", "yh"), 0, 0, tiled=True
     )[GROUPS - 1]
-    spread, other_z, other, other3, own_z = lax.optimization_barrier((spread, other_z, other, other3, own_z))
+    spread, other_z = lax.optimization_barrier((spread, other_z))
     count = lax.axis_size(ROWS)
     every = lax.all_to_all(
         jnp.broadcast_to(spread[None], (count, *spread.shape)), ROWS, 0, 0, tiled=True
@@ -201,7 +207,7 @@
     out = jax.ShapeDtypeStruct((NB, NB), jnp.float32)
     pending, image = call(
         final_kernel, (out, out), [],
-        where, every, own, other3, other, own_z, other_z, rhs,
+        where, every, own, other3, other2, other01, own_z, other_z, rhs,
     )
     return pending.reshape(1, 1, NB, NB), image.reshape(1, 1, NB, NB)
 

time: 90.5 us -> 90.3 us (level)
  blocking collectives: 34.2 us -> 36.8 us
  waiting for transfers between devices: 34.1 us -> 32.5 us
  local copies, waits for them, and re-layouts: 1.99 us -> 0.41 us
    ppermute x4 -> x7, waiting for transfers between devices: 13.7 us -> 9.44 us  [the longest x1 6.62 us: local(): mate2 = lax.ppermute(own[2:3], 'xq', FLIP)]
    all_to_all x1, blocking collectives: 18.5 us -> 20.9 us  [local(): lax.all_to_all(jnp.broadcast_to(spread[None], (count, *spread.shape)), RO...]
    ppermute x1, waiting for transfers between devices: 0.01 us -> 1.93 us  [local(): mate3 = lax.ppermute(own3, 'xq', FLIP)]
    unnamed x7, local copies, waits for them, and re-layouts: 1.68 us -> 0.09 us
    ppermute x1, starting transfers between devices: 0.5 us -> 1.68 us  [local(): mate3 = lax.ppermute(own3, 'xq', FLIP)]
    ppermute x4 -> x7, starting transfers between devices: 3.37 us -> 3.29 us  [the longest x1 1.68 us: local(): mate01 = lax.ppermute(own[:2], 'xq', FLIP)]
  transfers between devices with their start and end apart: 13 -> 16, of which waited for: 4 -> 5; matrix products, arithmetic and copies ran while one was open for 0% -> 0% of each run, Pallas kernels for 5% -> 5%
where the time goes in v2:
time: 90.3 us; the launch traced here: 90.1 us
  blocking collectives  36.8 us (41%)
  waiting for transfers between devices  32.5 us (36%)
  starting transfers between devices  10.7 us (12%)
  Pallas kernels  6.42 us (7%)
  between operations  1.64 us (2%)
  other arithmetic  1.56 us (2%)
    ppermute x5, waiting for transfers between devices, to_pairs(): return lax.ppermute(a, ('yl', 'xp', 'xq'), sends)  21.1 us
    all_to_all x1, blocking collectives, local(): lax.all_to_all(jnp.broadcast_to(spread[None], (count, *spread.shape)), RO...  20.9 us
    all_to_all x1, blocking collectives, local(): lax.all_to_all(x0.reshape(GROUPS, 2 * NB // GROUPS, WIDE), ('z', 'yh'), 0...  15.9 us
    ppermute x1, waiting for transfers between devices, local(): mate2 = lax.ppermute(own[2:3], 'xq', FLIP)  6.62 us
    pallas_call x6, Pallas kernels, call(): pl.pallas_call(kernel, out_shape=outs, in_specs=[smem if a.dtype == jnp.i...  6.42 us
    ppermute x5, starting transfers between devices, to_pairs(): return lax.ppermute(a, ('yl', 'xp', 'xq'), sends)  5.21 us
    ppermute x1, waiting for transfers between devices, local(): lax.ppermute(jnp.where(lower_half, rhs[:, WIDE:], rhs[:, :WIDE]), 'xq', F...  2.8 us
    ppermute x1, waiting for transfers between devices, local(): mate3 = lax.ppermute(own3, 'xq', FLIP)  1.93 us
  transfers between devices with their start and end apart: 16, of which 5 were waited for; matrix products, arithmetic and copies ran while one was open for 0% of the time, Pallas kernels for 5%

profile of v2, /device:TPU:0, one launch (start us, length us, event | category | flops | bytes accessed | tf_op | source)
XLA Modules:
  0.0 90.1 jit_solution(11756289471156751620)
XLA Ops:
  0.6 0.0 copy-start
  1.5 1.5 %fusion.1.own_ref.w_own_ref = bf16[4,256,256]{2,1,0:T(8,128)(2,1)S(1)} fusion(bf16[1,1,256,4,1,256]{5,3,4,2,1,0:T(4,128)(2,1)} %param.7, bf16[1,1,256,4,1,256]{5,3,4,2,1,0:T(4,128)(2,1)} %param.6, f32[]{:T(128)S(6)} %copy.15, pred[4]{0:T(512)(128)(4,1)S(1)} %add_compare_fusion), kind=kLoop, calls=%fused_computation.2 | loop fusion | flops 1572864 | bytes 1572872 | tf_op jit(solution)/shard_map/transpose | solution.py:156
  3.0 1.7 %collective-permute-start.2 = (bf16[1,256,256]{2,1,0:T(8,128)(2,1)S(1)}, bf16[1,256,256]{2,1,0:T(8,128)(2,1)S(1)}, u32[]{:S(2)}, u32[]{:S(2)}) collective-permute-start(bf16[1,256,256]{2,1,0:T(8,128)(2,1)S(1)} %get-tuple-element.29), channel_id=1, source_target_pairs={{0,2},{2,0},{1,3},{3,1},{4,6},{6,4},{5,7},{7,5},{8,10},{10,8},{9,1... | collective-permute-start | bytes 393224 | tf_op jit(solution)/shard_map/ppermute | solution.py:158
  4.6 0.1 pad_add_fusion.where_ref
  4.7 0.5 collective-permute-start
  5.3 1.7 %collective-permute-start.8 = (bf16[2,256,256]{2,1,0:T(8,128)(2,1)S(1)}, bf16[2,256,256]{2,1,0:T(8,128)(2,1)S(1)}, u32[]{:S(2)}, u32[]{:S(2)}) collective-permute-start(bf16[2,256,256]{2,1,0:T(8,128)(2,1)S(1)} %slice.30), channel_id=1, source_target_pairs={{0,2},{2,0},{1,3},{3,1},{4,6},{6,4},{5,7},{7,5},{8,10},{10,8},{9,1... | collective-permute-start | bytes 786440 | tf_op jit(solution)/shard_map/ppermute | solution.py:167
  7.0 0.4 collective-permute-start.5
  7.4 0.0 collective-permute-start.1
  7.4 1.9 %collective-permute-done.2.rest_1_ = bf16[1,256,256]{2,1,0:T(8,128)(2,1)S(1)} collective-permute-done((bf16[1,256,256]{2,1,0:T(8,128)(2,1)S(1)}, bf16[1,256,256]{2,1,0:T(8,128)(2,1)S(1)}, u32[]{:S(2)}, u32[]{:S(2)}) %collective-permute-start.2) | collective-permute-done | bytes 131104 | tf_op jit(solution)/shard_map/ppermute | solution.py:158
  9.3 0.0 collective-permute-start.3
  9.3 2.8 %collective-permute-done.mate_rhs_ref = f32[256,128]{1,0:T(8,128)S(1)} collective-permute-done((f32[256,128]{1,0:T(8,128)S(1)}, f32[256,128]{1,0:T(8,128)S(1)}, u32[]{:S(2)}, u32[]{:S(2)}) %collective-permute-start) | collective-permute-done | bytes 131104 | tf_op jit(solution)/shard_map/ppermute | solution.py:160
  12.1 0.0 collective-permute-start.4
  12.1 0.0 copy-done.1
  12.1 0.6 shard_map.77.inv_ref
  12.8 6.6 %collective-permute-done.5.rest_4_ = bf16[1,256,256]{2,1,0:T(8,128)(2,1)S(1)} collective-permute-done((bf16[1,256,256]{2,1,0:T(8,128)(2,1)S(1)}, bf16[1,256,256]{2,1,0:T(8,128)(2,1)S(1)}, u32[]{:S(2)}, u32[]{:S(2)}) %collective-permute-start.5) | collective-permute-done | bytes 131104 | tf_op jit(solution)/shard_map/ppermute | solution.py:162
  19.4 0.0 collective-permute-start.6
  19.4 0.0 collective-permute-done.1.rest_0_.other3_ref
  19.4 0.0 collective-permute-done.3.rest_2_
  19.4 0.0 copy-start.2
  19.5 0.6 shard_map.78
  20.0 0.7 collective-permute-start.11
  20.7 0.7 collective-permute-start.10
  21.4 0.0 collective-permute-done.4.rest_3_.other2_ref
  21.4 0.6 collective-permute-start.7
  22.0 0.0 collective-permute-done.8.rest_7_
  22.0 0.1 collective-permute-start.9
  22.1 0.0 collective-permute-done.6.rest_5_
  22.1 0.0 collective-permute-done.11.rest_7_
  22.1 0.0 collective-permute-done.10.rest_6_
  22.1 0.6 shard_map.79
  22.7 1.3 %collective-permute-start.13 = (bf16[2,256,128]{2,1,0:T(8,128)(2,1)S(1)}, bf16[2,256,128]{2,1,0:T(8,128)(2,1)S(1)}, u32[]{:S(2)}, u32[]{:S(2)}) collective-permute-start(bf16[2,256,128]{2,1,0:T(8,128)(2,1)S(1)} %get-tuple-element.20.rest_13_), channel_id=1, source_target_pairs={{8,0},{10,2},{9,1},{11,3},{24,16},{26,18},{25,17},{27,19},{40,32},... | collective-permute-start | bytes 393224 | tf_op jit(solution)/shard_map/ppermute | solution.py:135
  24.0 1.3 %collective-permute-start.12 = (bf16[2,256,128]{2,1,0:T(8,128)(2,1)S(1)}, bf16[2,256,128]{2,1,0:T(8,128)(2,1)S(1)}, u32[]{:S(2)}, u32[]{:S(2)}) collective-permute-start(bf16[2,256,128]{2,1,0:T(8,128)(2,1)S(1)} %get-tuple-element.20.rest_13_), channel_id=1, source_target_pairs={{8,6},{10,4},{14,0},{12,2},{9,7},{11,5},{15,1},{13,3},{24,22},{26,... | collective-permute-start | bytes 393224 | tf_op jit(solution)/shard_map/ppermute | solution.py:135
  25.3 0.0 copy-done.2
  25.3 0.1 copy.14
  25.4 0.5 collective-permute-start.15
  25.9 0.0 collective-permute-done.7.rest_6_.other01_ref
  25.9 0.0 collective-permute-done.9.rest_8_
  25.9 13.9 %collective-permute-done.13.rest_11_ = bf16[2,256,128]{2,1,0:T(8,128)(2,1)S(1)} collective-permute-done((bf16[2,256,128]{2,1,0:T(8,128)(2,1)S(1)}, bf16[2,256,128]{2,1,0:T(8,128)(2,1)S(1)}, u32[]{:S(2)}, u32[]{:S(2)}) %collective-permute-start.13) | collective-permute-done | bytes 131104 | tf_op jit(solution)/shard_map/ppermute | solution.py:135
  39.8 0.0 collective-permute-done.12.rest_9_.rest_10_
  39.8 1.0 %shard_map.80 = (bf16[2,256,128]{2,1,0:T(8,128)(2,1)S(1)}, f32[2,256,128]{2,1,0:T(8,128)S(1)}) custom-call(s32[4]{0:T(128)S(1)} %pad_add_fusion.where_ref, bf16[2,2,256,256]{3,2,1,0:T(8,128)(2,1)S(1)} %shard_map.77.inv_ref, f32[256,256]{1,0:T(8,128)S(1)} %bitcast.26, f32[256,128]{1,0:T(8,128)S(1)} %collective-permute-done.mate_rhs_ref, ...), custom_call_target="tpu_custom_call" | custom-call | tf_op jit(solution)/shard_map/pallas_call | solution.py:120
  40.8 1.3 %collective-permute-start.14 = (bf16[2,256,128]{2,1,0:T(8,128)(2,1)S(1)}, bf16[2,256,128]{2,1,0:T(8,128)(2,1)S(1)}, u32[]{:S(2)}, u32[]{:S(2)}) collective-permute-start(bf16[2,256,128]{2,1,0:T(8,128)(2,1)S(1)} %get-tuple-element.22.rest_11_), channel_id=1, source_target_pairs={{6,0},{4,2},{7,1},{5,3},{22,16},{20,18},{23,17},{21,19},{38,32},{3... | collective-permute-start | bytes 393224 | tf_op jit(solution)/shard_map/ppermute | solution.py:135
  42.1 7.2 %collective-permute-done.14.rest_9_ = bf16[2,256,128]{2,1,0:T(8,128)(2,1)S(1)} collective-permute-done((bf16[2,256,128]{2,1,0:T(8,128)(2,1)S(1)}, bf16[2,256,128]{2,1,0:T(8,128)(2,1)S(1)}, u32[]{:S(2)}, u32[]{:S(2)}) %collective-permute-start.14) | collective-permute-done | bytes 131104 | tf_op jit(solution)/shard_map/ppermute | solution.py:135
  49.3 1.6 %shard_map.81 = bf16[2,256,128]{2,1,0:T(8,128)(2,1)S(1)} custom-call(s32[4]{0:T(128)S(1)} %pad_add_fusion.where_ref, bf16[2,2,256,256]{3,2,1,0:T(8,128)(2,1)S(1)} %shard_map.77.inv_ref, f32[256,256]{1,0:T(8,128)S(1)} %bitcast.27, f32[256,128]{1,0:T(8,128)S(1)} %collective-permute-done.mate_rhs_ref, bf16[4,256,256]{2,1,0:T(8,128)(2,1)S(1)} %fusion.1.own_ref.w_own_ref, ...), custom_call_target="tpu_custom_call" | custom-call | tf_op jit(solution)/shard_map/pallas_call | solution.py:120
  50.9 15.9 %all_to_all.10 = bf16[8,64,128]{2,1,0:T(8,128)(2,1)S(1)} all-to-all(bf16[8,64,128]{2,1,0:T(8,128)(2,1)S(1)} %bitcast.31), channel_id=1, replica_groups=mesh['z'=4,'yh'=2,'yl'=2,'xp'=2,'xq'=2,'col'=2] {'z','yh'}, dimensions={0} | all-to-all | bytes 262144 | tf_op jit(solution)/shard_map/all_to_all | solution.py:198
  66.8 0.0 collective-permute-done.15.z_other_ref
  66.8 0.2 broadcast_in_dim.29
  67.1 20.9 %all_to_all.11.x_ref = bf16[64,64,128]{2,1,0:T(8,128)(2,1)S(1)} all-to-all(bf16[64,64,128]{2,1,0:T(8,128)(2,1)S(1)} %broadcast_in_dim.29), channel_id=1, replica_groups=mesh['z'=4,'yh'=2,'yl'=2,'xp'=2,'xq'=2,'col'=2] {'z','yh','yl','xp','xq'}, dimensions={0} | all-to-all | bytes 2097152 | tf_op jit(solution)/shard_map/all_to_all | solution.py:203
  88.0 2.1 %shard_map.82 = (f32[256,256]{1,0:T(8,128)}, f32[256,256]{1,0:T(8,128)}) custom-call(s32[4]{0:T(128)S(1)} %pad_add_fusion.where_ref, bf16[64,64,128]{2,1,0:T(8,128)(2,1)S(1)} %all_to_all.11.x_ref, bf16[4,256,256]{2,1,0:T(8,128)(2,1)S(1)} %fusion.1.own_ref.w_own_ref, bf16[1,256,256]{2,1,0:T(8,128)(2,1)S(1)} %collective-permute-done.1.rest_0_.other3_ref, ...), custom_call_target="tpu_custom_call" | custom-call | tf_op jit(solution)/shard_map/pallas_call | solution.py:120
  (9 shorter events, 0.1 us)
Async XLA Ops:
  0.6 4.1 %copy-start = (f32[1,1,256,256]{3,2,1,0:T(8,128)S(1)}, f32[1,1,256,256]{3,2,1,0:T(8,128)}, u32[]{:S(2)}) copy-start(f32[1,1,256,256]{3,2,1,0:T(8,128)} %param.11) | copy-start | bytes 786436
  0.6 11.5 %copy-start.1 = (f32[4,2,256,256]{3,2,1,0:T(8,128)S(1)}, f32[4,2,256,256]{3,2,1,0:T(8,128)}, u32[]{:S(2)}) copy-start(f32[4,2,256,256]{3,2,1,0:T(8,128)} %inv_ref.1) | copy-start | bytes 6291460
  3.0 6.3 %collective-permute-start.2 = (bf16[1,256,256]{2,1,0:T(8,128)(2,1)S(1)}, bf16[1,256,256]{2,1,0:T(8,128)(2,1)S(1)}, u32[]{:S(2)}, u32[]{:S(2)}) collective-permute-start(bf16[1,256,256]{2,1,0:T(8,128)(2,1)S(1)} %get-tuple-element.29), channel_id=1, source_target_pairs={{0,2},{2,0},{1,3},{3,1},{4,6},{6,4},{5,7},{7,5},{8,10},{10,8},{9,1... | collective-permute-start | bytes 393224 | tf_op jit(solution)/shard_map/ppermute | solution.py:158
  4.7 7.4 %collective-permute-start = (f32[256,128]{1,0:T(8,128)S(1)}, f32[256,128]{1,0:T(8,128)S(1)}, u32[]{:S(2)}, u32[]{:S(2)}) collective-permute-start(f32[256,128]{1,0:T(8,128)S(1)} %slice_select_fusion), channel_id=1, source_target_pairs={{0,2},{2,0},{1,3},{3,1},{4,6},{6,4},{5,7},{7,5},{8,10},{10,8},{9,1... | collective-permute-start | bytes 393224 | tf_op jit(solution)/shard_map/ppermute | solution.py:160
  5.3 16.7 %collective-permute-start.8 = (bf16[2,256,256]{2,1,0:T(8,128)(2,1)S(1)}, bf16[2,256,256]{2,1,0:T(8,128)(2,1)S(1)}, u32[]{:S(2)}, u32[]{:S(2)}) collective-permute-start(bf16[2,256,256]{2,1,0:T(8,128)(2,1)S(1)} %slice.30), channel_id=1, source_target_pairs={{0,2},{2,0},{1,3},{3,1},{4,6},{6,4},{5,7},{7,5},{8,10},{10,8},{9,1... | collective-permute-start | bytes 786440 | tf_op jit(solution)/shard_map/ppermute | solution.py:167
  7.0 12.4 %collective-permute-start.5 = (bf16[1,256,256]{2,1,0:T(8,128)(2,1)S(1)}, bf16[1,256,256]{2,1,0:T(8,128)(2,1)S(1)}, u32[]{:S(2)}, u32[]{:S(2)}) collective-permute-start(bf16[1,256,256]{2,1,0:T(8,128)(2,1)S(1)} %get-tuple-element.28), channel_id=1, source_target_pairs={{0,2},{2,0},{1,3},{3,1},{4,6},{6,4},{5,7},{7,5},{8,10},{10,8},{9,1... | collective-permute-start | bytes 393224 | tf_op jit(solution)/shard_map/ppermute | solution.py:162
  7.4 12.0 %collective-permute-start.1 = (bf16[1,256,256]{2,1,0:T(8,128)(2,1)S(1)}, bf16[1,256,256]{2,1,0:T(8,128)(2,1)S(1)}, u32[]{:S(2)}, u32[]{:S(2)}) collective-permute-start(bf16[1,256,256]{2,1,0:T(8,128)(2,1)S(1)} %get-tuple-element.29), channel_id=1, source_target_pairs={{0,1},{1,0},{2,3},{3,2},{4,5},{5,4},{6,7},{7,6},{8,9},{9,8},{10,11... | collective-permute-start | bytes 393224 | tf_op jit(solution)/shard_map/ppermute | solution.py:159
  9.3 10.1 %collective-permute-start.3 = (bf16[1,256,256]{2,1,0:T(8,128)(2,1)S(1)}, bf16[1,256,256]{2,1,0:T(8,128)(2,1)S(1)}, u32[]{:S(2)}, u32[]{:S(2)}) collective-permute-start(bf16[1,256,256]{2,1,0:T(8,128)(2,1)S(1)} %collective-permute-done.2.rest_1_), channel_id=1, source_target_pairs={{0,1},{1,0},{2,3},{3,2},{4,5},{5,4},{6,7},{7,6},{8,9},{9,8},{10,11... | collective-permute-start | bytes 393224 | tf_op jit(solution)/shard_map/ppermute | solution.py:161
  12.1 9.3 %collective-permute-start.4 = (bf16[1,256,256]{2,1,0:T(8,128)(2,1)S(1)}, bf16[1,256,256]{2,1,0:T(8,128)(2,1)S(1)}, u32[]{:S(2)}, u32[]{:S(2)}) collective-permute-start(bf16[1,256,256]{2,1,0:T(8,128)(2,1)S(1)} %get-tuple-element.28), channel_id=1, source_target_pairs={{0,1},{1,0},{2,3},{3,2},{4,5},{5,4},{6,7},{7,6},{8,9},{9,8},{10,11... | collective-permute-start | bytes 393224 | tf_op jit(solution)/shard_map/ppermute | solution.py:163
  19.4 2.7 %collective-permute-start.6 = (bf16[1,256,256]{2,1,0:T(8,128)(2,1)S(1)}, bf16[1,256,256]{2,1,0:T(8,128)(2,1)S(1)}, u32[]{:S(2)}, u32[]{:S(2)}) collective-permute-start(bf16[1,256,256]{2,1,0:T(8,128)(2,1)S(1)} %collective-permute-done.5.rest_4_), channel_id=1, source_target_pairs={{0,1},{1,0},{2,3},{3,2},{4,5},{5,4},{6,7},{7,6},{8,9},{9,8},{10,11... | collective-permute-start | bytes 393224 | tf_op jit(solution)/shard_map/ppermute | solution.py:169
  19.4 5.8 %copy-start.2 = (bf16[1,1,256,4,1,256]{5,3,4,2,1,0:T(4,128)(2,1)S(1)}, bf16[1,1,256,4,1,256]{5,3,4,2,1,0:T(4,128)(2,1)}, u32[]{:S(2)}) copy-start(bf16[1,1,256,4,1,256]{5,3,4,2,1,0:T(4,128)(2,1)} %param.8) | copy-start | bytes 1572868
  20.0 2.1 %collective-permute-start.11 = (bf16[2,256,128]{2,1,0:T(8,128)(2,1)S(1)}, bf16[2,256,128]{2,1,0:T(8,128)(2,1)S(1)}, u32[]{:S(2)}, u32[]{:S(2)}) collective-permute-start(bf16[2,256,128]{2,1,0:T(8,128)(2,1)S(1)} %get-tuple-element.18.rest_9_), channel_id=1, source_target_pairs={{14,6},{12,4},{15,7},{13,5},{30,22},{28,20},{31,23},{29,21},{46,38... | collective-permute-start | bytes 393224 | tf_op jit(solution)/shard_map/ppermute | solution.py:135
  20.7 1.4 %collective-permute-start.10 = (bf16[2,256,128]{2,1,0:T(8,128)(2,1)S(1)}, bf16[2,256,128]{2,1,0:T(8,128)(2,1)S(1)}, u32[]{:S(2)}, u32[]{:S(2)}) collective-permute-start(bf16[2,256,128]{2,1,0:T(8,128)(2,1)S(1)} %get-tuple-element.18.rest_9_), channel_id=1, source_target_pairs={{14,8},{12,10},{15,9},{13,11},{30,24},{28,26},{31,25},{29,27},{46,... | collective-permute-start | bytes 393224 | tf_op jit(solution)/shard_map/ppermute | solution.py:135
  21.4 4.5 %collective-permute-start.7 = (bf16[2,256,256]{2,1,0:T(8,128)(2,1)S(1)}, bf16[2,256,256]{2,1,0:T(8,128)(2,1)S(1)}, u32[]{:S(2)}, u32[]{:S(2)}) collective-permute-start(bf16[2,256,256]{2,1,0:T(8,128)(2,1)S(1)} %slice.30), channel_id=1, source_target_pairs={{0,1},{1,0},{2,3},{3,2},{4,5},{5,4},{6,7},{7,6},{8,9},{9,8},{10,11... | collective-permute-start | bytes 786440 | tf_op jit(solution)/shard_map/ppermute | solution.py:168
  22.0 3.9 %collective-permute-start.9 = (bf16[2,256,256]{2,1,0:T(8,128)(2,1)S(1)}, bf16[2,256,256]{2,1,0:T(8,128)(2,1)S(1)}, u32[]{:S(2)}, u32[]{:S(2)}) collective-permute-start(bf16[2,256,256]{2,1,0:T(8,128)(2,1)S(1)} %collective-permute-done.8.rest_7_), channel_id=1, source_target_pairs={{0,1},{1,0},{2,3},{3,2},{4,5},{5,4},{6,7},{7,6},{8,9},{9,8},{10,11... | collective-permute-start | bytes 786440 | tf_op jit(solution)/shard_map/ppermute | solution.py:170
  22.7 17.1 %collective-permute-start.13 = (bf16[2,256,128]{2,1,0:T(8,128)(2,1)S(1)}, bf16[2,256,128]{2,1,0:T(8,128)(2,1)S(1)}, u32[]{:S(2)}, u32[]{:S(2)}) collective-permute-start(bf16[2,256,128]{2,1,0:T(8,128)(2,1)S(1)} %get-tuple-element.20.rest_13_), channel_id=1, source_target_pairs={{8,0},{10,2},{9,1},{11,3},{24,16},{26,18},{25,17},{27,19},{40,32},... | collective-permute-start | bytes 393224 | tf_op jit(solution)/shard_map/ppermute | solution.py:135
  24.0 15.8 %collective-permute-start.12 = (bf16[2,256,128]{2,1,0:T(8,128)(2,1)S(1)}, bf16[2,256,128]{2,1,0:T(8,128)(2,1)S(1)}, u32[]{:S(2)}, u32[]{:S(2)}) collective-permute-start(bf16[2,256,128]{2,1,0:T(8,128)(2,1)S(1)} %get-tuple-element.20.rest_13_), channel_id=1, source_target_pairs={{8,6},{10,4},{14,0},{12,2},{9,7},{11,5},{15,1},{13,3},{24,22},{26,... | collective-permute-start | bytes 393224 | tf_op jit(solution)/shard_map/ppermute | solution.py:135
  25.4 41.5 %collective-permute-start.15 = (bf16[4,256,256]{2,1,0:T(8,128)(2,1)S(1)}, bf16[4,256,256]{2,1,0:T(8,128)(2,1)S(1)}, u32[]{:S(2)}, u32[]{:S(2)}) collective-permute-start(bf16[4,256,256]{2,1,0:T(8,128)(2,1)S(1)} %bitcast.29), channel_id=1, source_target_pairs={{0,1},{1,0},{2,3},{3,2},{4,5},{5,4},{6,7},{7,6},{8,9},{9,8},{10,11... | collective-permute-start | bytes 1572872 | tf_op jit(solution)/shard_map/ppermute | solution.py:171
  40.8 8.5 %collective-permute-start.14 = (bf16[2,256,128]{2,1,0:T(8,128)(2,1)S(1)}, bf16[2,256,128]{2,1,0:T(8,128)(2,1)S(1)}, u32[]{:S(2)}, u32[]{:S(2)}) collective-permute-start(bf16[2,256,128]{2,1,0:T(8,128)(2,1)S(1)} %get-tuple-element.22.rest_11_), channel_id=1, source_target_pairs={{6,0},{4,2},{7,1},{5,3},{22,16},{20,18},{23,17},{21,19},{38,32},{3... | collective-permute-start | bytes 393224 | tf_op jit(solution)/shard_map/ppermute | solution.py:135

commit v3 on v2

--- a/solution.py
+++ b/solution.py
@@ -41,10 +41,10 @@
 ):
     groups = min(HALF - turn, 3)
     foreign, rest = rest[: 3 * groups], rest[3 * groups :]
-    if turn:
-        *seen, acc_ref, prev_ref, out_ref, sum_ref = rest
-    else:
-        *seen, acc_ref, prev_ref, out_ref = rest
+    seen, rest = rest[: len(arriving) + len(early)], rest[len(arriving) + len(early) :]
+    acc_ref = None if turn else rest[0]
+    prev_ref, out_ref = rest[-3:-1] if early else rest[-2:]
+    sum_ref = rest[-1] if early else None
     pair, odd, half, parity = (where_ref[i] for i in range(4))
 
     def blocks(b):
@@ -66,7 +66,7 @@
 
     @pl.when(pair == turn)
     def _():
-        accs = fresh() if turn >= HALF - 2 else (acc_ref[0], acc_ref[1])
+        accs = fresh() if turn else (acc_ref[0], acc_ref[1])
         for b, x in zip(arriving, seen):
             accs = less(accs, b, x)
         high = jnp.where(odd == 1, *accs)
@@ -83,7 +83,7 @@
     def _():
         out_ref[...] = prev_ref[...]
 
-    if turn:
+    if early:
         @pl.when(pair == turn - 1)
         def _():
             accs = fresh()
@@ -177,21 +177,21 @@
         (other3, mate3, mate3_other), (other2, mate2, mate2_other), (other01, mate01, mate01_other)
     )
 
-    def solve(turn, arriving, early, acc, prev):
+    def solve(turn, arriving, early, *last):
         return call(
             functools.partial(pair_kernel, turn, [b for b, _ in arriving], [b for b, _ in early]),
-            (shape, sums) if turn else shape, [],
+            (shape, sums) if early else shape, [],
             where, inverses, rhs, mate_rhs, own, *sum(foreign[: HALF - turn], ()),
-            *[x for _, x in arriving + early], acc, prev,
+            *[x for _, x in arriving + early], *last,
         )
 
-    x3, acc = solve(3, [], [], jnp.zeros(sums.shape, sums.dtype), jnp.zeros(shape.shape, shape.dtype))
+    x3 = solve(3, [], [], jnp.zeros(shape.shape, shape.dtype))
     a = to_pairs(x3, [(3, 2)])
     b = to_pairs(x3, [(3, 1)])
-    x2, acc = solve(2, [(3, a)], [(3, b)], acc, x3)
+    x2 = solve(2, [(3, a)], [], x3)
     c = to_pairs(x2, [(2, 1), (3, 0)])
     d = to_pairs(x2, [(2, 0)])
-    x1, acc = solve(1, [(2, c)], [(3, c), (2, d)], acc, x2)
+    x1, acc = solve(1, [(3, b), (2, c)], [(3, c), (2, d)], x2)
     e = to_pairs(x1, [(1, 0)])
     x0 = solve(0, [(1, e)], [], acc, x1)
 

time: 90.3 us -> 89.2 us (0.988)
  waiting for transfers between devices: 32.5 us -> 31.1 us
    ppermute x1, waiting for transfers between devices: 6.62 us -> 0.9 us  [local(): mate2 = lax.ppermute(own[2:3], 'xq', FLIP)]
    ppermute x1, waiting for transfers between devices: 2.8 us -> 8.42 us  [local(): lax.ppermute(jnp.where(lower_half, rhs[:, WIDE:], rhs[:, :WIDE]), 'xq', F...]
    ppermute x5, waiting for transfers between devices: 21.1 us -> 19.5 us  [to_pairs(): return lax.ppermute(a, ('yl', 'xp', 'xq'), sends)]
    ppermute x1, starting transfers between devices: 0.5 us -> 1.68 us  [local(): lax.ppermute(jnp.where(lower_half, rhs[:, WIDE:], rhs[:, :WIDE]), 'xq', F...]
    ppermute x1, starting transfers between devices: 1.68 us -> 0.5 us  [local(): mate01 = lax.ppermute(own[:2], 'xq', FLIP)]
where the time goes in v3:
time: 89.2 us; the launch traced here: 88.9 us
  blocking collectives  36.5 us (41%)
  waiting for transfers between devices  31.1 us (35%)
  starting transfers between devices  10.6 us (12%)
  Pallas kernels  6.4 us (7%)
  between operations  1.64 us (2%)
  other arithmetic  1.56 us (2%)
  local copies, waits for them, and re-layouts  1.09 us (1%)
    all_to_all x1, blocking collectives, local(): lax.all_to_all(jnp.broadcast_to(spread[None], (count, *spread.shape)), RO...  20.9 us
    ppermute x5, waiting for transfers between devices, to_pairs(): return lax.ppermute(a, ('yl', 'xp', 'xq'), sends)  19.5 us
    all_to_all x1, blocking collectives, local(): lax.all_to_all(x0.reshape(GROUPS, 2 * NB // GROUPS, WIDE), ('z', 'yh'), 0...  15.7 us
    ppermute x1, waiting for transfers between devices, local(): lax.ppermute(jnp.where(lower_half, rhs[:, WIDE:], rhs[:, :WIDE]), 'xq', F...  8.42 us
    pallas_call x6, Pallas kernels, call(): pl.pallas_call(kernel, out_shape=outs, in_specs=[smem if a.dtype == jnp.i...  6.4 us
    ppermute x5, starting transfers between devices, to_pairs(): return lax.ppermute(a, ('yl', 'xp', 'xq'), sends)  5.2 us
    ppermute x1, waiting for transfers between devices, local(): mate3 = lax.ppermute(own3, 'xq', FLIP)  2.24 us
  transfers between devices with their start and end apart: 16, of which 5 were waited for; matrix products, arithmetic and copies ran while one was open for 0% of the time, Pallas kernels for 5%

profile of v3, /device:TPU:0, one launch (start us, length us, event | category | flops | bytes accessed | tf_op | source)
XLA Modules:
  0.0 88.9 jit_solution(17872401041132991820)
XLA Ops:
  0.6 0.0 copy-start
  0.6 0.0 copy-start.1
  1.5 1.5 %fusion.1.own_ref.w_own_ref = bf16[4,256,256]{2,1,0:T(8,128)(2,1)S(1)} fusion(bf16[1,1,256,4,1,256]{5,3,4,2,1,0:T(4,128)(2,1)} %param.7, bf16[1,1,256,4,1,256]{5,3,4,2,1,0:T(4,128)(2,1)} %param.6, f32[]{:T(128)S(6)} %copy.15, pred[4]{0:T(512)(128)(4,1)S(1)} %add_compare_fusion), kind=kLoop, calls=%fused_computation.2 | loop fusion | flops 1572864 | bytes 1572872 | tf_op jit(solution)/shard_map/transpose | solution.py:156
  2.9 0.7 fusion.2
  3.7 1.6 %collective-permute-start.2 = (bf16[1,256,256]{2,1,0:T(8,128)(2,1)}, bf16[1,256,256]{2,1,0:T(8,128)(2,1)S(1)}, u32[]{:S(2)}, u32[]{:S(2)}) collective-permute-start(bf16[1,256,256]{2,1,0:T(8,128)(2,1)} %get-tuple-element.21), channel_id=1, source_target_pairs={{0,2},{2,0},{1,3},{3,1},{4,6},{6,4},{5,7},{7,5},{8,10},{10,8},{9,1... | collective-permute-start | bytes 393224 | tf_op jit(solution)/shard_map/ppermute | solution.py:158
  5.3 0.5 collective-permute-start.8
  5.8 0.1 pad_add_fusion.where_ref
  5.9 1.7 %collective-permute-start = (f32[256,128]{1,0:T(8,128)S(1)}, f32[256,128]{1,0:T(8,128)S(1)}, u32[]{:S(2)}, u32[]{:S(2)}) collective-permute-start(f32[256,128]{1,0:T(8,128)S(1)} %slice_select_fusion), channel_id=1, source_target_pairs={{0,2},{2,0},{1,3},{3,1},{4,6},{6,4},{5,7},{7,5},{8,10},{10,8},{9,1... | collective-permute-start | bytes 393224 | tf_op jit(solution)/shard_map/ppermute | solution.py:160
  7.6 0.4 collective-permute-start.5
  8.0 0.0 collective-permute-start.1
  8.0 2.2 %collective-permute-done.2.rest_1_ = bf16[1,256,256]{2,1,0:T(8,128)(2,1)S(1)} collective-permute-done((bf16[1,256,256]{2,1,0:T(8,128)(2,1)}, bf16[1,256,256]{2,1,0:T(8,128)(2,1)S(1)}, u32[]{:S(2)}, u32[]{:S(2)}) %collective-permute-start.2) | collective-permute-done | bytes 131104 | tf_op jit(solution)/shard_map/ppermute | solution.py:158
  10.2 0.0 collective-permute-start.3
  10.2 8.4 %collective-permute-done.mate_rhs_ref = f32[256,128]{1,0:T(8,128)S(1)} collective-permute-done((f32[256,128]{1,0:T(8,128)S(1)}, f32[256,128]{1,0:T(8,128)S(1)}, u32[]{:S(2)}, u32[]{:S(2)}) %collective-permute-start) | collective-permute-done | bytes 131104 | tf_op jit(solution)/shard_map/ppermute | solution.py:160
  18.7 0.0 collective-permute-start.7
  18.7 0.6 shard_map.77.inv_ref
  19.3 0.9 %collective-permute-done.5.rest_4_ = bf16[1,256,256]{2,1,0:T(8,128)(2,1)S(1)} collective-permute-done((bf16[1,256,256]{2,1,0:T(8,128)(2,1)}, bf16[1,256,256]{2,1,0:T(8,128)(2,1)S(1)}, u32[]{:S(2)}, u32[]{:S(2)}) %collective-permute-start.5) | collective-permute-done | bytes 131104 | tf_op jit(solution)/shard_map/ppermute | solution.py:162
  20.2 0.0 collective-permute-start.4
  20.2 0.0 collective-permute-done.1.rest_0_.other3_ref
  20.2 0.5 collective-permute-start.6
  20.7 0.0 collective-permute-done.3.rest_2_
  20.7 0.0 copy-start.2
  20.8 0.6 shard_map.78.rest_7_
  21.3 0.7 collective-permute-start.11
  22.0 0.0 collective-permute-done.8.rest_7_
  22.0 0.2 collective-permute-start.9
  22.2 0.0 collective-permute-done.4.rest_3_.other2_ref
  22.2 0.7 collective-permute-start.10
  22.8 0.0 collective-permute-done.6.rest_5_
  22.9 0.0 collective-permute-done.11.rest_6_
  22.9 0.6 shard_map.79.rest_13_
  23.4 1.3 %collective-permute-start.13 = (bf16[2,256,128]{2,1,0:T(8,128)(2,1)S(1)}, bf16[2,256,128]{2,1,0:T(8,128)(2,1)S(1)}, u32[]{:S(2)}, u32[]{:S(2)}) collective-permute-start(bf16[2,256,128]{2,1,0:T(8,128)(2,1)S(1)} %shard_map.79.rest_13_), channel_id=1, source_target_pairs={{8,0},{10,2},{9,1},{11,3},{24,16},{26,18},{25,17},{27,19},{40,32},... | collective-permute-start | bytes 393224 | tf_op jit(solution)/shard_map/ppermute | solution.py:135
  24.7 1.3 %collective-permute-start.12 = (bf16[2,256,128]{2,1,0:T(8,128)(2,1)S(1)}, bf16[2,256,128]{2,1,0:T(8,128)(2,1)S(1)}, u32[]{:S(2)}, u32[]{:S(2)}) collective-permute-start(bf16[2,256,128]{2,1,0:T(8,128)(2,1)S(1)} %shard_map.79.rest_13_), channel_id=1, source_target_pairs={{8,6},{10,4},{14,0},{12,2},{9,7},{11,5},{15,1},{13,3},{24,22},{26,... | collective-permute-start | bytes 393224 | tf_op jit(solution)/shard_map/ppermute | solution.py:135
  26.0 0.1 copy.14
  26.1 0.0 collective-permute-done.7.rest_6_.other01_ref
  26.1 0.5 collective-permute-start.15
  26.6 0.0 collective-permute-done.10.rest_9_
  26.6 0.0 collective-permute-done.9.rest_8_
  26.6 12.3 %collective-permute-done.13.rest_12_ = bf16[2,256,128]{2,1,0:T(8,128)(2,1)S(1)} collective-permute-done((bf16[2,256,128]{2,1,0:T(8,128)(2,1)S(1)}, bf16[2,256,128]{2,1,0:T(8,128)(2,1)S(1)}, u32[]{:S(2)}, u32[]{:S(2)}) %collective-permute-start.13) | collective-permute-done | bytes 131104 | tf_op jit(solution)/shard_map/ppermute | solution.py:135
  38.9 0.0 collective-permute-done.12.rest_10_.rest_11_
  38.9 1.0 %shard_map.80 = (bf16[2,256,128]{2,1,0:T(8,128)(2,1)S(1)}, f32[2,256,128]{2,1,0:T(8,128)S(1)}) custom-call(s32[4]{0:T(128)S(1)} %pad_add_fusion.where_ref, bf16[2,2,256,256]{3,2,1,0:T(8,128)(2,1)S(1)} %shard_map.77.inv_ref, f32[256,256]{1,0:T(8,128)S(1)} %bitcast.26, f32[256,128]{1,0:T(8,128)S(1)} %collective-permute-done.mate_rhs_ref, ...), custom_call_target="tpu_custom_call" | custom-call | tf_op jit(solution)/shard_map/pallas_call | solution.py:120
  39.9 1.3 %collective-permute-start.14 = (bf16[2,256,128]{2,1,0:T(8,128)(2,1)S(1)}, bf16[2,256,128]{2,1,0:T(8,128)(2,1)S(1)}, u32[]{:S(2)}, u32[]{:S(2)}) collective-permute-start(bf16[2,256,128]{2,1,0:T(8,128)(2,1)S(1)} %get-tuple-element.14.rest_11_), channel_id=1, source_target_pairs={{6,0},{4,2},{7,1},{5,3},{22,16},{20,18},{23,17},{21,19},{38,32},{3... | collective-permute-start | bytes 393224 | tf_op jit(solution)/shard_map/ppermute | solution.py:135
  41.2 7.2 %collective-permute-done.14.rest_9_ = bf16[2,256,128]{2,1,0:T(8,128)(2,1)S(1)} collective-permute-done((bf16[2,256,128]{2,1,0:T(8,128)(2,1)S(1)}, bf16[2,256,128]{2,1,0:T(8,128)(2,1)S(1)}, u32[]{:S(2)}, u32[]{:S(2)}) %collective-permute-start.14) | collective-permute-done | bytes 131104 | tf_op jit(solution)/shard_map/ppermute | solution.py:135
  48.5 1.6 %shard_map.81 = bf16[2,256,128]{2,1,0:T(8,128)(2,1)S(1)} custom-call(s32[4]{0:T(128)S(1)} %pad_add_fusion.where_ref, bf16[2,2,256,256]{3,2,1,0:T(8,128)(2,1)S(1)} %shard_map.77.inv_ref, f32[256,256]{1,0:T(8,128)S(1)} %bitcast.27, f32[256,128]{1,0:T(8,128)S(1)} %collective-permute-done.mate_rhs_ref, bf16[4,256,256]{2,1,0:T(8,128)(2,1)S(1)} %fusion.1.own_ref.w_own_ref, ...), custom_call_target="tpu_custom_call" | custom-call | tf_op jit(solution)/shard_map/pallas_call | solution.py:120
  50.1 15.7 %all_to_all.10 = bf16[8,64,128]{2,1,0:T(8,128)(2,1)S(1)} all-to-all(bf16[8,64,128]{2,1,0:T(8,128)(2,1)S(1)} %bitcast.31), channel_id=1, replica_groups=mesh['z'=4,'yh'=2,'yl'=2,'xp'=2,'xq'=2,'col'=2] {'z','yh'}, dimensions={0} | all-to-all | bytes 262144 | tf_op jit(solution)/shard_map/all_to_all | solution.py:198
  65.7 0.0 collective-permute-done.15.z_other_ref
  65.7 0.2 broadcast_in_dim.25
  66.0 20.9 %all_to_all.11.x_ref = bf16[64,64,128]{2,1,0:T(8,128)(2,1)S(1)} all-to-all(bf16[64,64,128]{2,1,0:T(8,128)(2,1)S(1)} %broadcast_in_dim.25), channel_id=1, replica_groups=mesh['z'=4,'yh'=2,'yl'=2,'xp'=2,'xq'=2,'col'=2] {'z','yh','yl','xp','xq'}, dimensions={0} | all-to-all | bytes 2097152 | tf_op jit(solution)/shard_map/all_to_all | solution.py:203
  86.9 2.1 %shard_map.82 = (f32[256,256]{1,0:T(8,128)}, f32[256,256]{1,0:T(8,128)}) custom-call(s32[4]{0:T(128)S(1)} %pad_add_fusion.where_ref, bf16[64,64,128]{2,1,0:T(8,128)(2,1)S(1)} %all_to_all.11.x_ref, bf16[4,256,256]{2,1,0:T(8,128)(2,1)S(1)} %fusion.1.own_ref.w_own_ref, bf16[1,256,256]{2,1,0:T(8,128)(2,1)S(1)} %collective-permute-done.1.rest_0_.other3_ref, ...), custom_call_target="tpu_custom_call" | custom-call | tf_op jit(solution)/shard_map/pallas_call | solution.py:120
  (10 shorter events, 0.1 us)
Async XLA Ops:
  0.6 5.2 %copy-start = (f32[1,1,256,256]{3,2,1,0:T(8,128)S(1)}, f32[1,1,256,256]{3,2,1,0:T(8,128)}, u32[]{:S(2)}) copy-start(f32[1,1,256,256]{3,2,1,0:T(8,128)} %param.11) | copy-start | bytes 786436
  0.6 18.0 %copy-start.1 = (f32[4,2,256,256]{3,2,1,0:T(8,128)S(1)}, f32[4,2,256,256]{3,2,1,0:T(8,128)}, u32[]{:S(2)}) copy-start(f32[4,2,256,256]{3,2,1,0:T(8,128)} %inv_ref.1) | copy-start | bytes 6291460
  3.7 6.6 %collective-permute-start.2 = (bf16[1,256,256]{2,1,0:T(8,128)(2,1)}, bf16[1,256,256]{2,1,0:T(8,128)(2,1)S(1)}, u32[]{:S(2)}, u32[]{:S(2)}) collective-permute-start(bf16[1,256,256]{2,1,0:T(8,128)(2,1)} %get-tuple-element.21), channel_id=1, source_target_pairs={{0,2},{2,0},{1,3},{3,1},{4,6},{6,4},{5,7},{7,5},{8,10},{10,8},{9,1... | collective-permute-start | bytes 393224 | tf_op jit(solution)/shard_map/ppermute | solution.py:158
  5.3 16.7 %collective-permute-start.8 = (bf16[2,256,256]{2,1,0:T(8,128)(2,1)S(1)}, bf16[2,256,256]{2,1,0:T(8,128)(2,1)S(1)}, u32[]{:S(2)}, u32[]{:S(2)}) collective-permute-start(bf16[2,256,256]{2,1,0:T(8,128)(2,1)S(1)} %slice.30), channel_id=1, source_target_pairs={{0,2},{2,0},{1,3},{3,1},{4,6},{6,4},{5,7},{7,5},{8,10},{10,8},{9,1... | collective-permute-start | bytes 786440 | tf_op jit(solution)/shard_map/ppermute | solution.py:167
  5.8 14.4 %copy-start.3 = (bf16[1,256,256]{2,1,0:T(8,128)(2,1)S(1)}, bf16[1,256,256]{2,1,0:T(8,128)(2,1)}, u32[]{:S(2)}) copy-start(bf16[1,256,256]{2,1,0:T(8,128)(2,1)} %get-tuple-element.20) | copy-start | bytes 393220
  5.9 12.8 %collective-permute-start = (f32[256,128]{1,0:T(8,128)S(1)}, f32[256,128]{1,0:T(8,128)S(1)}, u32[]{:S(2)}, u32[]{:S(2)}) collective-permute-start(f32[256,128]{1,0:T(8,128)S(1)} %slice_select_fusion), channel_id=1, source_target_pairs={{0,2},{2,0},{1,3},{3,1},{4,6},{6,4},{5,7},{7,5},{8,10},{10,8},{9,1... | collective-permute-start | bytes 393224 | tf_op jit(solution)/shard_map/ppermute | solution.py:160
  7.6 12.6 %collective-permute-start.5 = (bf16[1,256,256]{2,1,0:T(8,128)(2,1)}, bf16[1,256,256]{2,1,0:T(8,128)(2,1)S(1)}, u32[]{:S(2)}, u32[]{:S(2)}) collective-permute-start(bf16[1,256,256]{2,1,0:T(8,128)(2,1)} %get-tuple-element.20), channel_id=1, source_target_pairs={{0,2},{2,0},{1,3},{3,1},{4,6},{6,4},{5,7},{7,5},{8,10},{10,8},{9,1... | collective-permute-start | bytes 393224 | tf_op jit(solution)/shard_map/ppermute | solution.py:162
  8.0 12.2 %collective-permute-start.1 = (bf16[1,256,256]{2,1,0:T(8,128)(2,1)}, bf16[1,256,256]{2,1,0:T(8,128)(2,1)S(1)}, u32[]{:S(2)}, u32[]{:S(2)}) collective-permute-start(bf16[1,256,256]{2,1,0:T(8,128)(2,1)} %get-tuple-element.21), channel_id=1, source_target_pairs={{0,1},{1,0},{2,3},{3,2},{4,5},{5,4},{6,7},{7,6},{8,9},{9,8},{10,11... | collective-permute-start | bytes 393224 | tf_op jit(solution)/shard_map/ppermute | solution.py:159
  10.2 10.5 %collective-permute-start.3 = (bf16[1,256,256]{2,1,0:T(8,128)(2,1)S(1)}, bf16[1,256,256]{2,1,0:T(8,128)(2,1)S(1)}, u32[]{:S(2)}, u32[]{:S(2)}) collective-permute-start(bf16[1,256,256]{2,1,0:T(8,128)(2,1)S(1)} %collective-permute-done.2.rest_1_), channel_id=1, source_target_pairs={{0,1},{1,0},{2,3},{3,2},{4,5},{5,4},{6,7},{7,6},{8,9},{9,8},{10,11... | collective-permute-start | bytes 393224 | tf_op jit(solution)/shard_map/ppermute | solution.py:161
  18.7 7.5 %collective-permute-start.7 = (bf16[2,256,256]{2,1,0:T(8,128)(2,1)S(1)}, bf16[2,256,256]{2,1,0:T(8,128)(2,1)S(1)}, u32[]{:S(2)}, u32[]{:S(2)}) collective-permute-start(bf16[2,256,256]{2,1,0:T(8,128)(2,1)S(1)} %slice.30), channel_id=1, source_target_pairs={{0,1},{1,0},{2,3},{3,2},{4,5},{5,4},{6,7},{7,6},{8,9},{9,8},{10,11... | collective-permute-start | bytes 786440 | tf_op jit(solution)/shard_map/ppermute | solution.py:168
  20.2 2.0 %collective-permute-start.4 = (bf16[1,256,256]{2,1,0:T(8,128)(2,1)S(1)}, bf16[1,256,256]{2,1,0:T(8,128)(2,1)S(1)}, u32[]{:S(2)}, u32[]{:S(2)}) collective-permute-start(bf16[1,256,256]{2,1,0:T(8,128)(2,1)S(1)} %copy-done.3), channel_id=1, source_target_pairs={{0,1},{1,0},{2,3},{3,2},{4,5},{5,4},{6,7},{7,6},{8,9},{9,8},{10,11... | collective-permute-start | bytes 393224 | tf_op jit(solution)/shard_map/ppermute | solution.py:163
  20.2 2.6 %collective-permute-start.6 = (bf16[1,256,256]{2,1,0:T(8,128)(2,1)S(1)}, bf16[1,256,256]{2,1,0:T(8,128)(2,1)S(1)}, u32[]{:S(2)}, u32[]{:S(2)}) collective-permute-start(bf16[1,256,256]{2,1,0:T(8,128)(2,1)S(1)} %collective-permute-done.5.rest_4_), channel_id=1, source_target_pairs={{0,1},{1,0},{2,3},{3,2},{4,5},{5,4},{6,7},{7,6},{8,9},{9,8},{10,11... | collective-permute-start | bytes 393224 | tf_op jit(solution)/shard_map/ppermute | solution.py:169
  20.7 5.3 %copy-start.2 = (bf16[1,1,256,4,1,256]{5,3,4,2,1,0:T(4,128)(2,1)S(1)}, bf16[1,1,256,4,1,256]{5,3,4,2,1,0:T(4,128)(2,1)}, u32[]{:S(2)}) copy-start(bf16[1,1,256,4,1,256]{5,3,4,2,1,0:T(4,128)(2,1)} %param.8) | copy-start | bytes 1572868
  21.3 1.5 %collective-permute-start.11 = (bf16[2,256,128]{2,1,0:T(8,128)(2,1)S(1)}, bf16[2,256,128]{2,1,0:T(8,128)(2,1)S(1)}, u32[]{:S(2)}, u32[]{:S(2)}) collective-permute-start(bf16[2,256,128]{2,1,0:T(8,128)(2,1)S(1)} %shard_map.78.rest_7_), channel_id=1, source_target_pairs={{14,8},{12,10},{15,9},{13,11},{30,24},{28,26},{31,25},{29,27},{46,... | collective-permute-start | bytes 393224 | tf_op jit(solution)/shard_map/ppermute | solution.py:135
  22.0 4.6 %collective-permute-start.9 = (bf16[2,256,256]{2,1,0:T(8,128)(2,1)S(1)}, bf16[2,256,256]{2,1,0:T(8,128)(2,1)S(1)}, u32[]{:S(2)}, u32[]{:S(2)}) collective-permute-start(bf16[2,256,256]{2,1,0:T(8,128)(2,1)S(1)} %collective-permute-done.8.rest_7_), channel_id=1, source_target_pairs={{0,1},{1,0},{2,3},{3,2},{4,5},{5,4},{6,7},{7,6},{8,9},{9,8},{10,11... | collective-permute-start | bytes 786440 | tf_op jit(solution)/shard_map/ppermute | solution.py:170
  22.2 4.5 %collective-permute-start.10 = (bf16[2,256,128]{2,1,0:T(8,128)(2,1)S(1)}, bf16[2,256,128]{2,1,0:T(8,128)(2,1)S(1)}, u32[]{:S(2)}, u32[]{:S(2)}) collective-permute-start(bf16[2,256,128]{2,1,0:T(8,128)(2,1)S(1)} %shard_map.78.rest_7_), channel_id=1, source_target_pairs={{14,6},{12,4},{15,7},{13,5},{30,22},{28,20},{31,23},{29,21},{46,38... | collective-permute-start | bytes 393224 | tf_op jit(solution)/shard_map/ppermute | solution.py:135
  23.4 15.5 %collective-permute-start.13 = (bf16[2,256,128]{2,1,0:T(8,128)(2,1)S(1)}, bf16[2,256,128]{2,1,0:T(8,128)(2,1)S(1)}, u32[]{:S(2)}, u32[]{:S(2)}) collective-permute-start(bf16[2,256,128]{2,1,0:T(8,128)(2,1)S(1)} %shard_map.79.rest_13_), channel_id=1, source_target_pairs={{8,0},{10,2},{9,1},{11,3},{24,16},{26,18},{25,17},{27,19},{40,32},... | collective-permute-start | bytes 393224 | tf_op jit(solution)/shard_map/ppermute | solution.py:135
  24.7 14.2 %collective-permute-start.12 = (bf16[2,256,128]{2,1,0:T(8,128)(2,1)S(1)}, bf16[2,256,128]{2,1,0:T(8,128)(2,1)S(1)}, u32[]{:S(2)}, u32[]{:S(2)}) collective-permute-start(bf16[2,256,128]{2,1,0:T(8,128)(2,1)S(1)} %shard_map.79.rest_13_), channel_id=1, source_target_pairs={{8,6},{10,4},{14,0},{12,2},{9,7},{11,5},{15,1},{13,3},{24,22},{26,... | collective-permute-start | bytes 393224 | tf_op jit(solution)/shard_map/ppermute | solution.py:135
  26.1 39.6 %collective-permute-start.15 = (bf16[4,256,256]{2,1,0:T(8,128)(2,1)S(1)}, bf16[4,256,256]{2,1,0:T(8,128)(2,1)S(1)}, u32[]{:S(2)}, u32[]{:S(2)}) collective-permute-start(bf16[4,256,256]{2,1,0:T(8,128)(2,1)S(1)} %bitcast.29), channel_id=1, source_target_pairs={{0,1},{1,0},{2,3},{3,2},{4,5},{5,4},{6,7},{7,6},{8,9},{9,8},{10,11... | collective-permute-start | bytes 1572872 | tf_op jit(solution)/shard_map/ppermute | solution.py:171
  39.9 8.5 %collective-permute-start.14 = (bf16[2,256,128]{2,1,0:T(8,128)(2,1)S(1)}, bf16[2,256,128]{2,1,0:T(8,128)(2,1)S(1)}, u32[]{:S(2)}, u32[]{:S(2)}) collective-permute-start(bf16[2,256,128]{2,1,0:T(8,128)(2,1)S(1)} %get-tuple-element.14.rest_11_), channel_id=1, source_target_pairs={{6,0},{4,2},{7,1},{5,3},{22,16},{20,18},{23,17},{21,19},{38,32},{3... | collective-permute-start | bytes 393224 | tf_op jit(solution)/shard_map/ppermute | solution.py:135

commit v4 on v3

--- a/solution.py
+++ b/solution.py
@@ -135,6 +135,14 @@
     return lax.ppermute(a, ("yl", "xp", "xq"), sends)
 
 
+def to_mate(a, full, partly):
+    sends = []
+    for m in full + partly:
+        for odd, core in ((0, 1),) if m in partly else ((0, 0), (0, 1), (1, 0), (1, 1)):
+            sends.append((4 * m + 2 * odd + core, 4 * m + 2 * (1 - odd) + core))
+    return lax.ppermute(a, ("yl", "xp", "xq", "col"), sends)
+
+
 def local(pencil_left, pencil_right, basis_panel, block_inverses, pencil_shift, start_vectors):
     row = lax.axis_index(ROWS)
     parity = lax.axis_index("col")
@@ -155,16 +163,16 @@
     both = left.astype(jnp.float32) - pencil_shift * right.astype(jnp.float32)
     own = jnp.transpose(jnp.where(live, both, 0.0).astype(jnp.bfloat16), (1, 0, 2))
     own3 = own[HALF - 1 :]
-    mate3 = lax.ppermute(own3, "xq", FLIP)
+    mate3 = to_mate(own3, [0, 1, 2], [3])
     other3 = lax.ppermute(own3, "col", FLIP)
     mate_rhs = lax.ppermute(jnp.where(lower_half, rhs[:, WIDE:], rhs[:, :WIDE]), "xq", FLIP)
     mate3_other = lax.ppermute(mate3, "col", FLIP)
-    mate2 = lax.ppermute(own[2:3], "xq", FLIP)
+    mate2 = to_mate(own[2:3], [0, 1], [2])
     other2 = lax.ppermute(own[2:3], "col", FLIP)
     inverses = call(
         split_kernel, jax.ShapeDtypeStruct((2, 2, NB, NB), jnp.bfloat16), [], where, block_inverses
     )
-    mate01 = lax.ppermute(own[:2], "xq", FLIP)
+    mate01 = to_mate(own[:2], [0], [1])
     other01 = lax.ppermute(own[:2], "col", FLIP)
     mate2_other = lax.ppermute(mate2, "col", FLIP)
     mate01_other = lax.ppermute(mate01, "col", FLIP)

time: 89.2 us -> 86.4 us (0.969)
  waiting for transfers between devices: 31.1 us -> 22.3 us
  starting transfers between devices: 10.6 us -> 16.8 us
    ppermute x3, starting transfers between devices: 2.53 us -> 8.15 us  [to_mate(): return lax.ppermute(a, ('yl', 'xp', 'xq', 'col'), sends)]
    ppermute x5, waiting for transfers between devices: 19.5 us -> 14.7 us  [to_pairs(): return lax.ppermute(a, ('yl', 'xp', 'xq'), sends)]
    ppermute x3, waiting for transfers between devices: 3.14 us -> 0.77 us  [to_mate(): return lax.ppermute(a, ('yl', 'xp', 'xq', 'col'), sends)]
    ppermute x1, waiting for transfers between devices: 8.42 us -> 6.8 us  [local(): lax.ppermute(jnp.where(lower_half, rhs[:, WIDE:], rhs[:, :WIDE]), 'xq', F...]
where the time goes in v4:
time: 86.4 us; the launch traced here: 86 us
  blocking collectives  36.2 us (42%)
  waiting for transfers between devices  22.3 us (26%)
  starting transfers between devices  16.8 us (19%)
  Pallas kernels  6.4 us (7%)
  between operations  1.7 us (2%)
  other arithmetic  1.56 us (2%)
  local copies, waits for them, and re-layouts  1.09 us (1%)
    all_to_all x1, blocking collectives, local(): lax.all_to_all(jnp.broadcast_to(spread[None], (count, *spread.shape)), RO...  20.2 us
    all_to_all x1, blocking collectives, local(): lax.all_to_all(x0.reshape(GROUPS, 2 * NB // GROUPS, WIDE), ('z', 'yh'), 0...  15.9 us
    ppermute x5, waiting for transfers between devices, to_pairs(): return lax.ppermute(a, ('yl', 'xp', 'xq'), sends)  14.7 us
    ppermute x3, starting transfers between devices, to_mate(): return lax.ppermute(a, ('yl', 'xp', 'xq', 'col'), sends)  8.15 us
    ppermute x1, waiting for transfers between devices, local(): lax.ppermute(jnp.where(lower_half, rhs[:, WIDE:], rhs[:, :WIDE]), 'xq', F...  6.8 us
    pallas_call x6, Pallas kernels, call(): pl.pallas_call(kernel, out_shape=outs, in_specs=[smem if a.dtype == jnp.i...  6.4 us
    ppermute x5, starting transfers between devices, to_pairs(): return lax.ppermute(a, ('yl', 'xp', 'xq'), sends)  5.2 us
  transfers between devices with their start and end apart: 16, of which 5 were waited for; matrix products, arithmetic and copies ran while one was open for 0% of the time, Pallas kernels for 5%

profile of v4, /device:TPU:0, one launch (start us, length us, event | category | flops | bytes accessed | tf_op | source)
XLA Modules:
  0.0 86.0 jit_solution(7784433532517564914)
XLA Ops:
  0.6 0.0 copy-start
  1.5 1.5 %fusion.1.own_ref.w_own_ref = bf16[4,256,256]{2,1,0:T(8,128)(2,1)S(1)} fusion(bf16[1,1,256,4,1,256]{5,3,4,2,1,0:T(4,128)(2,1)} %param.7, bf16[1,1,256,4,1,256]{5,3,4,2,1,0:T(4,128)(2,1)} %param.6, f32[]{:T(128)S(6)} %copy.15, pred[4]{0:T(512)(128)(4,1)S(1)} %add_compare_fusion), kind=kLoop, calls=%fused_computation.2 | loop fusion | flops 1572864 | bytes 1572872 | tf_op jit(solution)/shard_map/transpose | solution.py:164
  2.9 0.7 fusion.2
  3.7 3.5 %collective-permute-start.2 = (bf16[1,256,256]{2,1,0:T(8,128)(2,1)}, bf16[1,256,256]{2,1,0:T(8,128)(2,1)S(1)}, u32[]{:S(2)}, u32[]{:S(2)}) collective-permute-start(bf16[1,256,256]{2,1,0:T(8,128)(2,1)} %get-tuple-element.21), channel_id=1, source_target_pairs={{0,2},{1,3},{2,0},{3,1},{4,6},{5,7},{6,4},{7,5},{8,10},{9,11},{10,... | collective-permute-start | bytes 393224 | tf_op jit(solution)/shard_map/ppermute | solution.py:143
  7.2 2.3 %collective-permute-start.8 = (bf16[2,256,256]{2,1,0:T(8,128)(2,1)S(1)}, bf16[2,256,256]{2,1,0:T(8,128)(2,1)S(1)}, u32[]{:S(2)}, u32[]{:S(2)}) collective-permute-start(bf16[2,256,256]{2,1,0:T(8,128)(2,1)S(1)} %slice.30), channel_id=1, source_target_pairs={{0,2},{1,3},{2,0},{3,1},{5,7},{16,18},{17,19},{18,16},{19,17},{21,... | collective-permute-start | bytes 786440 | tf_op jit(solution)/shard_map/ppermute | solution.py:143
  9.5 0.0 copy-start.3
  9.6 0.1 pad_add_fusion.where_ref
  9.7 1.7 %collective-permute-start = (f32[256,128]{1,0:T(8,128)S(1)}, f32[256,128]{1,0:T(8,128)S(1)}, u32[]{:S(2)}, u32[]{:S(2)}) collective-permute-start(f32[256,128]{1,0:T(8,128)S(1)} %slice_select_fusion), channel_id=1, source_target_pairs={{0,2},{2,0},{1,3},{3,1},{4,6},{6,4},{5,7},{7,5},{8,10},{10,8},{9,1... | collective-permute-start | bytes 393224 | tf_op jit(solution)/shard_map/ppermute | solution.py:168
  11.3 2.3 %collective-permute-start.5 = (bf16[1,256,256]{2,1,0:T(8,128)(2,1)}, bf16[1,256,256]{2,1,0:T(8,128)(2,1)S(1)}, u32[]{:S(2)}, u32[]{:S(2)}) collective-permute-start(bf16[1,256,256]{2,1,0:T(8,128)(2,1)} %get-tuple-element.20), channel_id=1, source_target_pairs={{0,2},{1,3},{2,0},{3,1},{4,6},{5,7},{6,4},{7,5},{9,11},{16,18},{17... | collective-permute-start | bytes 393224 | tf_op jit(solution)/shard_map/ppermute | solution.py:143
  13.7 0.1 collective-permute-start.1
  13.8 0.0 collective-permute-done.2.rest_1_
  13.8 0.5 collective-permute-start.3
  14.3 6.8 %collective-permute-done.mate_rhs_ref = f32[256,128]{1,0:T(8,128)S(1)} collective-permute-done((f32[256,128]{1,0:T(8,128)S(1)}, f32[256,128]{1,0:T(8,128)S(1)}, u32[]{:S(2)}, u32[]{:S(2)}) %collective-permute-start) | collective-permute-done | bytes 131104 | tf_op jit(solution)/shard_map/ppermute | solution.py:168
  21.1 0.0 collective-permute-start.7
  21.1 0.6 shard_map.77.inv_ref
  21.7 0.8 collective-permute-done.5.rest_4_
  22.5 0.0 collective-permute-start.4
  22.5 0.0 collective-permute-done.1.rest_0_.other3_ref
  22.5 0.5 collective-permute-start.6
  23.0 0.0 collective-permute-done.3.rest_2_
  23.0 0.0 copy-start.2
  23.0 0.6 shard_map.78.rest_7_
  23.6 0.7 collective-permute-start.11
  24.3 0.0 collective-permute-done.8.rest_7_
  24.3 0.2 collective-permute-start.9
  24.4 0.0 collective-permute-done.4.rest_3_.other2_ref
  24.4 0.7 collective-permute-start.10
  25.1 0.0 collective-permute-done.6.rest_5_
  25.1 0.0 collective-permute-done.11.rest_6_
  25.1 0.6 shard_map.79.rest_13_
  25.7 1.3 %collective-permute-start.13 = (bf16[2,256,128]{2,1,0:T(8,128)(2,1)S(1)}, bf16[2,256,128]{2,1,0:T(8,128)(2,1)S(1)}, u32[]{:S(2)}, u32[]{:S(2)}) collective-permute-start(bf16[2,256,128]{2,1,0:T(8,128)(2,1)S(1)} %shard_map.79.rest_13_), channel_id=1, source_target_pairs={{8,0},{10,2},{9,1},{11,3},{24,16},{26,18},{25,17},{27,19},{40,32},... | collective-permute-start | bytes 393224 | tf_op jit(solution)/shard_map/ppermute | solution.py:135
  27.0 1.3 %collective-permute-start.12 = (bf16[2,256,128]{2,1,0:T(8,128)(2,1)S(1)}, bf16[2,256,128]{2,1,0:T(8,128)(2,1)S(1)}, u32[]{:S(2)}, u32[]{:S(2)}) collective-permute-start(bf16[2,256,128]{2,1,0:T(8,128)(2,1)S(1)} %shard_map.79.rest_13_), channel_id=1, source_target_pairs={{8,6},{10,4},{14,0},{12,2},{9,7},{11,5},{15,1},{13,3},{24,22},{26,... | collective-permute-start | bytes 393224 | tf_op jit(solution)/shard_map/ppermute | solution.py:135
  28.3 0.1 copy.14
  28.4 0.0 collective-permute-done.7.rest_6_.other01_ref
  28.4 0.5 collective-permute-start.15
  28.9 0.0 collective-permute-done.10.rest_9_
  28.9 0.0 collective-permute-done.9.rest_8_
  28.9 4.5 %collective-permute-done.13.rest_12_ = bf16[2,256,128]{2,1,0:T(8,128)(2,1)S(1)} collective-permute-done((bf16[2,256,128]{2,1,0:T(8,128)(2,1)S(1)}, bf16[2,256,128]{2,1,0:T(8,128)(2,1)S(1)}, u32[]{:S(2)}, u32[]{:S(2)}) %collective-permute-start.13) | collective-permute-done | bytes 131104 | tf_op jit(solution)/shard_map/ppermute | solution.py:135
  33.4 3.4 %collective-permute-done.12.rest_10_.rest_11_ = bf16[2,256,128]{2,1,0:T(8,128)(2,1)S(1)} collective-permute-done((bf16[2,256,128]{2,1,0:T(8,128)(2,1)S(1)}, bf16[2,256,128]{2,1,0:T(8,128)(2,1)S(1)}, u32[]{:S(2)}, u32[]{:S(2)}) %collective-permute-start.12) | collective-permute-done | bytes 131104 | tf_op jit(solution)/shard_map/ppermute | solution.py:135
  36.8 1.0 %shard_map.80 = (bf16[2,256,128]{2,1,0:T(8,128)(2,1)S(1)}, f32[2,256,128]{2,1,0:T(8,128)S(1)}) custom-call(s32[4]{0:T(128)S(1)} %pad_add_fusion.where_ref, bf16[2,2,256,256]{3,2,1,0:T(8,128)(2,1)S(1)} %shard_map.77.inv_ref, f32[256,256]{1,0:T(8,128)S(1)} %bitcast.26, f32[256,128]{1,0:T(8,128)S(1)} %collective-permute-done.mate_rhs_ref, ...), custom_call_target="tpu_custom_call" | custom-call | tf_op jit(solution)/shard_map/pallas_call | solution.py:120
  37.8 1.3 %collective-permute-start.14 = (bf16[2,256,128]{2,1,0:T(8,128)(2,1)S(1)}, bf16[2,256,128]{2,1,0:T(8,128)(2,1)S(1)}, u32[]{:S(2)}, u32[]{:S(2)}) collective-permute-start(bf16[2,256,128]{2,1,0:T(8,128)(2,1)S(1)} %get-tuple-element.14.rest_11_), channel_id=1, source_target_pairs={{6,0},{4,2},{7,1},{5,3},{22,16},{20,18},{23,17},{21,19},{38,32},{3... | collective-permute-start | bytes 393224 | tf_op jit(solution)/shard_map/ppermute | solution.py:135
  39.1 6.8 %collective-permute-done.14.rest_9_ = bf16[2,256,128]{2,1,0:T(8,128)(2,1)S(1)} collective-permute-done((bf16[2,256,128]{2,1,0:T(8,128)(2,1)S(1)}, bf16[2,256,128]{2,1,0:T(8,128)(2,1)S(1)}, u32[]{:S(2)}, u32[]{:S(2)}) %collective-permute-start.14) | collective-permute-done | bytes 131104 | tf_op jit(solution)/shard_map/ppermute | solution.py:135
  45.9 1.6 %shard_map.81 = bf16[2,256,128]{2,1,0:T(8,128)(2,1)S(1)} custom-call(s32[4]{0:T(128)S(1)} %pad_add_fusion.where_ref, bf16[2,2,256,256]{3,2,1,0:T(8,128)(2,1)S(1)} %shard_map.77.inv_ref, f32[256,256]{1,0:T(8,128)S(1)} %bitcast.27, f32[256,128]{1,0:T(8,128)S(1)} %collective-permute-done.mate_rhs_ref, bf16[4,256,256]{2,1,0:T(8,128)(2,1)S(1)} %fusion.1.own_ref.w_own_ref, ...), custom_call_target="tpu_custom_call" | custom-call | tf_op jit(solution)/shard_map/pallas_call | solution.py:120
  47.5 15.9 %all_to_all.10 = bf16[8,64,128]{2,1,0:T(8,128)(2,1)S(1)} all-to-all(bf16[8,64,128]{2,1,0:T(8,128)(2,1)S(1)} %bitcast.31), channel_id=1, replica_groups=mesh['z'=4,'yh'=2,'yl'=2,'xp'=2,'xq'=2,'col'=2] {'z','yh'}, dimensions={0} | all-to-all | bytes 262144 | tf_op jit(solution)/shard_map/all_to_all | solution.py:206
  63.5 0.0 collective-permute-done.15.z_other_ref
  63.5 0.2 broadcast_in_dim.25
  63.7 20.2 %all_to_all.11.x_ref = bf16[64,64,128]{2,1,0:T(8,128)(2,1)S(1)} all-to-all(bf16[64,64,128]{2,1,0:T(8,128)(2,1)S(1)} %broadcast_in_dim.25), channel_id=1, replica_groups=mesh['z'=4,'yh'=2,'yl'=2,'xp'=2,'xq'=2,'col'=2] {'z','yh','yl','xp','xq'}, dimensions={0} | all-to-all | bytes 2097152 | tf_op jit(solution)/shard_map/all_to_all | solution.py:211
  84.0 2.1 %shard_map.82 = (f32[256,256]{1,0:T(8,128)}, f32[256,256]{1,0:T(8,128)}) custom-call(s32[4]{0:T(128)S(1)} %pad_add_fusion.where_ref, bf16[64,64,128]{2,1,0:T(8,128)(2,1)S(1)} %all_to_all.11.x_ref, bf16[4,256,256]{2,1,0:T(8,128)(2,1)S(1)} %fusion.1.own_ref.w_own_ref, bf16[1,256,256]{2,1,0:T(8,128)(2,1)S(1)} %collective-permute-done.1.rest_0_.other3_ref, ...), custom_call_target="tpu_custom_call" | custom-call | tf_op jit(solution)/shard_map/pallas_call | solution.py:120
  (10 shorter events, 0.1 us)
Async XLA Ops:
  0.6 9.0 %copy-start = (f32[1,1,256,256]{3,2,1,0:T(8,128)S(1)}, f32[1,1,256,256]{3,2,1,0:T(8,128)}, u32[]{:S(2)}) copy-start(f32[1,1,256,256]{3,2,1,0:T(8,128)} %param.11) | copy-start | bytes 786436
  0.6 20.4 %copy-start.1 = (f32[4,2,256,256]{3,2,1,0:T(8,128)S(1)}, f32[4,2,256,256]{3,2,1,0:T(8,128)}, u32[]{:S(2)}) copy-start(f32[4,2,256,256]{3,2,1,0:T(8,128)} %inv_ref.1) | copy-start | bytes 6291460
  3.7 10.1 %collective-permute-start.2 = (bf16[1,256,256]{2,1,0:T(8,128)(2,1)}, bf16[1,256,256]{2,1,0:T(8,128)(2,1)S(1)}, u32[]{:S(2)}, u32[]{:S(2)}) collective-permute-start(bf16[1,256,256]{2,1,0:T(8,128)(2,1)} %get-tuple-element.21), channel_id=1, source_target_pairs={{0,2},{1,3},{2,0},{3,1},{4,6},{5,7},{6,4},{7,5},{8,10},{9,11},{10,... | collective-permute-start | bytes 393224 | tf_op jit(solution)/shard_map/ppermute | solution.py:143
  7.2 17.1 %collective-permute-start.8 = (bf16[2,256,256]{2,1,0:T(8,128)(2,1)S(1)}, bf16[2,256,256]{2,1,0:T(8,128)(2,1)S(1)}, u32[]{:S(2)}, u32[]{:S(2)}) collective-permute-start(bf16[2,256,256]{2,1,0:T(8,128)(2,1)S(1)} %slice.30), channel_id=1, source_target_pairs={{0,2},{1,3},{2,0},{3,1},{5,7},{16,18},{17,19},{18,16},{19,17},{21,... | collective-permute-start | bytes 786440 | tf_op jit(solution)/shard_map/ppermute | solution.py:143
  9.5 12.9 %copy-start.3 = (bf16[1,256,256]{2,1,0:T(8,128)(2,1)S(1)}, bf16[1,256,256]{2,1,0:T(8,128)(2,1)}, u32[]{:S(2)}) copy-start(bf16[1,256,256]{2,1,0:T(8,128)(2,1)} %get-tuple-element.20) | copy-start | bytes 393220
  9.7 11.4 %collective-permute-start = (f32[256,128]{1,0:T(8,128)S(1)}, f32[256,128]{1,0:T(8,128)S(1)}, u32[]{:S(2)}, u32[]{:S(2)}) collective-permute-start(f32[256,128]{1,0:T(8,128)S(1)} %slice_select_fusion), channel_id=1, source_target_pairs={{0,2},{2,0},{1,3},{3,1},{4,6},{6,4},{5,7},{7,5},{8,10},{10,8},{9,1... | collective-permute-start | bytes 393224 | tf_op jit(solution)/shard_map/ppermute | solution.py:168
  11.3 11.1 %collective-permute-start.5 = (bf16[1,256,256]{2,1,0:T(8,128)(2,1)}, bf16[1,256,256]{2,1,0:T(8,128)(2,1)S(1)}, u32[]{:S(2)}, u32[]{:S(2)}) collective-permute-start(bf16[1,256,256]{2,1,0:T(8,128)(2,1)} %get-tuple-element.20), channel_id=1, source_target_pairs={{0,2},{1,3},{2,0},{3,1},{4,6},{5,7},{6,4},{7,5},{9,11},{16,18},{17... | collective-permute-start | bytes 393224 | tf_op jit(solution)/shard_map/ppermute | solution.py:143
  13.7 8.8 %collective-permute-start.1 = (bf16[1,256,256]{2,1,0:T(8,128)(2,1)}, bf16[1,256,256]{2,1,0:T(8,128)(2,1)S(1)}, u32[]{:S(2)}, u32[]{:S(2)}) collective-permute-start(bf16[1,256,256]{2,1,0:T(8,128)(2,1)} %get-tuple-element.21), channel_id=1, source_target_pairs={{0,1},{1,0},{2,3},{3,2},{4,5},{5,4},{6,7},{7,6},{8,9},{9,8},{10,11... | collective-permute-start | bytes 393224 | tf_op jit(solution)/shard_map/ppermute | solution.py:167
  13.8 9.2 %collective-permute-start.3 = (bf16[1,256,256]{2,1,0:T(8,128)(2,1)S(1)}, bf16[1,256,256]{2,1,0:T(8,128)(2,1)S(1)}, u32[]{:S(2)}, u32[]{:S(2)}) collective-permute-start(bf16[1,256,256]{2,1,0:T(8,128)(2,1)S(1)} %collective-permute-done.2.rest_1_), channel_id=1, source_target_pairs={{0,1},{1,0},{2,3},{3,2},{4,5},{5,4},{6,7},{7,6},{8,9},{9,8},{10,11... | collective-permute-start | bytes 393224 | tf_op jit(solution)/shard_map/ppermute | solution.py:169
  21.1 7.3 %collective-permute-start.7 = (bf16[2,256,256]{2,1,0:T(8,128)(2,1)S(1)}, bf16[2,256,256]{2,1,0:T(8,128)(2,1)S(1)}, u32[]{:S(2)}, u32[]{:S(2)}) collective-permute-start(bf16[2,256,256]{2,1,0:T(8,128)(2,1)S(1)} %slice.30), channel_id=1, source_target_pairs={{0,1},{1,0},{2,3},{3,2},{4,5},{5,4},{6,7},{7,6},{8,9},{9,8},{10,11... | collective-permute-start | bytes 786440 | tf_op jit(solution)/shard_map/ppermute | solution.py:176
  22.5 2.0 %collective-permute-start.4 = (bf16[1,256,256]{2,1,0:T(8,128)(2,1)S(1)}, bf16[1,256,256]{2,1,0:T(8,128)(2,1)S(1)}, u32[]{:S(2)}, u32[]{:S(2)}) collective-permute-start(bf16[1,256,256]{2,1,0:T(8,128)(2,1)S(1)} %copy-done.3), channel_id=1, source_target_pairs={{0,1},{1,0},{2,3},{3,2},{4,5},{5,4},{6,7},{7,6},{8,9},{9,8},{10,11... | collective-permute-start | bytes 393224 | tf_op jit(solution)/shard_map/ppermute | solution.py:171
  22.5 2.6 %collective-permute-start.6 = (bf16[1,256,256]{2,1,0:T(8,128)(2,1)S(1)}, bf16[1,256,256]{2,1,0:T(8,128)(2,1)S(1)}, u32[]{:S(2)}, u32[]{:S(2)}) collective-permute-start(bf16[1,256,256]{2,1,0:T(8,128)(2,1)S(1)} %collective-permute-done.5.rest_4_), channel_id=1, source_target_pairs={{0,1},{1,0},{2,3},{3,2},{4,5},{5,4},{6,7},{7,6},{8,9},{9,8},{10,11... | collective-permute-start | bytes 393224 | tf_op jit(solution)/shard_map/ppermute | solution.py:177
  23.0 5.3 %copy-start.2 = (bf16[1,1,256,4,1,256]{5,3,4,2,1,0:T(4,128)(2,1)S(1)}, bf16[1,1,256,4,1,256]{5,3,4,2,1,0:T(4,128)(2,1)}, u32[]{:S(2)}) copy-start(bf16[1,1,256,4,1,256]{5,3,4,2,1,0:T(4,128)(2,1)} %param.8) | copy-start | bytes 1572868
  23.6 1.5 %collective-permute-start.11 = (bf16[2,256,128]{2,1,0:T(8,128)(2,1)S(1)}, bf16[2,256,128]{2,1,0:T(8,128)(2,1)S(1)}, u32[]{:S(2)}, u32[]{:S(2)}) collective-permute-start(bf16[2,256,128]{2,1,0:T(8,128)(2,1)S(1)} %shard_map.78.rest_7_), channel_id=1, source_target_pairs={{14,8},{12,10},{15,9},{13,11},{30,24},{28,26},{31,25},{29,27},{46,... | collective-permute-start | bytes 393224 | tf_op jit(solution)/shard_map/ppermute | solution.py:135
  24.3 4.6 %collective-permute-start.9 = (bf16[2,256,256]{2,1,0:T(8,128)(2,1)S(1)}, bf16[2,256,256]{2,1,0:T(8,128)(2,1)S(1)}, u32[]{:S(2)}, u32[]{:S(2)}) collective-permute-start(bf16[2,256,256]{2,1,0:T(8,128)(2,1)S(1)} %collective-permute-done.8.rest_7_), channel_id=1, source_target_pairs={{0,1},{1,0},{2,3},{3,2},{4,5},{5,4},{6,7},{7,6},{8,9},{9,8},{10,11... | collective-permute-start | bytes 786440 | tf_op jit(solution)/shard_map/ppermute | solution.py:178
  24.4 4.5 %collective-permute-start.10 = (bf16[2,256,128]{2,1,0:T(8,128)(2,1)S(1)}, bf16[2,256,128]{2,1,0:T(8,128)(2,1)S(1)}, u32[]{:S(2)}, u32[]{:S(2)}) collective-permute-start(bf16[2,256,128]{2,1,0:T(8,128)(2,1)S(1)} %shard_map.78.rest_7_), channel_id=1, source_target_pairs={{14,6},{12,4},{15,7},{13,5},{30,22},{28,20},{31,23},{29,21},{46,38... | collective-permute-start | bytes 393224 | tf_op jit(solution)/shard_map/ppermute | solution.py:135
  25.7 7.7 %collective-permute-start.13 = (bf16[2,256,128]{2,1,0:T(8,128)(2,1)S(1)}, bf16[2,256,128]{2,1,0:T(8,128)(2,1)S(1)}, u32[]{:S(2)}, u32[]{:S(2)}) collective-permute-start(bf16[2,256,128]{2,1,0:T(8,128)(2,1)S(1)} %shard_map.79.rest_13_), channel_id=1, source_target_pairs={{8,0},{10,2},{9,1},{11,3},{24,16},{26,18},{25,17},{27,19},{40,32},... | collective-permute-start | bytes 393224 | tf_op jit(solution)/shard_map/ppermute | solution.py:135
  27.0 9.8 %collective-permute-start.12 = (bf16[2,256,128]{2,1,0:T(8,128)(2,1)S(1)}, bf16[2,256,128]{2,1,0:T(8,128)(2,1)S(1)}, u32[]{:S(2)}, u32[]{:S(2)}) collective-permute-start(bf16[2,256,128]{2,1,0:T(8,128)(2,1)S(1)} %shard_map.79.rest_13_), channel_id=1, source_target_pairs={{8,6},{10,4},{14,0},{12,2},{9,7},{11,5},{15,1},{13,3},{24,22},{26,... | collective-permute-start | bytes 393224 | tf_op jit(solution)/shard_map/ppermute | solution.py:135
  28.4 35.1 %collective-permute-start.15 = (bf16[4,256,256]{2,1,0:T(8,128)(2,1)S(1)}, bf16[4,256,256]{2,1,0:T(8,128)(2,1)S(1)}, u32[]{:S(2)}, u32[]{:S(2)}) collective-permute-start(bf16[4,256,256]{2,1,0:T(8,128)(2,1)S(1)} %bitcast.29), channel_id=1, source_target_pairs={{0,1},{1,0},{2,3},{3,2},{4,5},{5,4},{6,7},{7,6},{8,9},{9,8},{10,11... | collective-permute-start | bytes 1572872 | tf_op jit(solution)/shard_map/ppermute | solution.py:179
  37.8 8.1 %collective-permute-start.14 = (bf16[2,256,128]{2,1,0:T(8,128)(2,1)S(1)}, bf16[2,256,128]{2,1,0:T(8,128)(2,1)S(1)}, u32[]{:S(2)}, u32[]{:S(2)}) collective-permute-start(bf16[2,256,128]{2,1,0:T(8,128)(2,1)S(1)} %get-tuple-element.14.rest_11_), channel_id=1, source_target_pairs={{6,0},{4,2},{7,1},{5,3},{22,16},{20,18},{23,17},{21,19},{38,32},{3... | collective-permute-start | bytes 393224 | tf_op jit(solution)/shard_map/ppermute | solution.py:135

commit v5 on v3

--- a/solution.py
+++ b/solution.py
@@ -12,8 +12,9 @@
 HALF = STEPS // 2
 NB = 256
 WIDE = NB // 2
-GROUPS = 8
+DEPTH = 4
 ROWS = ("z", "yh", "yl", "xp", "xq")
+PLANE = ("z", "yl", "xp", "xq")
 FLIP = [(0, 1), (1, 0)]
 
 
@@ -92,26 +93,31 @@
             sum_ref[0], sum_ref[1] = accs
 
 
-def final_kernel(
-    where_ref, x_ref, w_own_ref, other3_ref, other2_ref, other01_ref, z_own_ref, z_other_ref,
-    rhs_ref, pending_ref, image_ref,
+def pack_kernel(
+    w_own_ref, other3_ref, other2_ref, other01_ref, z_own_ref, z_other_ref, out_ref
 ):
+    for b in range(HALF):
+        other = other01_ref[b] if b < 2 else (other2_ref, other3_ref)[b - 2][0]
+        blocks = ((w_own_ref[b], other), (z_own_ref[b], z_other_ref[b]))
+        for n in range(2):
+            for side in range(2):
+                at = (side * HALF + b) * NB
+                out_ref[n, :, at : at + NB] = blocks[n][side]
+
+
+def final_kernel(where_ref, x_ref, rows_ref, rhs_ref, pending_ref, image_ref, order_ref):
     parity = where_ref[3]
-    pending = rhs_ref[...]
-    image = jnp.zeros_like(pending)
     for b in range(HALF):
         yl, xp = b // 2, b % 2
-        own, other = w_own_ref[b], (other01_ref[b] if b < 2 else (other2_ref, other3_ref)[b - 2][0])
-        for w, z, p in ((own, z_own_ref, parity), (other, z_other_ref, 1 - parity)):
-            columns = []
+        for side, p in enumerate((parity, 1 - parity)):
             for half in range(2):
-                at = [(((4 * p + i) * 2 + yl) * 2 + xp) * 2 + (half ^ xp) for i in range(4)]
-                columns.append(jnp.concatenate([x_ref[n] for n in at], 0))
-            x = jnp.concatenate(columns, 1)
-            pending = pending - dot(w, x)
-            image = image + dot(z[b], x)
-    pending_ref[...] = pending
-    image_ref[...] = image
+                for i in range(2):
+                    at = (((2 * p + i) * 2 + yl) * 2 + xp) * 2 + (half ^ xp)
+                    to = (side * HALF + b) * NB + i * WIDE
+                    order_ref[to : to + WIDE, half * WIDE : (half + 1) * WIDE] = x_ref[at]
+    x = order_ref[...]
+    pending_ref[...] = rhs_ref[...] - dot(rows_ref[0], x)
+    image_ref[...] = dot(rows_ref[1], x)
 
 
 def call(kernel, outs, scratch, *args, limit=12 << 20):
@@ -193,21 +199,27 @@
     d = to_pairs(x2, [(2, 0)])
     x1, acc = solve(1, [(3, b), (2, c)], [(3, c), (2, d)], x2)
     e = to_pairs(x1, [(1, 0)])
+    rows = call(
+        pack_kernel, jax.ShapeDtypeStruct((2, NB, STEPS * NB), jnp.bfloat16), [],
+        own, other3, other2, other01, own_z, other_z,
+    )
     x0 = solve(0, [(1, e)], [], acc, x1)
 
+    quarters = x0.reshape(DEPTH, 1, 2 * NB // DEPTH, WIDE)
+    quarters = jnp.broadcast_to(quarters, (DEPTH, 2, *quarters.shape[2:]))
     spread = lax.all_to_all(
-        x0.reshape(GROUPS, 2 * NB // GROUPS, WIDE), ("z", "yh"), 0, 0, tiled=True
-    )[GROUPS - 1]
-    spread, other_z = lax.optimization_barrier((spread, other_z))
-    count = lax.axis_size(ROWS)
+        quarters.reshape(2 * DEPTH, *quarters.shape[2:]), ("z", "yh"), 0, 0, tiled=True
+    )[2 * DEPTH - 1]
+    spread, rows = lax.optimization_barrier((spread, rows))
+    count = lax.axis_size(PLANE)
     every = lax.all_to_all(
-        jnp.broadcast_to(spread[None], (count, *spread.shape)), ROWS, 0, 0, tiled=True
+        jnp.broadcast_to(spread[None], (count, *spread.shape)), PLANE, 0, 0, tiled=True
     )
 
     out = jax.ShapeDtypeStruct((NB, NB), jnp.float32)
     pending, image = call(
-        final_kernel, (out, out), [],
-        where, every, own, other3, other2, other01, own_z, other_z, rhs,
+        final_kernel, (out, out), [pltpu.VMEM((STEPS * NB, NB), jnp.bfloat16)],
+        where, every, rows, rhs,
     )
     return pending.reshape(1, 1, NB, NB), image.reshape(1, 1, NB, NB)
 

time: 89.2 us -> 90.3 us (1.012)
  blocking collectives: 36.5 us -> 18 us
  starting transfers between devices: 10.6 us -> 18.3 us
  local copies, waits for them, and re-layouts: 1.09 us -> 7.04 us
  waiting for transfers between devices: 31.1 us -> 36.5 us
    all_to_all x2 -> x1, blocking collectives: 36.5 us -> 18 us  [local(): lax.all_to_all(jnp.broadcast_to(spread[None], (count, *spread.shape)), PL...]
    all_to_all x0 -> x1, starting transfers between devices: none -> 7.65 us  [local(): lax.all_to_all(quarters.reshape(2 * DEPTH, *quarters.shape[2:]), ('z', 'y...]
    all_to_all x0 -> x1, waiting for transfers between devices: none -> 5.71 us  [local(): lax.all_to_all(quarters.reshape(2 * DEPTH, *quarters.shape[2:]), ('z', 'y...]
    unnamed x9 -> x15, local copies, waits for them, and re-layouts: 0.09 us -> 4.56 us
    ppermute x1, waiting for transfers between devices: 2.24 us -> 0.56 us  [local(): mate3 = lax.ppermute(own3, 'xq', FLIP)]
    ppermute x1, waiting for transfers between devices: 0.9 us -> 1.81 us  [local(): mate2 = lax.ppermute(own[2:3], 'xq', FLIP)]
    pallas_call x6 -> x7, Pallas kernels: 6.4 us -> 6.68 us  [call(): pl.pallas_call(kernel, out_shape=outs, in_specs=[smem if a.dtype == jnp.i...]
  transfers between devices with their start and end apart: 16 -> 17, of which waited for: 5 -> 6; matrix products, arithmetic and copies ran while one was open for 0% -> 2% of each run, Pallas kernels for 5% -> 5%
where the time goes in v5:
time: 90.3 us; the launch traced here: 89.7 us
  waiting for transfers between devices  36.5 us (40%)
  starting transfers between devices  18.3 us (20%)
  blocking collectives  18 us (20%)
  local copies, waits for them, and re-layouts  7.04 us (8%)
  Pallas kernels  6.68 us (7%)
  other arithmetic  1.56 us (2%)
  between operations  1.56 us (2%)
    ppermute x5, waiting for transfers between devices, to_pairs(): return lax.ppermute(a, ('yl', 'xp', 'xq'), sends)  19.4 us
    all_to_all x1, blocking collectives, local(): lax.all_to_all(jnp.broadcast_to(spread[None], (count, *spread.shape)), PL...  18 us
    ppermute x1, waiting for transfers between devices, local(): lax.ppermute(jnp.where(lower_half, rhs[:, WIDE:], rhs[:, :WIDE]), 'xq', F...  9 us
    all_to_all x1, starting transfers between devices, local(): lax.all_to_all(quarters.reshape(2 * DEPTH, *quarters.shape[2:]), ('z', 'y...  7.65 us
    pallas_call x7, Pallas kernels, call(): pl.pallas_call(kernel, out_shape=outs, in_specs=[smem if a.dtype == jnp.i...  6.68 us
    all_to_all x1, waiting for transfers between devices, local(): lax.all_to_all(quarters.reshape(2 * DEPTH, *quarters.shape[2:]), ('z', 'y...  5.71 us
    ppermute x5, starting transfers between devices, to_pairs(): return lax.ppermute(a, ('yl', 'xp', 'xq'), sends)  5.2 us
    unnamed x15, local copies, waits for them, and re-layouts  4.56 us
  transfers between devices with their start and end apart: 17, of which 6 were waited for; matrix products, arithmetic and copies ran while one was open for 2% of the time, Pallas kernels for 5%

profile of v5, /device:TPU:0, one launch (start us, length us, event | category | flops | bytes accessed | tf_op | source)
XLA Modules:
  0.0 89.7 jit_solution(2606640354294555819)
XLA Ops:
  1.4 1.5 %fusion.1.own_ref.w_own_ref = bf16[4,256,256]{2,1,0:T(8,128)(2,1)S(1)} fusion(bf16[1,1,256,4,1,256]{5,3,4,2,1,0:T(4,128)(2,1)} %param.7, bf16[1,1,256,4,1,256]{5,3,4,2,1,0:T(4,128)(2,1)} %param.6, f32[]{:T(128)S(6)} %copy.15, pred[4]{0:T(512)(128)(4,1)S(1)} %add_compare_fusion), kind=kLoop, calls=%fused_computation.2 | loop fusion | flops 1572864 | bytes 1572872 | tf_op jit(solution)/shard_map/transpose | solution.py:162
  2.8 1.7 %collective-permute-start.2 = (bf16[1,256,256]{2,1,0:T(8,128)(2,1)S(1)}, bf16[1,256,256]{2,1,0:T(8,128)(2,1)S(1)}, u32[]{:S(2)}, u32[]{:S(2)}) collective-permute-start(bf16[1,256,256]{2,1,0:T(8,128)(2,1)S(1)} %get-tuple-element.21), channel_id=1, source_target_pairs={{0,2},{2,0},{1,3},{3,1},{4,6},{6,4},{5,7},{7,5},{8,10},{10,8},{9,1... | collective-permute-start | bytes 393224 | tf_op jit(solution)/shard_map/ppermute | solution.py:164
  4.5 0.7 slice.30
  5.2 0.4 collective-permute-start.8
  5.7 0.1 pad_add_fusion.where_ref
  5.8 1.7 %collective-permute-start = (f32[256,128]{1,0:T(8,128)S(1)}, f32[256,128]{1,0:T(8,128)S(1)}, u32[]{:S(2)}, u32[]{:S(2)}) collective-permute-start(f32[256,128]{1,0:T(8,128)S(1)} %slice_select_fusion), channel_id=1, source_target_pairs={{0,2},{2,0},{1,3},{3,1},{4,6},{6,4},{5,7},{7,5},{8,10},{10,8},{9,1... | collective-permute-start | bytes 393224 | tf_op jit(solution)/shard_map/ppermute | solution.py:166
  7.5 0.4 collective-permute-start.5
  7.9 0.0 collective-permute-start.1
  7.9 0.6 collective-permute-done.2.rest_1_
  8.4 0.0 collective-permute-start.3
  8.4 9.0 %collective-permute-done.mate_rhs_ref = f32[256,128]{1,0:T(8,128)S(1)} collective-permute-done((f32[256,128]{1,0:T(8,128)S(1)}, f32[256,128]{1,0:T(8,128)S(1)}, u32[]{:S(2)}, u32[]{:S(2)}) %collective-permute-start) | collective-permute-done | bytes 131104 | tf_op jit(solution)/shard_map/ppermute | solution.py:166
  17.4 0.0 collective-permute-start.7
  17.4 1.8 %collective-permute-done.5.rest_4_ = bf16[1,256,256]{2,1,0:T(8,128)(2,1)S(1)} collective-permute-done((bf16[1,256,256]{2,1,0:T(8,128)(2,1)S(1)}, bf16[1,256,256]{2,1,0:T(8,128)(2,1)S(1)}, u32[]{:S(2)}, u32[]{:S(2)}) %collective-permute-start.5) | collective-permute-done | bytes 131104 | tf_op jit(solution)/shard_map/ppermute | solution.py:168
  19.3 0.0 collective-permute-start.4
  19.3 1.6 %copy-done.1 = f32[4,2,256,256]{3,2,1,0:T(8,128)S(1)} copy-done((f32[4,2,256,256]{3,2,1,0:T(8,128)S(1)}, f32[4,2,256,256]{3,2,1,0:T(8,128)}, u32[]{:S(2)}) %copy-start.1) | copy-done | bytes 2097176
  20.9 0.6 shard_map.77.inv_ref
  21.5 0.0 collective-permute-done.1.rest_0_.other3_ref
  21.5 0.6 collective-permute-start.6
  22.1 0.0 collective-permute-done.3.rest_2_
  22.1 0.6 shard_map.78.rest_7_
  22.7 0.7 collective-permute-start.11
  23.4 0.0 collective-permute-done.8.rest_7_
  23.4 0.1 collective-permute-start.9
  23.5 0.1 copy.14
  23.6 0.6 collective-permute-start.15
  24.1 0.7 collective-permute-start.10
  24.8 0.0 collective-permute-done.11.rest_6_
  24.8 0.6 shard_map.79.rest_13_
  25.4 1.3 %collective-permute-start.13 = (bf16[2,256,128]{2,1,0:T(8,128)(2,1)S(1)}, bf16[2,256,128]{2,1,0:T(8,128)(2,1)S(1)}, u32[]{:S(2)}, u32[]{:S(2)}) collective-permute-start(bf16[2,256,128]{2,1,0:T(8,128)(2,1)S(1)} %shard_map.79.rest_13_), channel_id=1, source_target_pairs={{8,0},{10,2},{9,1},{11,3},{24,16},{26,18},{25,17},{27,19},{40,32},... | collective-permute-start | bytes 393224 | tf_op jit(solution)/shard_map/ppermute | solution.py:141
  26.7 0.0 collective-permute-done.7.rest_6_.other01_ref
  26.7 1.3 %collective-permute-start.12 = (bf16[2,256,128]{2,1,0:T(8,128)(2,1)S(1)}, bf16[2,256,128]{2,1,0:T(8,128)(2,1)S(1)}, u32[]{:S(2)}, u32[]{:S(2)}) collective-permute-start(bf16[2,256,128]{2,1,0:T(8,128)(2,1)S(1)} %shard_map.79.rest_13_), channel_id=1, source_target_pairs={{8,6},{10,4},{14,0},{12,2},{9,7},{11,5},{15,1},{13,3},{24,22},{26,... | collective-permute-start | bytes 393224 | tf_op jit(solution)/shard_map/ppermute | solution.py:141
  28.0 12.2 %collective-permute-done.13.rest_12_ = bf16[2,256,128]{2,1,0:T(8,128)(2,1)S(1)} collective-permute-done((bf16[2,256,128]{2,1,0:T(8,128)(2,1)S(1)}, bf16[2,256,128]{2,1,0:T(8,128)(2,1)S(1)}, u32[]{:S(2)}, u32[]{:S(2)}) %collective-permute-start.13) | collective-permute-done | bytes 131104 | tf_op jit(solution)/shard_map/ppermute | solution.py:141
  40.2 0.0 collective-permute-done.12.rest_10_.rest_11_
  40.2 1.0 %shard_map.80 = (bf16[2,256,128]{2,1,0:T(8,128)(2,1)S(1)}, f32[2,256,128]{2,1,0:T(8,128)S(1)}) custom-call(s32[4]{0:T(128)S(1)} %pad_add_fusion.where_ref, bf16[2,2,256,256]{3,2,1,0:T(8,128)(2,1)S(1)} %shard_map.77.inv_ref, f32[256,256]{1,0:T(8,128)S(1)} %bitcast.27, f32[256,128]{1,0:T(8,128)S(1)} %collective-permute-done.mate_rhs_ref, ...), custom_call_target="tpu_custom_call" | custom-call | tf_op jit(solution)/shard_map/pallas_call | solution.py:126
  41.2 1.3 %collective-permute-start.14 = (bf16[2,256,128]{2,1,0:T(8,128)(2,1)S(1)}, bf16[2,256,128]{2,1,0:T(8,128)(2,1)S(1)}, u32[]{:S(2)}, u32[]{:S(2)}) collective-permute-start(bf16[2,256,128]{2,1,0:T(8,128)(2,1)S(1)} %get-tuple-element.14.rest_11_), channel_id=1, source_target_pairs={{6,0},{4,2},{7,1},{5,3},{22,16},{20,18},{23,17},{21,19},{38,32},{3... | collective-permute-start | bytes 393224 | tf_op jit(solution)/shard_map/ppermute | solution.py:141
  42.5 7.2 %collective-permute-done.14.rest_9_ = bf16[2,256,128]{2,1,0:T(8,128)(2,1)S(1)} collective-permute-done((bf16[2,256,128]{2,1,0:T(8,128)(2,1)S(1)}, bf16[2,256,128]{2,1,0:T(8,128)(2,1)S(1)}, u32[]{:S(2)}, u32[]{:S(2)}) %collective-permute-start.14) | collective-permute-done | bytes 131104 | tf_op jit(solution)/shard_map/ppermute | solution.py:141
  49.7 1.6 %shard_map.81 = bf16[2,256,128]{2,1,0:T(8,128)(2,1)S(1)} custom-call(s32[4]{0:T(128)S(1)} %pad_add_fusion.where_ref, bf16[2,2,256,256]{3,2,1,0:T(8,128)(2,1)S(1)} %shard_map.77.inv_ref, f32[256,256]{1,0:T(8,128)S(1)} %bitcast.28, f32[256,128]{1,0:T(8,128)S(1)} %collective-permute-done.mate_rhs_ref, bf16[4,256,256]{2,1,0:T(8,128)(2,1)S(1)} %fusion.1.own_ref.w_own_ref, ...), custom_call_target="tpu_custom_call" | custom-call | tf_op jit(solution)/shard_map/pallas_call | solution.py:126
  51.4 0.7 broadcast_in_dim.33
  52.1 7.6 %all-to-all-start = ((bf16[8,128,128]{2,1,0:T(8,128)(2,1)}), bf16[8,128,128]{2,1,0:T(8,128)(2,1)}, u32[]{:S(2)}, u32[]{:S(2)}) async-start(bf16[8,128,128]{2,1,0:T(8,128)(2,1)} %bitcast.8), calls=%async_computation | async-start | bytes 524288 | tf_op jit(solution)/shard_map/all_to_all | solution.py:210
  59.8 0.8 copy-done.4
  60.6 1.0 %copy-done.3 = bf16[1,1,256,4,1,256]{5,2,3,4,1,0:T(8,128)(2,1)S(1)} copy-done((bf16[1,1,256,4,1,256]{5,2,3,4,1,0:T(8,128)(2,1)S(1)}, bf16[1,1,256,4,1,256]{5,2,3,4,1,0:T(8,128)(2,1)}, u32[]{:S(2)}) %copy-start.3) | copy-done | bytes 524312
  61.6 1.0 %copy-done.5 = bf16[4,256,256]{2,1,0:T(8,128)(2,1)S(1)} copy-done((bf16[4,256,256]{2,1,0:T(8,128)(2,1)S(1)}, bf16[4,256,256]{2,1,0:T(8,128)(2,1)}, u32[]{:S(2)}) %copy-start.5) | copy-done | bytes 524312
  62.6 0.3 shard_map.82.rows_ref
  62.9 5.7 %all-to-all-done = bf16[8,128,128]{2,1,0:T(8,128)(2,1)} async-done(((bf16[8,128,128]{2,1,0:T(8,128)(2,1)}), bf16[8,128,128]{2,1,0:T(8,128)(2,1)}, u32[]{:S(2)}, u32[]{:S(2)}) %all-to-all-start) | async-done | bytes 262176 | tf_op jit(solution)/shard_map/all_to_all | solution.py:210
  68.6 0.8 slice_bitcast_fusion
  69.4 0.2 broadcast_in_dim.34
  69.6 18.0 %all_to_all.10.x_ref = bf16[32,128,128]{2,1,0:T(8,128)(2,1)S(1)} all-to-all(bf16[32,128,128]{2,1,0:T(8,128)(2,1)S(1)} %broadcast_in_dim.34), channel_id=1, replica_groups=mesh['z'=4,'yh'=2,'yl'=2,'xp'=2,'xq'=2,'col'=2] {'z','yl','xp','xq'}, dimensions={0} | all-to-all | bytes 2097152 | tf_op jit(solution)/shard_map/all_to_all | solution.py:215
  87.6 2.1 %shard_map.83 = (f32[256,256]{1,0:T(8,128)}, f32[256,256]{1,0:T(8,128)}) custom-call(s32[4]{0:T(128)S(1)} %pad_add_fusion.where_ref, bf16[32,128,128]{2,1,0:T(8,128)(2,1)S(1)} %all_to_all.10.x_ref, bf16[2,256,2048]{2,1,0:T(8,128)(2,1)S(1)} %shard_map.82.rows_ref, f32[256,256]{1,0:T(8,128)S(1)} %bitcast.29), custom_call_target="tpu_custom_call" | custom-call | tf_op jit(solution)/shard_map/pallas_call | solution.py:126
  (19 shorter events, 0.1 us)
Async XLA Ops:
  0.6 5.1 %copy-start = (f32[1,1,256,256]{3,2,1,0:T(8,128)S(1)}, f32[1,1,256,256]{3,2,1,0:T(8,128)}, u32[]{:S(2)}) copy-start(f32[1,1,256,256]{3,2,1,0:T(8,128)} %param.11) | copy-start | bytes 786436
  2.8 5.6 %collective-permute-start.2 = (bf16[1,256,256]{2,1,0:T(8,128)(2,1)S(1)}, bf16[1,256,256]{2,1,0:T(8,128)(2,1)S(1)}, u32[]{:S(2)}, u32[]{:S(2)}) collective-permute-start(bf16[1,256,256]{2,1,0:T(8,128)(2,1)S(1)} %get-tuple-element.21), channel_id=1, source_target_pairs={{0,2},{2,0},{1,3},{3,1},{4,6},{6,4},{5,7},{7,5},{8,10},{10,8},{9,1... | collective-permute-start | bytes 393224 | tf_op jit(solution)/shard_map/ppermute | solution.py:164
  5.2 18.1 %collective-permute-start.8 = (bf16[2,256,256]{2,1,0:T(8,128)(2,1)}, bf16[2,256,256]{2,1,0:T(8,128)(2,1)S(1)}, u32[]{:S(2)}, u32[]{:S(2)}) collective-permute-start(bf16[2,256,256]{2,1,0:T(8,128)(2,1)} %slice.30), channel_id=1, source_target_pairs={{0,2},{2,0},{1,3},{3,1},{4,6},{6,4},{5,7},{7,5},{8,10},{10,8},{9,1... | collective-permute-start | bytes 786440 | tf_op jit(solution)/shard_map/ppermute | solution.py:173
  5.8 11.7 %collective-permute-start = (f32[256,128]{1,0:T(8,128)S(1)}, f32[256,128]{1,0:T(8,128)S(1)}, u32[]{:S(2)}, u32[]{:S(2)}) collective-permute-start(f32[256,128]{1,0:T(8,128)S(1)} %slice_select_fusion), channel_id=1, source_target_pairs={{0,2},{2,0},{1,3},{3,1},{4,6},{6,4},{5,7},{7,5},{8,10},{10,8},{9,1... | collective-permute-start | bytes 393224 | tf_op jit(solution)/shard_map/ppermute | solution.py:166
  7.5 11.8 %collective-permute-start.5 = (bf16[1,256,256]{2,1,0:T(8,128)(2,1)S(1)}, bf16[1,256,256]{2,1,0:T(8,128)(2,1)S(1)}, u32[]{:S(2)}, u32[]{:S(2)}) collective-permute-start(bf16[1,256,256]{2,1,0:T(8,128)(2,1)S(1)} %get-tuple-element.20), channel_id=1, source_target_pairs={{0,2},{2,0},{1,3},{3,1},{4,6},{6,4},{5,7},{7,5},{8,10},{10,8},{9,1... | collective-permute-start | bytes 393224 | tf_op jit(solution)/shard_map/ppermute | solution.py:168
  7.9 13.6 %collective-permute-start.1 = (bf16[1,256,256]{2,1,0:T(8,128)(2,1)S(1)}, bf16[1,256,256]{2,1,0:T(8,128)(2,1)S(1)}, u32[]{:S(2)}, u32[]{:S(2)}) collective-permute-start(bf16[1,256,256]{2,1,0:T(8,128)(2,1)S(1)} %get-tuple-element.21), channel_id=1, source_target_pairs={{0,1},{1,0},{2,3},{3,2},{4,5},{5,4},{6,7},{7,6},{8,9},{9,8},{10,11... | collective-permute-start | bytes 393224 | tf_op jit(solution)/shard_map/ppermute | solution.py:165
  8.4 13.6 %collective-permute-start.3 = (bf16[1,256,256]{2,1,0:T(8,128)(2,1)S(1)}, bf16[1,256,256]{2,1,0:T(8,128)(2,1)S(1)}, u32[]{:S(2)}, u32[]{:S(2)}) collective-permute-start(bf16[1,256,256]{2,1,0:T(8,128)(2,1)S(1)} %collective-permute-done.2.rest_1_), channel_id=1, source_target_pairs={{0,1},{1,0},{2,3},{3,2},{4,5},{5,4},{6,7},{7,6},{8,9},{9,8},{10,11... | collective-permute-start | bytes 393224 | tf_op jit(solution)/shard_map/ppermute | solution.py:167
  17.4 9.2 %collective-permute-start.7 = (bf16[2,256,256]{2,1,0:T(8,128)(2,1)}, bf16[2,256,256]{2,1,0:T(8,128)(2,1)S(1)}, u32[]{:S(2)}, u32[]{:S(2)}) collective-permute-start(bf16[2,256,256]{2,1,0:T(8,128)(2,1)} %slice.30), channel_id=1, source_target_pairs={{0,1},{1,0},{2,3},{3,2},{4,5},{5,4},{6,7},{7,6},{8,9},{9,8},{10,11... | collective-permute-start | bytes 786440 | tf_op jit(solution)/shard_map/ppermute | solution.py:174
  19.3 4.3 %collective-permute-start.4 = (bf16[1,256,256]{2,1,0:T(8,128)(2,1)S(1)}, bf16[1,256,256]{2,1,0:T(8,128)(2,1)S(1)}, u32[]{:S(2)}, u32[]{:S(2)}) collective-permute-start(bf16[1,256,256]{2,1,0:T(8,128)(2,1)S(1)} %get-tuple-element.20), channel_id=1, source_target_pairs={{0,1},{1,0},{2,3},{3,2},{4,5},{5,4},{6,7},{7,6},{8,9},{9,8},{10,11... | collective-permute-start | bytes 393224 | tf_op jit(solution)/shard_map/ppermute | solution.py:169
  19.3 1.6 %copy-start.1 = (f32[4,2,256,256]{3,2,1,0:T(8,128)S(1)}, f32[4,2,256,256]{3,2,1,0:T(8,128)}, u32[]{:S(2)}) copy-start(f32[4,2,256,256]{3,2,1,0:T(8,128)} %inv_ref.1) | copy-start | bytes 6291460
  20.9 2.6 %copy-start.6 = (bf16[1,1,256,4,1,256]{5,3,4,2,1,0:T(4,128)(2,1)S(1)}, bf16[1,1,256,4,1,256]{5,3,4,2,1,0:T(4,128)(2,1)}, u32[]{:S(2)}) copy-start(bf16[1,1,256,4,1,256]{5,3,4,2,1,0:T(4,128)(2,1)} %param.8) | copy-start | bytes 1572868
  21.5 2.6 %collective-permute-start.6 = (bf16[1,256,256]{2,1,0:T(8,128)(2,1)S(1)}, bf16[1,256,256]{2,1,0:T(8,128)(2,1)S(1)}, u32[]{:S(2)}, u32[]{:S(2)}) collective-permute-start(bf16[1,256,256]{2,1,0:T(8,128)(2,1)S(1)} %collective-permute-done.5.rest_4_), channel_id=1, source_target_pairs={{0,1},{1,0},{2,3},{3,2},{4,5},{5,4},{6,7},{7,6},{8,9},{9,8},{10,11... | collective-permute-start | bytes 393224 | tf_op jit(solution)/shard_map/ppermute | solution.py:175
  22.7 2.1 %collective-permute-start.11 = (bf16[2,256,128]{2,1,0:T(8,128)(2,1)S(1)}, bf16[2,256,128]{2,1,0:T(8,128)(2,1)S(1)}, u32[]{:S(2)}, u32[]{:S(2)}) collective-permute-start(bf16[2,256,128]{2,1,0:T(8,128)(2,1)S(1)} %shard_map.78.rest_7_), channel_id=1, source_target_pairs={{14,8},{12,10},{15,9},{13,11},{30,24},{28,26},{31,25},{29,27},{46,... | collective-permute-start | bytes 393224 | tf_op jit(solution)/shard_map/ppermute | solution.py:141
  23.4 4.6 %collective-permute-start.9 = (bf16[2,256,256]{2,1,0:T(8,128)(2,1)S(1)}, bf16[2,256,256]{2,1,0:T(8,128)(2,1)S(1)}, u32[]{:S(2)}, u32[]{:S(2)}) collective-permute-start(bf16[2,256,256]{2,1,0:T(8,128)(2,1)S(1)} %collective-permute-done.8.rest_7_), channel_id=1, source_target_pairs={{0,1},{1,0},{2,3},{3,2},{4,5},{5,4},{6,7},{7,6},{8,9},{9,8},{10,11... | collective-permute-start | bytes 786440 | tf_op jit(solution)/shard_map/ppermute | solution.py:176
  23.6 17.7 %copy-start.2 = (bf16[1,1,256,4,1,256]{5,2,3,4,1,0:T(8,128)(2,1)}, bf16[1,1,256,4,1,256]{5,2,3,4,1,0:T(8,128)(2,1)S(1)}, u32[]{:S(2)}) copy-start(bf16[1,1,256,4,1,256]{5,2,3,4,1,0:T(8,128)(2,1)S(1)} %copy.14) | copy-start | bytes 1572868
  23.6 36.2 %collective-permute-start.15 = (bf16[4,256,256]{2,1,0:T(8,128)(2,1)S(1)}, bf16[4,256,256]{2,1,0:T(8,128)(2,1)S(1)}, u32[]{:S(2)}, u32[]{:S(2)}) collective-permute-start(bf16[4,256,256]{2,1,0:T(8,128)(2,1)S(1)} %bitcast.30), channel_id=1, source_target_pairs={{0,1},{1,0},{2,3},{3,2},{4,5},{5,4},{6,7},{7,6},{8,9},{9,8},{10,11... | collective-permute-start | bytes 1572872 | tf_op jit(solution)/shard_map/ppermute | solution.py:177
  24.1 3.9 %collective-permute-start.10 = (bf16[2,256,128]{2,1,0:T(8,128)(2,1)S(1)}, bf16[2,256,128]{2,1,0:T(8,128)(2,1)S(1)}, u32[]{:S(2)}, u32[]{:S(2)}) collective-permute-start(bf16[2,256,128]{2,1,0:T(8,128)(2,1)S(1)} %shard_map.78.rest_7_), channel_id=1, source_target_pairs={{14,6},{12,4},{15,7},{13,5},{30,22},{28,20},{31,23},{29,21},{46,38... | collective-permute-start | bytes 393224 | tf_op jit(solution)/shard_map/ppermute | solution.py:141
  25.4 14.8 %collective-permute-start.13 = (bf16[2,256,128]{2,1,0:T(8,128)(2,1)S(1)}, bf16[2,256,128]{2,1,0:T(8,128)(2,1)S(1)}, u32[]{:S(2)}, u32[]{:S(2)}) collective-permute-start(bf16[2,256,128]{2,1,0:T(8,128)(2,1)S(1)} %shard_map.79.rest_13_), channel_id=1, source_target_pairs={{8,0},{10,2},{9,1},{11,3},{24,16},{26,18},{25,17},{27,19},{40,32},... | collective-permute-start | bytes 393224 | tf_op jit(solution)/shard_map/ppermute | solution.py:141
  26.7 13.5 %collective-permute-start.12 = (bf16[2,256,128]{2,1,0:T(8,128)(2,1)S(1)}, bf16[2,256,128]{2,1,0:T(8,128)(2,1)S(1)}, u32[]{:S(2)}, u32[]{:S(2)}) collective-permute-start(bf16[2,256,128]{2,1,0:T(8,128)(2,1)S(1)} %shard_map.79.rest_13_), channel_id=1, source_target_pairs={{8,6},{10,4},{14,0},{12,2},{9,7},{11,5},{15,1},{13,3},{24,22},{26,... | collective-permute-start | bytes 393224 | tf_op jit(solution)/shard_map/ppermute | solution.py:141
  41.2 8.5 %collective-permute-start.14 = (bf16[2,256,128]{2,1,0:T(8,128)(2,1)S(1)}, bf16[2,256,128]{2,1,0:T(8,128)(2,1)S(1)}, u32[]{:S(2)}, u32[]{:S(2)}) collective-permute-start(bf16[2,256,128]{2,1,0:T(8,128)(2,1)S(1)} %get-tuple-element.14.rest_11_), channel_id=1, source_target_pairs={{6,0},{4,2},{7,1},{5,3},{22,16},{20,18},{23,17},{21,19},{38,32},{3... | collective-permute-start | bytes 393224 | tf_op jit(solution)/shard_map/ppermute | solution.py:141
  52.1 16.5 %all-to-all-start = ((bf16[8,128,128]{2,1,0:T(8,128)(2,1)}), bf16[8,128,128]{2,1,0:T(8,128)(2,1)}, u32[]{:S(2)}, u32[]{:S(2)}) async-start(bf16[8,128,128]{2,1,0:T(8,128)(2,1)} %bitcast.8), calls=%async_computation | async-start | bytes 524288 | tf_op jit(solution)/shard_map/all_to_all | solution.py:210
  59.7 0.8 copy-start.4
  60.6 1.0 %copy-start.3 = (bf16[1,1,256,4,1,256]{5,2,3,4,1,0:T(8,128)(2,1)S(1)}, bf16[1,1,256,4,1,256]{5,2,3,4,1,0:T(8,128)(2,1)}, u32[]{:S(2)}) copy-start(bf16[1,1,256,4,1,256]{5,2,3,4,1,0:T(8,128)(2,1)} %copy-done.2) | copy-start | bytes 1572868
  61.6 1.0 %copy-start.5 = (bf16[4,256,256]{2,1,0:T(8,128)(2,1)S(1)}, bf16[4,256,256]{2,1,0:T(8,128)(2,1)}, u32[]{:S(2)}) copy-start(bf16[4,256,256]{2,1,0:T(8,128)(2,1)} %copy-done.4) | copy-start | bytes 1572868

commit v6 on v5

--- a/solution.py
+++ b/solution.py
@@ -105,7 +105,9 @@
                 out_ref[n, :, at : at + NB] = blocks[n][side]
 
 
-def final_kernel(where_ref, x_ref, rows_ref, rhs_ref, pending_ref, image_ref, order_ref):
+def final_kernel(
+    where_ref, x_ref, rows_ref, rhs_ref, pending_out, image_out, order_ref, pending_ref, image_ref, sems
+):
     parity = where_ref[3]
     for b in range(HALF):
         yl, xp = b // 2, b % 2
@@ -117,17 +119,24 @@
                     order_ref[to : to + WIDE, half * WIDE : (half + 1) * WIDE] = x_ref[at]
     x = order_ref[...]
     pending_ref[...] = rhs_ref[...] - dot(rows_ref[0], x)
+    first = pltpu.make_async_copy(pending_ref, pending_out, sems.at[0])
+    first.start()
     image_ref[...] = dot(rows_ref[1], x)
-
-
-def call(kernel, outs, scratch, *args, limit=12 << 20):
+    second = pltpu.make_async_copy(image_ref, image_out, sems.at[1])
+    second.start()
+    first.wait()
+    second.wait()
+
+
+def call(kernel, outs, scratch, *args, limit=12 << 20, out_space=pltpu.VMEM):
     vmem = pl.BlockSpec(memory_space=pltpu.VMEM)
     smem = pl.BlockSpec(memory_space=pltpu.SMEM)
+    result = pl.BlockSpec(memory_space=out_space)
     return pl.pallas_call(
         kernel,
         out_shape=outs,
         in_specs=[smem if a.dtype == jnp.int32 else vmem for a in args],
-        out_specs=jax.tree.map(lambda _: vmem, outs),
+        out_specs=jax.tree.map(lambda _: result, outs),
         scratch_shapes=scratch,
         compiler_params=pltpu.CompilerParams(vmem_limit_bytes=limit),
     )(*args)
@@ -164,12 +173,13 @@
     mate3 = lax.ppermute(own3, "xq", FLIP)
     other3 = lax.ppermute(own3, "col", FLIP)
     mate_rhs = lax.ppermute(jnp.where(lower_half, rhs[:, WIDE:], rhs[:, :WIDE]), "xq", FLIP)
-    mate3_other = lax.ppermute(mate3, "col", FLIP)
     mate2 = lax.ppermute(own[2:3], "xq", FLIP)
     other2 = lax.ppermute(own[2:3], "col", FLIP)
     inverses = call(
         split_kernel, jax.ShapeDtypeStruct((2, 2, NB, NB), jnp.bfloat16), [], where, block_inverses
     )
+    inverses, mate3 = lax.optimization_barrier((inverses, mate3))
+    mate3_other = lax.ppermute(mate3, "col", FLIP)
     mate01 = lax.ppermute(own[:2], "xq", FLIP)
     other01 = lax.ppermute(own[:2], "col", FLIP)
     mate2_other = lax.ppermute(mate2, "col", FLIP)
@@ -218,8 +228,12 @@
 
     out = jax.ShapeDtypeStruct((NB, NB), jnp.float32)
     pending, image = call(
-        final_kernel, (out, out), [pltpu.VMEM((STEPS * NB, NB), jnp.bfloat16)],
-        where, every, rows, rhs,
+        final_kernel, (out, out),
+        [
+            pltpu.VMEM((STEPS * NB, NB), jnp.bfloat16), pltpu.VMEM((NB, NB), jnp.float32),
+            pltpu.VMEM((NB, NB), jnp.float32), pltpu.SemaphoreType.DMA((2,)),
+        ],
+        where, every, rows, rhs, out_space=pl.ANY,
     )
     return pending.reshape(1, 1, NB, NB), image.reshape(1, 1, NB, NB)
 

time: 90.3 us -> 88 us (0.975)
  waiting for transfers between devices: 36.5 us -> 33.7 us
    ppermute x1, waiting for transfers between devices: 9 us -> 6.74 us  [local(): lax.ppermute(jnp.where(lower_half, rhs[:, WIDE:], rhs[:, :WIDE]), 'xq', F...]
  transfers between devices with their start and end apart: 17 -> 17, of which waited for: 6 -> 5; matrix products, arithmetic and copies ran while one was open for 2% -> 2% of each run, Pallas kernels for 5% -> 5%
where the time goes in v6:
time: 88 us; the launch traced here: 87.4 us
  waiting for transfers between devices  33.7 us (38%)
  starting transfers between devices  18.8 us (21%)
  blocking collectives  18 us (20%)
  local copies, waits for them, and re-layouts  7.04 us (8%)
  Pallas kernels  6.7 us (8%)
  between operations  1.58 us (2%)
  other arithmetic  1.56 us (2%)
    ppermute x5, waiting for transfers between devices, to_pairs(): return lax.ppermute(a, ('yl', 'xp', 'xq'), sends)  19.4 us
    all_to_all x1, blocking collectives, local(): lax.all_to_all(jnp.broadcast_to(spread[None], (count, *spread.shape)), PL...  18 us
    all_to_all x1, starting transfers between devices, local(): lax.all_to_all(quarters.reshape(2 * DEPTH, *quarters.shape[2:]), ('z', 'y...  7.65 us
    ppermute x1, waiting for transfers between devices, local(): lax.ppermute(jnp.where(lower_half, rhs[:, WIDE:], rhs[:, :WIDE]), 'xq', F...  6.74 us
    pallas_call x7, Pallas kernels, call(): pl.pallas_call(kernel, out_shape=outs, in_specs=[smem if a.dtype == jnp.i...  6.7 us
    all_to_all x1, waiting for transfers between devices, local(): lax.all_to_all(quarters.reshape(2 * DEPTH, *quarters.shape[2:]), ('z', 'y...  5.71 us
    ppermute x5, starting transfers between devices, to_pairs(): return lax.ppermute(a, ('yl', 'xp', 'xq'), sends)  5.2 us
    unnamed x15, local copies, waits for them, and re-layouts  4.56 us
  transfers between devices with their start and end apart: 17, of which 5 were waited for; matrix products, arithmetic and copies ran while one was open for 2% of the time, Pallas kernels for 5%

profile of v6, /device:TPU:0, one launch (start us, length us, event | category | flops | bytes accessed | tf_op | source)
XLA Modules:
  0.0 87.4 jit_solution(17245439668319867873)
XLA Ops:
  1.4 1.5 %fusion.1.own_ref.w_own_ref = bf16[4,256,256]{2,1,0:T(8,128)(2,1)S(1)} fusion(bf16[1,1,256,4,1,256]{5,3,4,2,1,0:T(4,128)(2,1)} %param.7, bf16[1,1,256,4,1,256]{5,3,4,2,1,0:T(4,128)(2,1)} %param.6, f32[]{:T(128)S(6)} %copy.15, pred[4]{0:T(512)(128)(4,1)S(1)} %add_compare_fusion), kind=kLoop, calls=%fused_computation.2 | loop fusion | flops 1572864 | bytes 1572872 | tf_op jit(solution)/shard_map/transpose | solution.py:171
  2.8 1.7 %collective-permute-start = (bf16[1,256,256]{2,1,0:T(8,128)(2,1)S(1)}, bf16[1,256,256]{2,1,0:T(8,128)(2,1)S(1)}, u32[]{:S(2)}, u32[]{:S(2)}) collective-permute-start(bf16[1,256,256]{2,1,0:T(8,128)(2,1)S(1)} %get-tuple-element.25), channel_id=1, source_target_pairs={{0,2},{2,0},{1,3},{3,1},{4,6},{6,4},{5,7},{7,5},{8,10},{10,8},{9,1... | collective-permute-start | bytes 393224 | tf_op jit(solution)/shard_map/ppermute | solution.py:173
  4.5 0.7 slice.30
  5.2 0.4 collective-permute-start.8
  5.7 0.1 pad_add_fusion.where_ref
  5.8 1.7 %collective-permute-start.1 = (f32[256,128]{1,0:T(8,128)S(1)}, f32[256,128]{1,0:T(8,128)S(1)}, u32[]{:S(2)}, u32[]{:S(2)}) collective-permute-start(f32[256,128]{1,0:T(8,128)S(1)} %slice_select_fusion), channel_id=1, source_target_pairs={{0,2},{2,0},{1,3},{3,1},{4,6},{6,4},{5,7},{7,5},{8,10},{10,8},{9,1... | collective-permute-start | bytes 393224 | tf_op jit(solution)/shard_map/ppermute | solution.py:175
  7.5 0.4 collective-permute-start.5
  7.9 0.0 collective-permute-start.2
  7.9 1.6 %copy-done.1 = f32[4,2,256,256]{3,2,1,0:T(8,128)S(1)} copy-done((f32[4,2,256,256]{3,2,1,0:T(8,128)S(1)}, f32[4,2,256,256]{3,2,1,0:T(8,128)}, u32[]{:S(2)}) %copy-start.1) | copy-done | bytes 2097176
  9.5 0.6 shard_map.77.inv_ref
  10.1 0.0 collective-permute-done.rest_1_
  10.1 0.6 collective-permute-start.3
  10.7 6.7 %collective-permute-done.1.mate_rhs_ref = f32[256,128]{1,0:T(8,128)S(1)} collective-permute-done((f32[256,128]{1,0:T(8,128)S(1)}, f32[256,128]{1,0:T(8,128)S(1)}, u32[]{:S(2)}, u32[]{:S(2)}) %collective-permute-start.1) | collective-permute-done | bytes 131104 | tf_op jit(solution)/shard_map/ppermute | solution.py:175
  17.4 1.8 %collective-permute-done.5.rest_4_ = bf16[1,256,256]{2,1,0:T(8,128)(2,1)S(1)} collective-permute-done((bf16[1,256,256]{2,1,0:T(8,128)(2,1)S(1)}, bf16[1,256,256]{2,1,0:T(8,128)(2,1)S(1)}, u32[]{:S(2)}, u32[]{:S(2)}) %collective-permute-start.5) | collective-permute-done | bytes 131104 | tf_op jit(solution)/shard_map/ppermute | solution.py:176
  19.3 0.0 collective-permute-start.4
  19.3 0.0 collective-permute-done.2.rest_0_.other3_ref
  19.3 0.5 collective-permute-start.6
  19.8 0.0 collective-permute-done.3.rest_2_
  19.8 0.6 shard_map.78.rest_7_
  20.4 0.7 collective-permute-start.11
  21.1 0.1 collective-permute-start.9
  21.2 0.1 copy.14
  21.3 0.6 collective-permute-start.15
  21.8 0.0 collective-permute-done.6.rest_5_
  21.8 0.7 collective-permute-start.10
  22.5 0.0 collective-permute-done.11.rest_6_
  22.5 0.6 shard_map.79.rest_13_
  23.1 1.3 %collective-permute-start.13 = (bf16[2,256,128]{2,1,0:T(8,128)(2,1)S(1)}, bf16[2,256,128]{2,1,0:T(8,128)(2,1)S(1)}, u32[]{:S(2)}, u32[]{:S(2)}) collective-permute-start(bf16[2,256,128]{2,1,0:T(8,128)(2,1)S(1)} %shard_map.79.rest_13_), channel_id=1, source_target_pairs={{8,0},{10,2},{9,1},{11,3},{24,16},{26,18},{25,17},{27,19},{40,32},... | collective-permute-start | bytes 393224 | tf_op jit(solution)/shard_map/ppermute | solution.py:150
  24.4 0.0 collective-permute-done.7.rest_6_.other01_ref
  24.4 1.3 %collective-permute-start.12 = (bf16[2,256,128]{2,1,0:T(8,128)(2,1)S(1)}, bf16[2,256,128]{2,1,0:T(8,128)(2,1)S(1)}, u32[]{:S(2)}, u32[]{:S(2)}) collective-permute-start(bf16[2,256,128]{2,1,0:T(8,128)(2,1)S(1)} %shard_map.79.rest_13_), channel_id=1, source_target_pairs={{8,6},{10,4},{14,0},{12,2},{9,7},{11,5},{15,1},{13,3},{24,22},{26,... | collective-permute-start | bytes 393224 | tf_op jit(solution)/shard_map/ppermute | solution.py:150
  25.7 0.0 collective-permute-done.9.rest_8_
  25.7 12.2 %collective-permute-done.13.rest_12_ = bf16[2,256,128]{2,1,0:T(8,128)(2,1)S(1)} collective-permute-done((bf16[2,256,128]{2,1,0:T(8,128)(2,1)S(1)}, bf16[2,256,128]{2,1,0:T(8,128)(2,1)S(1)}, u32[]{:S(2)}, u32[]{:S(2)}) %collective-permute-start.13) | collective-permute-done | bytes 131104 | tf_op jit(solution)/shard_map/ppermute | solution.py:150
  37.9 0.0 collective-permute-done.12.rest_10_.rest_11_
  37.9 1.0 %shard_map.80 = (bf16[2,256,128]{2,1,0:T(8,128)(2,1)S(1)}, f32[2,256,128]{2,1,0:T(8,128)S(1)}) custom-call(s32[4]{0:T(128)S(1)} %pad_add_fusion.where_ref, bf16[2,2,256,256]{3,2,1,0:T(8,128)(2,1)S(1)} %shard_map.77.inv_ref, f32[256,256]{1,0:T(8,128)S(1)} %bitcast.27, f32[256,128]{1,0:T(8,128)S(1)} %collective-permute-done.1.mate_rhs_ref, ...), custom_call_target="tpu_custom_call" | custom-call | tf_op jit(solution)/shard_map/pallas_call | solution.py:135
  38.9 1.3 %collective-permute-start.14 = (bf16[2,256,128]{2,1,0:T(8,128)(2,1)S(1)}, bf16[2,256,128]{2,1,0:T(8,128)(2,1)S(1)}, u32[]{:S(2)}, u32[]{:S(2)}) collective-permute-start(bf16[2,256,128]{2,1,0:T(8,128)(2,1)S(1)} %get-tuple-element.18.rest_11_), channel_id=1, source_target_pairs={{6,0},{4,2},{7,1},{5,3},{22,16},{20,18},{23,17},{21,19},{38,32},{3... | collective-permute-start | bytes 393224 | tf_op jit(solution)/shard_map/ppermute | solution.py:150
  40.2 7.2 %collective-permute-done.14.rest_9_ = bf16[2,256,128]{2,1,0:T(8,128)(2,1)S(1)} collective-permute-done((bf16[2,256,128]{2,1,0:T(8,128)(2,1)S(1)}, bf16[2,256,128]{2,1,0:T(8,128)(2,1)S(1)}, u32[]{:S(2)}, u32[]{:S(2)}) %collective-permute-start.14) | collective-permute-done | bytes 131104 | tf_op jit(solution)/shard_map/ppermute | solution.py:150
  47.4 1.6 %shard_map.81 = bf16[2,256,128]{2,1,0:T(8,128)(2,1)S(1)} custom-call(s32[4]{0:T(128)S(1)} %pad_add_fusion.where_ref, bf16[2,2,256,256]{3,2,1,0:T(8,128)(2,1)S(1)} %shard_map.77.inv_ref, f32[256,256]{1,0:T(8,128)S(1)} %bitcast.28, f32[256,128]{1,0:T(8,128)S(1)} %collective-permute-done.1.mate_rhs_ref, bf16[4,256,256]{2,1,0:T(8,128)(2,1)S(1)} %fusion.1.own_ref.w_own_ref, ...), custom_call_target="tpu_custom_call" | custom-call | tf_op jit(solution)/shard_map/pallas_call | solution.py:135
  49.0 0.7 broadcast_in_dim.33
  49.8 7.7 %all-to-all-start = ((bf16[8,128,128]{2,1,0:T(8,128)(2,1)}), bf16[8,128,128]{2,1,0:T(8,128)(2,1)}, u32[]{:S(2)}, u32[]{:S(2)}) async-start(bf16[8,128,128]{2,1,0:T(8,128)(2,1)} %bitcast.8), calls=%async_computation | async-start | bytes 524288 | tf_op jit(solution)/shard_map/all_to_all | solution.py:220
  57.4 0.8 copy-done.4
  58.2 1.0 %copy-done.3 = bf16[1,1,256,4,1,256]{5,2,3,4,1,0:T(8,128)(2,1)S(1)} copy-done((bf16[1,1,256,4,1,256]{5,2,3,4,1,0:T(8,128)(2,1)S(1)}, bf16[1,1,256,4,1,256]{5,2,3,4,1,0:T(8,128)(2,1)}, u32[]{:S(2)}) %copy-start.3) | copy-done | bytes 524312
  59.3 1.0 %copy-done.5 = bf16[4,256,256]{2,1,0:T(8,128)(2,1)S(1)} copy-done((bf16[4,256,256]{2,1,0:T(8,128)(2,1)S(1)}, bf16[4,256,256]{2,1,0:T(8,128)(2,1)}, u32[]{:S(2)}) %copy-start.5) | copy-done | bytes 524312
  60.3 0.3 shard_map.82.rows_ref
  60.6 5.7 %all-to-all-done = bf16[8,128,128]{2,1,0:T(8,128)(2,1)} async-done(((bf16[8,128,128]{2,1,0:T(8,128)(2,1)}), bf16[8,128,128]{2,1,0:T(8,128)(2,1)}, u32[]{:S(2)}, u32[]{:S(2)}) %all-to-all-start) | async-done | bytes 262176 | tf_op jit(solution)/shard_map/all_to_all | solution.py:220
  66.3 0.8 slice_bitcast_fusion
  67.1 0.2 broadcast_in_dim.34
  67.3 18.0 %all_to_all.10.x_ref = bf16[32,128,128]{2,1,0:T(8,128)(2,1)S(1)} all-to-all(bf16[32,128,128]{2,1,0:T(8,128)(2,1)S(1)} %broadcast_in_dim.34), channel_id=1, replica_groups=mesh['z'=4,'yh'=2,'yl'=2,'xp'=2,'xq'=2,'col'=2] {'z','yl','xp','xq'}, dimensions={0} | all-to-all | bytes 2097152 | tf_op jit(solution)/shard_map/all_to_all | solution.py:225
  85.3 2.1 %shard_map.83 = (f32[256,256]{1,0:T(8,128)}, f32[256,256]{1,0:T(8,128)}) custom-call(s32[4]{0:T(128)S(1)} %pad_add_fusion.where_ref, bf16[32,128,128]{2,1,0:T(8,128)(2,1)S(1)} %all_to_all.10.x_ref, bf16[2,256,2048]{2,1,0:T(8,128)(2,1)S(1)} %shard_map.82.rows_ref, f32[256,256]{1,0:T(8,128)S(1)} %bitcast.29), custom_call_target="tpu_custom_call" | custom-call | tf_op jit(solution)/shard_map/pallas_call | solution.py:135
  (19 shorter events, 0.1 us)
Async XLA Ops:
  0.6 5.1 %copy-start = (f32[1,1,256,256]{3,2,1,0:T(8,128)S(1)}, f32[1,1,256,256]{3,2,1,0:T(8,128)}, u32[]{:S(2)}) copy-start(f32[1,1,256,256]{3,2,1,0:T(8,128)} %param.11) | copy-start | bytes 786436
  2.8 7.3 %collective-permute-start = (bf16[1,256,256]{2,1,0:T(8,128)(2,1)S(1)}, bf16[1,256,256]{2,1,0:T(8,128)(2,1)S(1)}, u32[]{:S(2)}, u32[]{:S(2)}) collective-permute-start(bf16[1,256,256]{2,1,0:T(8,128)(2,1)S(1)} %get-tuple-element.25), channel_id=1, source_target_pairs={{0,2},{2,0},{1,3},{3,1},{4,6},{6,4},{5,7},{7,5},{8,10},{10,8},{9,1... | collective-permute-start | bytes 393224 | tf_op jit(solution)/shard_map/ppermute | solution.py:173
  5.2 15.8 %collective-permute-start.8 = (bf16[2,256,256]{2,1,0:T(8,128)(2,1)}, bf16[2,256,256]{2,1,0:T(8,128)(2,1)S(1)}, u32[]{:S(2)}, u32[]{:S(2)}) collective-permute-start(bf16[2,256,256]{2,1,0:T(8,128)(2,1)} %slice.30), channel_id=1, source_target_pairs={{0,2},{2,0},{1,3},{3,1},{4,6},{6,4},{5,7},{7,5},{8,10},{10,8},{9,1... | collective-permute-start | bytes 786440 | tf_op jit(solution)/shard_map/ppermute | solution.py:183
  5.8 11.7 %collective-permute-start.1 = (f32[256,128]{1,0:T(8,128)S(1)}, f32[256,128]{1,0:T(8,128)S(1)}, u32[]{:S(2)}, u32[]{:S(2)}) collective-permute-start(f32[256,128]{1,0:T(8,128)S(1)} %slice_select_fusion), channel_id=1, source_target_pairs={{0,2},{2,0},{1,3},{3,1},{4,6},{6,4},{5,7},{7,5},{8,10},{10,8},{9,1... | collective-permute-start | bytes 393224 | tf_op jit(solution)/shard_map/ppermute | solution.py:175
  7.5 11.8 %collective-permute-start.5 = (bf16[1,256,256]{2,1,0:T(8,128)(2,1)S(1)}, bf16[1,256,256]{2,1,0:T(8,128)(2,1)S(1)}, u32[]{:S(2)}, u32[]{:S(2)}) collective-permute-start(bf16[1,256,256]{2,1,0:T(8,128)(2,1)S(1)} %get-tuple-element.24), channel_id=1, source_target_pairs={{0,2},{2,0},{1,3},{3,1},{4,6},{6,4},{5,7},{7,5},{8,10},{10,8},{9,1... | collective-permute-start | bytes 393224 | tf_op jit(solution)/shard_map/ppermute | solution.py:176
  7.9 11.4 %collective-permute-start.2 = (bf16[1,256,256]{2,1,0:T(8,128)(2,1)S(1)}, bf16[1,256,256]{2,1,0:T(8,128)(2,1)S(1)}, u32[]{:S(2)}, u32[]{:S(2)}) collective-permute-start(bf16[1,256,256]{2,1,0:T(8,128)(2,1)S(1)} %get-tuple-element.25), channel_id=1, source_target_pairs={{0,1},{1,0},{2,3},{3,2},{4,5},{5,4},{6,7},{7,6},{8,9},{9,8},{10,11... | collective-permute-start | bytes 393224 | tf_op jit(solution)/shard_map/ppermute | solution.py:174
  7.9 1.6 %copy-start.1 = (f32[4,2,256,256]{3,2,1,0:T(8,128)S(1)}, f32[4,2,256,256]{3,2,1,0:T(8,128)}, u32[]{:S(2)}) copy-start(f32[4,2,256,256]{3,2,1,0:T(8,128)} %inv_ref.1) | copy-start | bytes 6291460
  9.5 11.7 %copy-start.6 = (bf16[1,1,256,4,1,256]{5,3,4,2,1,0:T(4,128)(2,1)S(1)}, bf16[1,1,256,4,1,256]{5,3,4,2,1,0:T(4,128)(2,1)}, u32[]{:S(2)}) copy-start(bf16[1,1,256,4,1,256]{5,3,4,2,1,0:T(4,128)(2,1)} %param.8) | copy-start | bytes 1572868
  10.1 9.7 %collective-permute-start.3 = (bf16[1,256,256]{2,1,0:T(8,128)(2,1)S(1)}, bf16[1,256,256]{2,1,0:T(8,128)(2,1)S(1)}, u32[]{:S(2)}, u32[]{:S(2)}) collective-permute-start(bf16[1,256,256]{2,1,0:T(8,128)(2,1)S(1)} %collective-permute-done.rest_1_), channel_id=1, source_target_pairs={{0,1},{1,0},{2,3},{3,2},{4,5},{5,4},{6,7},{7,6},{8,9},{9,8},{10,11... | collective-permute-start | bytes 393224 | tf_op jit(solution)/shard_map/ppermute | solution.py:182
  17.4 6.9 %collective-permute-start.7 = (bf16[2,256,256]{2,1,0:T(8,128)(2,1)}, bf16[2,256,256]{2,1,0:T(8,128)(2,1)S(1)}, u32[]{:S(2)}, u32[]{:S(2)}) collective-permute-start(bf16[2,256,256]{2,1,0:T(8,128)(2,1)} %slice.30), channel_id=1, source_target_pairs={{0,1},{1,0},{2,3},{3,2},{4,5},{5,4},{6,7},{7,6},{8,9},{9,8},{10,11... | collective-permute-start | bytes 786440 | tf_op jit(solution)/shard_map/ppermute | solution.py:184
  19.3 2.0 %collective-permute-start.4 = (bf16[1,256,256]{2,1,0:T(8,128)(2,1)S(1)}, bf16[1,256,256]{2,1,0:T(8,128)(2,1)S(1)}, u32[]{:S(2)}, u32[]{:S(2)}) collective-permute-start(bf16[1,256,256]{2,1,0:T(8,128)(2,1)S(1)} %get-tuple-element.24), channel_id=1, source_target_pairs={{0,1},{1,0},{2,3},{3,2},{4,5},{5,4},{6,7},{7,6},{8,9},{9,8},{10,11... | collective-permute-start | bytes 393224 | tf_op jit(solution)/shard_map/ppermute | solution.py:177
  19.3 2.6 %collective-permute-start.6 = (bf16[1,256,256]{2,1,0:T(8,128)(2,1)S(1)}, bf16[1,256,256]{2,1,0:T(8,128)(2,1)S(1)}, u32[]{:S(2)}, u32[]{:S(2)}) collective-permute-start(bf16[1,256,256]{2,1,0:T(8,128)(2,1)S(1)} %collective-permute-done.5.rest_4_), channel_id=1, source_target_pairs={{0,1},{1,0},{2,3},{3,2},{4,5},{5,4},{6,7},{7,6},{8,9},{9,8},{10,11... | collective-permute-start | bytes 393224 | tf_op jit(solution)/shard_map/ppermute | solution.py:185
  20.4 2.1 %collective-permute-start.11 = (bf16[2,256,128]{2,1,0:T(8,128)(2,1)S(1)}, bf16[2,256,128]{2,1,0:T(8,128)(2,1)S(1)}, u32[]{:S(2)}, u32[]{:S(2)}) collective-permute-start(bf16[2,256,128]{2,1,0:T(8,128)(2,1)S(1)} %shard_map.78.rest_7_), channel_id=1, source_target_pairs={{14,8},{12,10},{15,9},{13,11},{30,24},{28,26},{31,25},{29,27},{46,... | collective-permute-start | bytes 393224 | tf_op jit(solution)/shard_map/ppermute | solution.py:150
  21.1 4.6 %collective-permute-start.9 = (bf16[2,256,256]{2,1,0:T(8,128)(2,1)S(1)}, bf16[2,256,256]{2,1,0:T(8,128)(2,1)S(1)}, u32[]{:S(2)}, u32[]{:S(2)}) collective-permute-start(bf16[2,256,256]{2,1,0:T(8,128)(2,1)S(1)} %collective-permute-done.8.rest_7_), channel_id=1, source_target_pairs={{0,1},{1,0},{2,3},{3,2},{4,5},{5,4},{6,7},{7,6},{8,9},{9,8},{10,11... | collective-permute-start | bytes 786440 | tf_op jit(solution)/shard_map/ppermute | solution.py:186
  21.2 17.7 %copy-start.2 = (bf16[1,1,256,4,1,256]{5,2,3,4,1,0:T(8,128)(2,1)}, bf16[1,1,256,4,1,256]{5,2,3,4,1,0:T(8,128)(2,1)S(1)}, u32[]{:S(2)}) copy-start(bf16[1,1,256,4,1,256]{5,2,3,4,1,0:T(8,128)(2,1)S(1)} %copy.14) | copy-start | bytes 1572868
  21.3 36.2 %collective-permute-start.15 = (bf16[4,256,256]{2,1,0:T(8,128)(2,1)S(1)}, bf16[4,256,256]{2,1,0:T(8,128)(2,1)S(1)}, u32[]{:S(2)}, u32[]{:S(2)}) collective-permute-start(bf16[4,256,256]{2,1,0:T(8,128)(2,1)S(1)} %bitcast.30), channel_id=1, source_target_pairs={{0,1},{1,0},{2,3},{3,2},{4,5},{5,4},{6,7},{7,6},{8,9},{9,8},{10,11... | collective-permute-start | bytes 1572872 | tf_op jit(solution)/shard_map/ppermute | solution.py:187
  21.8 3.9 %collective-permute-start.10 = (bf16[2,256,128]{2,1,0:T(8,128)(2,1)S(1)}, bf16[2,256,128]{2,1,0:T(8,128)(2,1)S(1)}, u32[]{:S(2)}, u32[]{:S(2)}) collective-permute-start(bf16[2,256,128]{2,1,0:T(8,128)(2,1)S(1)} %shard_map.78.rest_7_), channel_id=1, source_target_pairs={{14,6},{12,4},{15,7},{13,5},{30,22},{28,20},{31,23},{29,21},{46,38... | collective-permute-start | bytes 393224 | tf_op jit(solution)/shard_map/ppermute | solution.py:150
  23.1 14.8 %collective-permute-start.13 = (bf16[2,256,128]{2,1,0:T(8,128)(2,1)S(1)}, bf16[2,256,128]{2,1,0:T(8,128)(2,1)S(1)}, u32[]{:S(2)}, u32[]{:S(2)}) collective-permute-start(bf16[2,256,128]{2,1,0:T(8,128)(2,1)S(1)} %shard_map.79.rest_13_), channel_id=1, source_target_pairs={{8,0},{10,2},{9,1},{11,3},{24,16},{26,18},{25,17},{27,19},{40,32},... | collective-permute-start | bytes 393224 | tf_op jit(solution)/shard_map/ppermute | solution.py:150
  24.4 13.5 %collective-permute-start.12 = (bf16[2,256,128]{2,1,0:T(8,128)(2,1)S(1)}, bf16[2,256,128]{2,1,0:T(8,128)(2,1)S(1)}, u32[]{:S(2)}, u32[]{:S(2)}) collective-permute-start(bf16[2,256,128]{2,1,0:T(8,128)(2,1)S(1)} %shard_map.79.rest_13_), channel_id=1, source_target_pairs={{8,6},{10,4},{14,0},{12,2},{9,7},{11,5},{15,1},{13,3},{24,22},{26,... | collective-permute-start | bytes 393224 | tf_op jit(solution)/shard_map/ppermute | solution.py:150
  38.9 8.5 %collective-permute-start.14 = (bf16[2,256,128]{2,1,0:T(8,128)(2,1)S(1)}, bf16[2,256,128]{2,1,0:T(8,128)(2,1)S(1)}, u32[]{:S(2)}, u32[]{:S(2)}) collective-permute-start(bf16[2,256,128]{2,1,0:T(8,128)(2,1)S(1)} %get-tuple-element.18.rest_11_), channel_id=1, source_target_pairs={{6,0},{4,2},{7,1},{5,3},{22,16},{20,18},{23,17},{21,19},{38,32},{3... | collective-permute-start | bytes 393224 | tf_op jit(solution)/shard_map/ppermute | solution.py:150
  49.8 16.5 %all-to-all-start = ((bf16[8,128,128]{2,1,0:T(8,128)(2,1)}), bf16[8,128,128]{2,1,0:T(8,128)(2,1)}, u32[]{:S(2)}, u32[]{:S(2)}) async-start(bf16[8,128,128]{2,1,0:T(8,128)(2,1)} %bitcast.8), calls=%async_computation | async-start | bytes 524288 | tf_op jit(solution)/shard_map/all_to_all | solution.py:220
  57.4 0.8 copy-start.4
  58.2 1.0 %copy-start.3 = (bf16[1,1,256,4,1,256]{5,2,3,4,1,0:T(8,128)(2,1)S(1)}, bf16[1,1,256,4,1,256]{5,2,3,4,1,0:T(8,128)(2,1)}, u32[]{:S(2)}) copy-start(bf16[1,1,256,4,1,256]{5,2,3,4,1,0:T(8,128)(2,1)} %copy-done.2) | copy-start | bytes 1572868
  59.3 1.0 %copy-start.5 = (bf16[4,256,256]{2,1,0:T(8,128)(2,1)S(1)}, bf16[4,256,256]{2,1,0:T(8,128)(2,1)}, u32[]{:S(2)}) copy-start(bf16[4,256,256]{2,1,0:T(8,128)(2,1)} %copy-done.4) | copy-start | bytes 1572868

commit v7 on v5

--- a/solution.py
+++ b/solution.py
@@ -102,7 +102,7 @@
         for n in range(2):
             for side in range(2):
                 at = (side * HALF + b) * NB
-                out_ref[n, :, at : at + NB] = blocks[n][side]
+                out_ref[n * NB : (n + 1) * NB, at : at + NB] = blocks[n][side]
 
 
 def final_kernel(where_ref, x_ref, rows_ref, rhs_ref, pending_ref, image_ref, order_ref):
@@ -116,8 +116,9 @@
                     to = (side * HALF + b) * NB + i * WIDE
                     order_ref[to : to + WIDE, half * WIDE : (half + 1) * WIDE] = x_ref[at]
     x = order_ref[...]
-    pending_ref[...] = rhs_ref[...] - dot(rows_ref[0], x)
-    image_ref[...] = dot(rows_ref[1], x)
+    both = dot(rows_ref[...], x)
+    pending_ref[...] = rhs_ref[...] - both[:NB]
+    image_ref[...] = both[NB:]
 
 
 def call(kernel, outs, scratch, *args, limit=12 << 20):
@@ -200,7 +201,7 @@
     x1, acc = solve(1, [(3, b), (2, c)], [(3, c), (2, d)], x2)
     e = to_pairs(x1, [(1, 0)])
     rows = call(
-        pack_kernel, jax.ShapeDtypeStruct((2, NB, STEPS * NB), jnp.bfloat16), [],
+        pack_kernel, jax.ShapeDtypeStruct((2 * NB, STEPS * NB), jnp.bfloat16), [],
         own, other3, other2, other01, own_z, other_z,
     )
     x0 = solve(0, [(1, e)], [], acc, x1)

time: 90.3 us -> 90.3 us (level)
  no operation moved by 1% of the time
where the time goes in v7:
time: 90.3 us; the launch traced here: 89.7 us
  waiting for transfers between devices  36.5 us (40%)
  starting transfers between devices  18.3 us (20%)
  blocking collectives  18 us (20%)
  local copies, waits for them, and re-layouts  7.04 us (8%)
  Pallas kernels  6.69 us (7%)
  other arithmetic  1.56 us (2%)
  between operations  1.56 us (2%)
    ppermute x5, waiting for transfers between devices, to_pairs(): return lax.ppermute(a, ('yl', 'xp', 'xq'), sends)  19.4 us
    all_to_all x1, blocking collectives, local(): lax.all_to_all(jnp.broadcast_to(spread[None], (count, *spread.shape)), PL...  18 us
    ppermute x1, waiting for transfers between devices, local(): lax.ppermute(jnp.where(lower_half, rhs[:, WIDE:], rhs[:, :WIDE]), 'xq', F...  9 us
    all_to_all x1, starting transfers between devices, local(): lax.all_to_all(quarters.reshape(2 * DEPTH, *quarters.shape[2:]), ('z', 'y...  7.65 us
    pallas_call x7, Pallas kernels, call(): pl.pallas_call(kernel, out_shape=outs, in_specs=[smem if a.dtype == jnp.i...  6.69 us
    all_to_all x1, waiting for transfers between devices, local(): lax.all_to_all(quarters.reshape(2 * DEPTH, *quarters.shape[2:]), ('z', 'y...  5.71 us
    ppermute x5, starting transfers between devices, to_pairs(): return lax.ppermute(a, ('yl', 'xp', 'xq'), sends)  5.2 us
    unnamed x15, local copies, waits for them, and re-layouts  4.56 us
  transfers between devices with their start and end apart: 17, of which 6 were waited for; matrix products, arithmetic and copies ran while one was open for 2% of the time, Pallas kernels for 5%

profile of v7, /device:TPU:0, one launch (start us, length us, event | category | flops | bytes accessed | tf_op | source)
XLA Modules:
  0.0 89.7 jit_solution(14686833016530720955)
XLA Ops:
  1.4 1.5 %fusion.1.own_ref.w_own_ref = bf16[4,256,256]{2,1,0:T(8,128)(2,1)S(1)} fusion(bf16[1,1,256,4,1,256]{5,3,4,2,1,0:T(4,128)(2,1)} %param.7, bf16[1,1,256,4,1,256]{5,3,4,2,1,0:T(4,128)(2,1)} %param.6, f32[]{:T(128)S(6)} %copy.15, pred[4]{0:T(512)(128)(4,1)S(1)} %add_compare_fusion), kind=kLoop, calls=%fused_computation.2 | loop fusion | flops 1572864 | bytes 1572872 | tf_op jit(solution)/shard_map/transpose | solution.py:163
  2.8 1.7 %collective-permute-start.2 = (bf16[1,256,256]{2,1,0:T(8,128)(2,1)S(1)}, bf16[1,256,256]{2,1,0:T(8,128)(2,1)S(1)}, u32[]{:S(2)}, u32[]{:S(2)}) collective-permute-start(bf16[1,256,256]{2,1,0:T(8,128)(2,1)S(1)} %get-tuple-element.21), channel_id=1, source_target_pairs={{0,2},{2,0},{1,3},{3,1},{4,6},{6,4},{5,7},{7,5},{8,10},{10,8},{9,1... | collective-permute-start | bytes 393224 | tf_op jit(solution)/shard_map/ppermute | solution.py:165
  4.5 0.7 slice.30
  5.2 0.4 collective-permute-start.8
  5.7 0.1 pad_add_fusion.where_ref
  5.8 1.7 %collective-permute-start = (f32[256,128]{1,0:T(8,128)S(1)}, f32[256,128]{1,0:T(8,128)S(1)}, u32[]{:S(2)}, u32[]{:S(2)}) collective-permute-start(f32[256,128]{1,0:T(8,128)S(1)} %slice_select_fusion), channel_id=1, source_target_pairs={{0,2},{2,0},{1,3},{3,1},{4,6},{6,4},{5,7},{7,5},{8,10},{10,8},{9,1... | collective-permute-start | bytes 393224 | tf_op jit(solution)/shard_map/ppermute | solution.py:167
  7.5 0.4 collective-permute-start.5
  7.9 0.0 collective-permute-start.1
  7.9 0.6 collective-permute-done.2.rest_1_
  8.4 0.0 collective-permute-start.3
  8.4 9.0 %collective-permute-done.mate_rhs_ref = f32[256,128]{1,0:T(8,128)S(1)} collective-permute-done((f32[256,128]{1,0:T(8,128)S(1)}, f32[256,128]{1,0:T(8,128)S(1)}, u32[]{:S(2)}, u32[]{:S(2)}) %collective-permute-start) | collective-permute-done | bytes 131104 | tf_op jit(solution)/shard_map/ppermute | solution.py:167
  17.4 0.0 collective-permute-start.7
  17.4 1.8 %collective-permute-done.5.rest_4_ = bf16[1,256,256]{2,1,0:T(8,128)(2,1)S(1)} collective-permute-done((bf16[1,256,256]{2,1,0:T(8,128)(2,1)S(1)}, bf16[1,256,256]{2,1,0:T(8,128)(2,1)S(1)}, u32[]{:S(2)}, u32[]{:S(2)}) %collective-permute-start.5) | collective-permute-done | bytes 131104 | tf_op jit(solution)/shard_map/ppermute | solution.py:169
  19.3 0.0 collective-permute-start.4
  19.3 1.6 %copy-done.1 = f32[4,2,256,256]{3,2,1,0:T(8,128)S(1)} copy-done((f32[4,2,256,256]{3,2,1,0:T(8,128)S(1)}, f32[4,2,256,256]{3,2,1,0:T(8,128)}, u32[]{:S(2)}) %copy-start.1) | copy-done | bytes 2097176
  20.9 0.6 shard_map.77.inv_ref
  21.5 0.0 collective-permute-done.1.rest_0_.other3_ref
  21.5 0.6 collective-permute-start.6
  22.1 0.0 collective-permute-done.3.rest_2_
  22.1 0.6 shard_map.78.rest_7_
  22.7 0.7 collective-permute-start.11
  23.4 0.0 collective-permute-done.8.rest_7_
  23.4 0.1 collective-permute-start.9
  23.5 0.1 copy.14
  23.6 0.6 collective-permute-start.15
  24.1 0.7 collective-permute-start.10
  24.8 0.0 collective-permute-done.11.rest_6_
  24.8 0.6 shard_map.79.rest_13_
  25.4 1.3 %collective-permute-start.13 = (bf16[2,256,128]{2,1,0:T(8,128)(2,1)S(1)}, bf16[2,256,128]{2,1,0:T(8,128)(2,1)S(1)}, u32[]{:S(2)}, u32[]{:S(2)}) collective-permute-start(bf16[2,256,128]{2,1,0:T(8,128)(2,1)S(1)} %shard_map.79.rest_13_), channel_id=1, source_target_pairs={{8,0},{10,2},{9,1},{11,3},{24,16},{26,18},{25,17},{27,19},{40,32},... | collective-permute-start | bytes 393224 | tf_op jit(solution)/shard_map/ppermute | solution.py:142
  26.7 0.0 collective-permute-done.7.rest_6_.other01_ref
  26.7 1.3 %collective-permute-start.12 = (bf16[2,256,128]{2,1,0:T(8,128)(2,1)S(1)}, bf16[2,256,128]{2,1,0:T(8,128)(2,1)S(1)}, u32[]{:S(2)}, u32[]{:S(2)}) collective-permute-start(bf16[2,256,128]{2,1,0:T(8,128)(2,1)S(1)} %shard_map.79.rest_13_), channel_id=1, source_target_pairs={{8,6},{10,4},{14,0},{12,2},{9,7},{11,5},{15,1},{13,3},{24,22},{26,... | collective-permute-start | bytes 393224 | tf_op jit(solution)/shard_map/ppermute | solution.py:142
  28.0 12.2 %collective-permute-done.13.rest_12_ = bf16[2,256,128]{2,1,0:T(8,128)(2,1)S(1)} collective-permute-done((bf16[2,256,128]{2,1,0:T(8,128)(2,1)S(1)}, bf16[2,256,128]{2,1,0:T(8,128)(2,1)S(1)}, u32[]{:S(2)}, u32[]{:S(2)}) %collective-permute-start.13) | collective-permute-done | bytes 131104 | tf_op jit(solution)/shard_map/ppermute | solution.py:142
  40.2 0.0 collective-permute-done.12.rest_10_.rest_11_
  40.2 1.0 %shard_map.80 = (bf16[2,256,128]{2,1,0:T(8,128)(2,1)S(1)}, f32[2,256,128]{2,1,0:T(8,128)S(1)}) custom-call(s32[4]{0:T(128)S(1)} %pad_add_fusion.where_ref, bf16[2,2,256,256]{3,2,1,0:T(8,128)(2,1)S(1)} %shard_map.77.inv_ref, f32[256,256]{1,0:T(8,128)S(1)} %bitcast.27, f32[256,128]{1,0:T(8,128)S(1)} %collective-permute-done.mate_rhs_ref, ...), custom_call_target="tpu_custom_call" | custom-call | tf_op jit(solution)/shard_map/pallas_call | solution.py:127
  41.2 1.3 %collective-permute-start.14 = (bf16[2,256,128]{2,1,0:T(8,128)(2,1)S(1)}, bf16[2,256,128]{2,1,0:T(8,128)(2,1)S(1)}, u32[]{:S(2)}, u32[]{:S(2)}) collective-permute-start(bf16[2,256,128]{2,1,0:T(8,128)(2,1)S(1)} %get-tuple-element.14.rest_11_), channel_id=1, source_target_pairs={{6,0},{4,2},{7,1},{5,3},{22,16},{20,18},{23,17},{21,19},{38,32},{3... | collective-permute-start | bytes 393224 | tf_op jit(solution)/shard_map/ppermute | solution.py:142
  42.5 7.2 %collective-permute-done.14.rest_9_ = bf16[2,256,128]{2,1,0:T(8,128)(2,1)S(1)} collective-permute-done((bf16[2,256,128]{2,1,0:T(8,128)(2,1)S(1)}, bf16[2,256,128]{2,1,0:T(8,128)(2,1)S(1)}, u32[]{:S(2)}, u32[]{:S(2)}) %collective-permute-start.14) | collective-permute-done | bytes 131104 | tf_op jit(solution)/shard_map/ppermute | solution.py:142
  49.7 1.6 %shard_map.81 = bf16[2,256,128]{2,1,0:T(8,128)(2,1)S(1)} custom-call(s32[4]{0:T(128)S(1)} %pad_add_fusion.where_ref, bf16[2,2,256,256]{3,2,1,0:T(8,128)(2,1)S(1)} %shard_map.77.inv_ref, f32[256,256]{1,0:T(8,128)S(1)} %bitcast.28, f32[256,128]{1,0:T(8,128)S(1)} %collective-permute-done.mate_rhs_ref, bf16[4,256,256]{2,1,0:T(8,128)(2,1)S(1)} %fusion.1.own_ref.w_own_ref, ...), custom_call_target="tpu_custom_call" | custom-call | tf_op jit(solution)/shard_map/pallas_call | solution.py:127
  51.4 0.7 broadcast_in_dim.33
  52.1 7.6 %all-to-all-start = ((bf16[8,128,128]{2,1,0:T(8,128)(2,1)}), bf16[8,128,128]{2,1,0:T(8,128)(2,1)}, u32[]{:S(2)}, u32[]{:S(2)}) async-start(bf16[8,128,128]{2,1,0:T(8,128)(2,1)} %bitcast.8), calls=%async_computation | async-start | bytes 524288 | tf_op jit(solution)/shard_map/all_to_all | solution.py:211
  59.8 0.8 copy-done.4
  60.6 1.0 %copy-done.3 = bf16[1,1,256,4,1,256]{5,2,3,4,1,0:T(8,128)(2,1)S(1)} copy-done((bf16[1,1,256,4,1,256]{5,2,3,4,1,0:T(8,128)(2,1)S(1)}, bf16[1,1,256,4,1,256]{5,2,3,4,1,0:T(8,128)(2,1)}, u32[]{:S(2)}) %copy-start.3) | copy-done | bytes 524312
  61.6 1.0 %copy-done.5 = bf16[4,256,256]{2,1,0:T(8,128)(2,1)S(1)} copy-done((bf16[4,256,256]{2,1,0:T(8,128)(2,1)S(1)}, bf16[4,256,256]{2,1,0:T(8,128)(2,1)}, u32[]{:S(2)}) %copy-start.5) | copy-done | bytes 524312
  62.6 0.3 shard_map.82.rows_ref
  62.9 5.7 %all-to-all-done = bf16[8,128,128]{2,1,0:T(8,128)(2,1)} async-done(((bf16[8,128,128]{2,1,0:T(8,128)(2,1)}), bf16[8,128,128]{2,1,0:T(8,128)(2,1)}, u32[]{:S(2)}, u32[]{:S(2)}) %all-to-all-start) | async-done | bytes 262176 | tf_op jit(solution)/shard_map/all_to_all | solution.py:211
  68.6 0.8 slice_bitcast_fusion
  69.4 0.2 broadcast_in_dim.34
  69.6 18.0 %all_to_all.10.x_ref = bf16[32,128,128]{2,1,0:T(8,128)(2,1)S(1)} all-to-all(bf16[32,128,128]{2,1,0:T(8,128)(2,1)S(1)} %broadcast_in_dim.34), channel_id=1, replica_groups=mesh['z'=4,'yh'=2,'yl'=2,'xp'=2,'xq'=2,'col'=2] {'z','yl','xp','xq'}, dimensions={0} | all-to-all | bytes 2097152 | tf_op jit(solution)/shard_map/all_to_all | solution.py:216
  87.6 2.1 %shard_map.83 = (f32[256,256]{1,0:T(8,128)}, f32[256,256]{1,0:T(8,128)}) custom-call(s32[4]{0:T(128)S(1)} %pad_add_fusion.where_ref, bf16[32,128,128]{2,1,0:T(8,128)(2,1)S(1)} %all_to_all.10.x_ref, bf16[512,2048]{1,0:T(8,128)(2,1)S(1)} %shard_map.82.rows_ref, f32[256,256]{1,0:T(8,128)S(1)} %bitcast.29), custom_call_target="tpu_custom_call" | custom-call | tf_op jit(solution)/shard_map/pallas_call | solution.py:127
  (19 shorter events, 0.1 us)
Async XLA Ops:
  0.6 5.1 %copy-start = (f32[1,1,256,256]{3,2,1,0:T(8,128)S(1)}, f32[1,1,256,256]{3,2,1,0:T(8,128)}, u32[]{:S(2)}) copy-start(f32[1,1,256,256]{3,2,1,0:T(8,128)} %param.11) | copy-start | bytes 786436
  2.8 5.6 %collective-permute-start.2 = (bf16[1,256,256]{2,1,0:T(8,128)(2,1)S(1)}, bf16[1,256,256]{2,1,0:T(8,128)(2,1)S(1)}, u32[]{:S(2)}, u32[]{:S(2)}) collective-permute-start(bf16[1,256,256]{2,1,0:T(8,128)(2,1)S(1)} %get-tuple-element.21), channel_id=1, source_target_pairs={{0,2},{2,0},{1,3},{3,1},{4,6},{6,4},{5,7},{7,5},{8,10},{10,8},{9,1... | collective-permute-start | bytes 393224 | tf_op jit(solution)/shard_map/ppermute | solution.py:165
  5.2 18.1 %collective-permute-start.8 = (bf16[2,256,256]{2,1,0:T(8,128)(2,1)}, bf16[2,256,256]{2,1,0:T(8,128)(2,1)S(1)}, u32[]{:S(2)}, u32[]{:S(2)}) collective-permute-start(bf16[2,256,256]{2,1,0:T(8,128)(2,1)} %slice.30), channel_id=1, source_target_pairs={{0,2},{2,0},{1,3},{3,1},{4,6},{6,4},{5,7},{7,5},{8,10},{10,8},{9,1... | collective-permute-start | bytes 786440 | tf_op jit(solution)/shard_map/ppermute | solution.py:174
  5.8 11.7 %collective-permute-start = (f32[256,128]{1,0:T(8,128)S(1)}, f32[256,128]{1,0:T(8,128)S(1)}, u32[]{:S(2)}, u32[]{:S(2)}) collective-permute-start(f32[256,128]{1,0:T(8,128)S(1)} %slice_select_fusion), channel_id=1, source_target_pairs={{0,2},{2,0},{1,3},{3,1},{4,6},{6,4},{5,7},{7,5},{8,10},{10,8},{9,1... | collective-permute-start | bytes 393224 | tf_op jit(solution)/shard_map/ppermute | solution.py:167
  7.5 11.8 %collective-permute-start.5 = (bf16[1,256,256]{2,1,0:T(8,128)(2,1)S(1)}, bf16[1,256,256]{2,1,0:T(8,128)(2,1)S(1)}, u32[]{:S(2)}, u32[]{:S(2)}) collective-permute-start(bf16[1,256,256]{2,1,0:T(8,128)(2,1)S(1)} %get-tuple-element.20), channel_id=1, source_target_pairs={{0,2},{2,0},{1,3},{3,1},{4,6},{6,4},{5,7},{7,5},{8,10},{10,8},{9,1... | collective-permute-start | bytes 393224 | tf_op jit(solution)/shard_map/ppermute | solution.py:169
  7.9 13.6 %collective-permute-start.1 = (bf16[1,256,256]{2,1,0:T(8,128)(2,1)S(1)}, bf16[1,256,256]{2,1,0:T(8,128)(2,1)S(1)}, u32[]{:S(2)}, u32[]{:S(2)}) collective-permute-start(bf16[1,256,256]{2,1,0:T(8,128)(2,1)S(1)} %get-tuple-element.21), channel_id=1, source_target_pairs={{0,1},{1,0},{2,3},{3,2},{4,5},{5,4},{6,7},{7,6},{8,9},{9,8},{10,11... | collective-permute-start | bytes 393224 | tf_op jit(solution)/shard_map/ppermute | solution.py:166
  8.4 13.6 %collective-permute-start.3 = (bf16[1,256,256]{2,1,0:T(8,128)(2,1)S(1)}, bf16[1,256,256]{2,1,0:T(8,128)(2,1)S(1)}, u32[]{:S(2)}, u32[]{:S(2)}) collective-permute-start(bf16[1,256,256]{2,1,0:T(8,128)(2,1)S(1)} %collective-permute-done.2.rest_1_), channel_id=1, source_target_pairs={{0,1},{1,0},{2,3},{3,2},{4,5},{5,4},{6,7},{7,6},{8,9},{9,8},{10,11... | collective-permute-start | bytes 393224 | tf_op jit(solution)/shard_map/ppermute | solution.py:168
  17.4 9.2 %collective-permute-start.7 = (bf16[2,256,256]{2,1,0:T(8,128)(2,1)}, bf16[2,256,256]{2,1,0:T(8,128)(2,1)S(1)}, u32[]{:S(2)}, u32[]{:S(2)}) collective-permute-start(bf16[2,256,256]{2,1,0:T(8,128)(2,1)} %slice.30), channel_id=1, source_target_pairs={{0,1},{1,0},{2,3},{3,2},{4,5},{5,4},{6,7},{7,6},{8,9},{9,8},{10,11... | collective-permute-start | bytes 786440 | tf_op jit(solution)/shard_map/ppermute | solution.py:175
  19.3 4.3 %collective-permute-start.4 = (bf16[1,256,256]{2,1,0:T(8,128)(2,1)S(1)}, bf16[1,256,256]{2,1,0:T(8,128)(2,1)S(1)}, u32[]{:S(2)}, u32[]{:S(2)}) collective-permute-start(bf16[1,256,256]{2,1,0:T(8,128)(2,1)S(1)} %get-tuple-element.20), channel_id=1, source_target_pairs={{0,1},{1,0},{2,3},{3,2},{4,5},{5,4},{6,7},{7,6},{8,9},{9,8},{10,11... | collective-permute-start | bytes 393224 | tf_op jit(solution)/shard_map/ppermute | solution.py:170
  19.3 1.6 %copy-start.1 = (f32[4,2,256,256]{3,2,1,0:T(8,128)S(1)}, f32[4,2,256,256]{3,2,1,0:T(8,128)}, u32[]{:S(2)}) copy-start(f32[4,2,256,256]{3,2,1,0:T(8,128)} %inv_ref.1) | copy-start | bytes 6291460
  20.9 2.6 %copy-start.6 = (bf16[1,1,256,4,1,256]{5,3,4,2,1,0:T(4,128)(2,1)S(1)}, bf16[1,1,256,4,1,256]{5,3,4,2,1,0:T(4,128)(2,1)}, u32[]{:S(2)}) copy-start(bf16[1,1,256,4,1,256]{5,3,4,2,1,0:T(4,128)(2,1)} %param.8) | copy-start | bytes 1572868
  21.5 2.6 %collective-permute-start.6 = (bf16[1,256,256]{2,1,0:T(8,128)(2,1)S(1)}, bf16[1,256,256]{2,1,0:T(8,128)(2,1)S(1)}, u32[]{:S(2)}, u32[]{:S(2)}) collective-permute-start(bf16[1,256,256]{2,1,0:T(8,128)(2,1)S(1)} %collective-permute-done.5.rest_4_), channel_id=1, source_target_pairs={{0,1},{1,0},{2,3},{3,2},{4,5},{5,4},{6,7},{7,6},{8,9},{9,8},{10,11... | collective-permute-start | bytes 393224 | tf_op jit(solution)/shard_map/ppermute | solution.py:176
  22.7 2.1 %collective-permute-start.11 = (bf16[2,256,128]{2,1,0:T(8,128)(2,1)S(1)}, bf16[2,256,128]{2,1,0:T(8,128)(2,1)S(1)}, u32[]{:S(2)}, u32[]{:S(2)}) collective-permute-start(bf16[2,256,128]{2,1,0:T(8,128)(2,1)S(1)} %shard_map.78.rest_7_), channel_id=1, source_target_pairs={{14,8},{12,10},{15,9},{13,11},{30,24},{28,26},{31,25},{29,27},{46,... | collective-permute-start | bytes 393224 | tf_op jit(solution)/shard_map/ppermute | solution.py:142
  23.4 4.6 %collective-permute-start.9 = (bf16[2,256,256]{2,1,0:T(8,128)(2,1)S(1)}, bf16[2,256,256]{2,1,0:T(8,128)(2,1)S(1)}, u32[]{:S(2)}, u32[]{:S(2)}) collective-permute-start(bf16[2,256,256]{2,1,0:T(8,128)(2,1)S(1)} %collective-permute-done.8.rest_7_), channel_id=1, source_target_pairs={{0,1},{1,0},{2,3},{3,2},{4,5},{5,4},{6,7},{7,6},{8,9},{9,8},{10,11... | collective-permute-start | bytes 786440 | tf_op jit(solution)/shard_map/ppermute | solution.py:177
  23.6 17.7 %copy-start.2 = (bf16[1,1,256,4,1,256]{5,2,3,4,1,0:T(8,128)(2,1)}, bf16[1,1,256,4,1,256]{5,2,3,4,1,0:T(8,128)(2,1)S(1)}, u32[]{:S(2)}) copy-start(bf16[1,1,256,4,1,256]{5,2,3,4,1,0:T(8,128)(2,1)S(1)} %copy.14) | copy-start | bytes 1572868
  23.6 36.2 %collective-permute-start.15 = (bf16[4,256,256]{2,1,0:T(8,128)(2,1)S(1)}, bf16[4,256,256]{2,1,0:T(8,128)(2,1)S(1)}, u32[]{:S(2)}, u32[]{:S(2)}) collective-permute-start(bf16[4,256,256]{2,1,0:T(8,128)(2,1)S(1)} %bitcast.30), channel_id=1, source_target_pairs={{0,1},{1,0},{2,3},{3,2},{4,5},{5,4},{6,7},{7,6},{8,9},{9,8},{10,11... | collective-permute-start | bytes 1572872 | tf_op jit(solution)/shard_map/ppermute | solution.py:178
  24.1 3.9 %collective-permute-start.10 = (bf16[2,256,128]{2,1,0:T(8,128)(2,1)S(1)}, bf16[2,256,128]{2,1,0:T(8,128)(2,1)S(1)}, u32[]{:S(2)}, u32[]{:S(2)}) collective-permute-start(bf16[2,256,128]{2,1,0:T(8,128)(2,1)S(1)} %shard_map.78.rest_7_), channel_id=1, source_target_pairs={{14,6},{12,4},{15,7},{13,5},{30,22},{28,20},{31,23},{29,21},{46,38... | collective-permute-start | bytes 393224 | tf_op jit(solution)/shard_map/ppermute | solution.py:142
  25.4 14.8 %collective-permute-start.13 = (bf16[2,256,128]{2,1,0:T(8,128)(2,1)S(1)}, bf16[2,256,128]{2,1,0:T(8,128)(2,1)S(1)}, u32[]{:S(2)}, u32[]{:S(2)}) collective-permute-start(bf16[2,256,128]{2,1,0:T(8,128)(2,1)S(1)} %shard_map.79.rest_13_), channel_id=1, source_target_pairs={{8,0},{10,2},{9,1},{11,3},{24,16},{26,18},{25,17},{27,19},{40,32},... | collective-permute-start | bytes 393224 | tf_op jit(solution)/shard_map/ppermute | solution.py:142
  26.7 13.5 %collective-permute-start.12 = (bf16[2,256,128]{2,1,0:T(8,128)(2,1)S(1)}, bf16[2,256,128]{2,1,0:T(8,128)(2,1)S(1)}, u32[]{:S(2)}, u32[]{:S(2)}) collective-permute-start(bf16[2,256,128]{2,1,0:T(8,128)(2,1)S(1)} %shard_map.79.rest_13_), channel_id=1, source_target_pairs={{8,6},{10,4},{14,0},{12,2},{9,7},{11,5},{15,1},{13,3},{24,22},{26,... | collective-permute-start | bytes 393224 | tf_op jit(solution)/shard_map/ppermute | solution.py:142
  41.2 8.5 %collective-permute-start.14 = (bf16[2,256,128]{2,1,0:T(8,128)(2,1)S(1)}, bf16[2,256,128]{2,1,0:T(8,128)(2,1)S(1)}, u32[]{:S(2)}, u32[]{:S(2)}) collective-permute-start(bf16[2,256,128]{2,1,0:T(8,128)(2,1)S(1)} %get-tuple-element.14.rest_11_), channel_id=1, source_target_pairs={{6,0},{4,2},{7,1},{5,3},{22,16},{20,18},{23,17},{21,19},{38,32},{3... | collective-permute-start | bytes 393224 | tf_op jit(solution)/shard_map/ppermute | solution.py:142
  52.1 16.5 %all-to-all-start = ((bf16[8,128,128]{2,1,0:T(8,128)(2,1)}), bf16[8,128,128]{2,1,0:T(8,128)(2,1)}, u32[]{:S(2)}, u32[]{:S(2)}) async-start(bf16[8,128,128]{2,1,0:T(8,128)(2,1)} %bitcast.8), calls=%async_computation | async-start | bytes 524288 | tf_op jit(solution)/shard_map/all_to_all | solution.py:211
  59.7 0.8 copy-start.4
  60.6 1.0 %copy-start.3 = (bf16[1,1,256,4,1,256]{5,2,3,4,1,0:T(8,128)(2,1)S(1)}, bf16[1,1,256,4,1,256]{5,2,3,4,1,0:T(8,128)(2,1)}, u32[]{:S(2)}) copy-start(bf16[1,1,256,4,1,256]{5,2,3,4,1,0:T(8,128)(2,1)} %copy-done.2) | copy-start | bytes 1572868
  61.6 1.0 %copy-start.5 = (bf16[4,256,256]{2,1,0:T(8,128)(2,1)S(1)}, bf16[4,256,256]{2,1,0:T(8,128)(2,1)}, u32[]{:S(2)}) copy-start(bf16[4,256,256]{2,1,0:T(8,128)(2,1)} %copy-done.4) | copy-start | bytes 1572868

commit v8 on v3

--- a/solution.py
+++ b/solution.py
@@ -12,8 +12,9 @@
 HALF = STEPS // 2
 NB = 256
 WIDE = NB // 2
-GROUPS = 8
+DEPTH = 4
 ROWS = ("z", "yh", "yl", "xp", "xq")
+PLANE = ("z", "yl", "xp", "xq")
 FLIP = [(0, 1), (1, 0)]
 
 
@@ -105,7 +106,7 @@
         for w, z, p in ((own, z_own_ref, parity), (other, z_other_ref, 1 - parity)):
             columns = []
             for half in range(2):
-                at = [(((4 * p + i) * 2 + yl) * 2 + xp) * 2 + (half ^ xp) for i in range(4)]
+                at = [(((2 * p + i) * 2 + yl) * 2 + xp) * 2 + (half ^ xp) for i in range(2)]
                 columns.append(jnp.concatenate([x_ref[n] for n in at], 0))
             x = jnp.concatenate(columns, 1)
             pending = pending - dot(w, x)
@@ -186,22 +187,24 @@
         )
 
     x3 = solve(3, [], [], jnp.zeros(shape.shape, shape.dtype))
-    a = to_pairs(x3, [(3, 2)])
+    a = to_pairs(x3, [(3, 2), (1, 3)])
     b = to_pairs(x3, [(3, 1)])
     x2 = solve(2, [(3, a)], [], x3)
-    c = to_pairs(x2, [(2, 1), (3, 0)])
+    c = to_pairs(x2, [(2, 1), (3, 0), (0, 2), (1, 3)])
     d = to_pairs(x2, [(2, 0)])
     x1, acc = solve(1, [(3, b), (2, c)], [(3, c), (2, d)], x2)
-    e = to_pairs(x1, [(1, 0)])
+    e = to_pairs(x1, [(1, 0), (3, 1)])
     x0 = solve(0, [(1, e)], [], acc, x1)
 
+    quarters = x0.reshape(DEPTH, 1, 2 * NB // DEPTH, WIDE)
+    quarters = jnp.broadcast_to(quarters, (DEPTH, 2, *quarters.shape[2:]))
     spread = lax.all_to_all(
-        x0.reshape(GROUPS, 2 * NB // GROUPS, WIDE), ("z", "yh"), 0, 0, tiled=True
-    )[GROUPS - 1]
+        quarters.reshape(2 * DEPTH, *quarters.shape[2:]), ("z", "yh"), 0, 0, tiled=True
+    )[2 * DEPTH - 1]
     spread, other_z = lax.optimization_barrier((spread, other_z))
-    count = lax.axis_size(ROWS)
+    count = lax.axis_size(PLANE)
     every = lax.all_to_all(
-        jnp.broadcast_to(spread[None], (count, *spread.shape)), ROWS, 0, 0, tiled=True
+        jnp.broadcast_to(spread[None], (count, *spread.shape)), PLANE, 0, 0, tiled=True
     )
 
     out = jax.ShapeDtypeStruct((NB, NB), jnp.float32)

time: 89.2 us -> 88.3 us (0.990)
  starting transfers between devices: 10.6 us -> 19.4 us
  waiting for transfers between devices: 31.1 us -> 23.7 us
  blocking collectives: 36.5 us -> 34.2 us
    ppermute x5, starting transfers between devices: 5.2 us -> 14.5 us  [to_pairs(): return lax.ppermute(a, ('yl', 'xp', 'xq'), sends)]
    ppermute x5, waiting for transfers between devices: 19.5 us -> 12.1 us  [to_pairs(): return lax.ppermute(a, ('yl', 'xp', 'xq'), sends)]
    all_to_all x2, blocking collectives: 36.5 us -> 34.2 us  [the longest x1 18 us: local(): lax.all_to_all(jnp.broadcast_to(spread[None], (count, *spread.shape)), PL...]
  transfers between devices with their start and end apart: 16 -> 16, of which waited for: 5 -> 5; matrix products, arithmetic and copies ran while one was open for 0% -> 0% of each run, Pallas kernels for 5% -> 4%
where the time goes in v8:
time: 88.3 us; the launch traced here: 88.1 us
  blocking collectives  34.2 us (39%)
  waiting for transfers between devices  23.7 us (27%)
  starting transfers between devices  19.4 us (22%)
  Pallas kernels  6.39 us (7%)
  between operations  1.65 us (2%)
  other arithmetic  1.56 us (2%)
  local copies, waits for them, and re-layouts  1.11 us (1%)
    all_to_all x1, blocking collectives, local(): lax.all_to_all(jnp.broadcast_to(spread[None], (count, *spread.shape)), PL...  18 us
    all_to_all x1, blocking collectives, local(): lax.all_to_all(quarters.reshape(2 * DEPTH, *quarters.shape[2:]), ('z', 'y...  16.3 us
    ppermute x5, starting transfers between devices, to_pairs(): return lax.ppermute(a, ('yl', 'xp', 'xq'), sends)  14.5 us
    ppermute x5, waiting for transfers between devices, to_pairs(): return lax.ppermute(a, ('yl', 'xp', 'xq'), sends)  12.1 us
    ppermute x1, waiting for transfers between devices, local(): lax.ppermute(jnp.where(lower_half, rhs[:, WIDE:], rhs[:, :WIDE]), 'xq', F...  7.79 us
    pallas_call x6, Pallas kernels, call(): pl.pallas_call(kernel, out_shape=outs, in_specs=[smem if a.dtype == jnp.i...  6.39 us
    ppermute x1, waiting for transfers between devices, local(): mate3 = lax.ppermute(own3, 'xq', FLIP)  2.24 us
  transfers between devices with their start and end apart: 16, of which 5 were waited for; matrix products, arithmetic and copies ran while one was open for 0% of the time, Pallas kernels for 4%

profile of v8, /device:TPU:0, one launch (start us, length us, event | category | flops | bytes accessed | tf_op | source)
XLA Modules:
  0.0 88.1 jit_solution(4460001011310595508)
XLA Ops:
  0.6 0.0 copy-start
  0.6 0.0 copy-start.1
  1.5 1.5 %fusion.1.own_ref.w_own_ref = bf16[4,256,256]{2,1,0:T(8,128)(2,1)S(1)} fusion(bf16[1,1,256,4,1,256]{5,3,4,2,1,0:T(4,128)(2,1)} %param.7, bf16[1,1,256,4,1,256]{5,3,4,2,1,0:T(4,128)(2,1)} %param.6, f32[]{:T(128)S(6)} %copy.15, pred[4]{0:T(512)(128)(4,1)S(1)} %add_compare_fusion), kind=kLoop, calls=%fused_computation.2 | loop fusion | flops 1572864 | bytes 1572872 | tf_op jit(solution)/shard_map/transpose | solution.py:157
  2.9 0.7 fusion.2
  3.7 1.6 %collective-permute-start.2 = (bf16[1,256,256]{2,1,0:T(8,128)(2,1)}, bf16[1,256,256]{2,1,0:T(8,128)(2,1)S(1)}, u32[]{:S(2)}, u32[]{:S(2)}) collective-permute-start(bf16[1,256,256]{2,1,0:T(8,128)(2,1)} %get-tuple-element.21), channel_id=1, source_target_pairs={{0,2},{2,0},{1,3},{3,1},{4,6},{6,4},{5,7},{7,5},{8,10},{10,8},{9,1... | collective-permute-start | bytes 393224 | tf_op jit(solution)/shard_map/ppermute | solution.py:159
  5.3 0.5 collective-permute-start.8
  5.8 0.1 pad_add_fusion.where_ref
  5.9 1.7 %collective-permute-start = (f32[256,128]{1,0:T(8,128)S(1)}, f32[256,128]{1,0:T(8,128)S(1)}, u32[]{:S(2)}, u32[]{:S(2)}) collective-permute-start(f32[256,128]{1,0:T(8,128)S(1)} %slice_select_fusion), channel_id=1, source_target_pairs={{0,2},{2,0},{1,3},{3,1},{4,6},{6,4},{5,7},{7,5},{8,10},{10,8},{9,1... | collective-permute-start | bytes 393224 | tf_op jit(solution)/shard_map/ppermute | solution.py:161
  7.6 0.4 collective-permute-start.5
  8.0 0.0 collective-permute-start.1
  8.0 2.2 %collective-permute-done.2.rest_1_ = bf16[1,256,256]{2,1,0:T(8,128)(2,1)S(1)} collective-permute-done((bf16[1,256,256]{2,1,0:T(8,128)(2,1)}, bf16[1,256,256]{2,1,0:T(8,128)(2,1)S(1)}, u32[]{:S(2)}, u32[]{:S(2)}) %collective-permute-start.2) | collective-permute-done | bytes 131104 | tf_op jit(solution)/shard_map/ppermute | solution.py:159
  10.2 0.0 collective-permute-start.3
  10.2 0.6 shard_map.77.inv_ref
  10.9 7.8 %collective-permute-done.mate_rhs_ref = f32[256,128]{1,0:T(8,128)S(1)} collective-permute-done((f32[256,128]{1,0:T(8,128)S(1)}, f32[256,128]{1,0:T(8,128)S(1)}, u32[]{:S(2)}, u32[]{:S(2)}) %collective-permute-start) | collective-permute-done | bytes 131104 | tf_op jit(solution)/shard_map/ppermute | solution.py:161
  18.7 0.0 collective-permute-start.4
  18.7 1.5 %collective-permute-done.5.rest_4_ = bf16[1,256,256]{2,1,0:T(8,128)(2,1)S(1)} collective-permute-done((bf16[1,256,256]{2,1,0:T(8,128)(2,1)}, bf16[1,256,256]{2,1,0:T(8,128)(2,1)S(1)}, u32[]{:S(2)}, u32[]{:S(2)}) %collective-permute-start.5) | collective-permute-done | bytes 131104 | tf_op jit(solution)/shard_map/ppermute | solution.py:163
  20.2 0.0 collective-permute-start.7
  20.2 0.0 collective-permute-done.1.rest_0_.other3_ref
  20.2 0.5 collective-permute-start.6
  20.7 0.0 collective-permute-done.3.rest_2_
  20.7 0.6 shard_map.78.rest_7_
  21.3 0.7 collective-permute-start.11
  22.0 0.0 collective-permute-done.8.rest_7_
  22.0 0.1 collective-permute-start.9
  22.1 0.0 collective-permute-done.4.rest_3_.other2_ref
  22.1 0.7 collective-permute-start.10
  22.8 0.0 collective-permute-done.6.rest_5_
  22.8 0.0 collective-permute-done.11.rest_6_
  22.8 0.6 shard_map.79.rest_13_
  23.4 0.0 copy-start.2
  23.4 1.4 %collective-permute-start.13 = (bf16[2,256,128]{2,1,0:T(8,128)(2,1)S(1)}, bf16[2,256,128]{2,1,0:T(8,128)(2,1)S(1)}, u32[]{:S(2)}, u32[]{:S(2)}) collective-permute-start(bf16[2,256,128]{2,1,0:T(8,128)(2,1)S(1)} %shard_map.79.rest_13_), channel_id=1, source_target_pairs={{8,0},{10,2},{9,1},{11,3},{24,16},{26,18},{25,17},{27,19},{40,32},... | collective-permute-start | bytes 393224 | tf_op jit(solution)/shard_map/ppermute | solution.py:136
  24.8 10.5 %collective-permute-start.12 = (bf16[2,256,128]{2,1,0:T(8,128)(2,1)S(1)}, bf16[2,256,128]{2,1,0:T(8,128)(2,1)S(1)}, u32[]{:S(2)}, u32[]{:S(2)}) collective-permute-start(bf16[2,256,128]{2,1,0:T(8,128)(2,1)S(1)} %shard_map.79.rest_13_), channel_id=1, source_target_pairs={{8,6},{10,4},{14,0},{12,2},{0,8},{2,10},{6,14},{4,12},{9,7},{11,5}... | collective-permute-start | bytes 393224 | tf_op jit(solution)/shard_map/ppermute | solution.py:136
  35.3 0.0 collective-permute-done.7.rest_6_.other01_ref
  35.3 0.0 collective-permute-done.10.rest_9_
  35.3 0.0 collective-permute-done.9.rest_8_
  35.3 5.1 %collective-permute-done.13.rest_12_ = bf16[2,256,128]{2,1,0:T(8,128)(2,1)S(1)} collective-permute-done((bf16[2,256,128]{2,1,0:T(8,128)(2,1)S(1)}, bf16[2,256,128]{2,1,0:T(8,128)(2,1)S(1)}, u32[]{:S(2)}, u32[]{:S(2)}) %collective-permute-start.13) | collective-permute-done | bytes 131104 | tf_op jit(solution)/shard_map/ppermute | solution.py:136
  40.4 0.0 collective-permute-done.12.rest_10_.rest_11_
  40.4 1.0 %shard_map.80 = (bf16[2,256,128]{2,1,0:T(8,128)(2,1)S(1)}, f32[2,256,128]{2,1,0:T(8,128)S(1)}) custom-call(s32[4]{0:T(128)S(1)} %pad_add_fusion.where_ref, bf16[2,2,256,256]{3,2,1,0:T(8,128)(2,1)S(1)} %shard_map.77.inv_ref, f32[256,256]{1,0:T(8,128)S(1)} %bitcast.27, f32[256,128]{1,0:T(8,128)S(1)} %collective-permute-done.mate_rhs_ref, ...), custom_call_target="tpu_custom_call" | custom-call | tf_op jit(solution)/shard_map/pallas_call | solution.py:121
  41.4 1.3 %collective-permute-start.14 = (bf16[2,256,128]{2,1,0:T(8,128)(2,1)S(1)}, bf16[2,256,128]{2,1,0:T(8,128)(2,1)S(1)}, u32[]{:S(2)}, u32[]{:S(2)}) collective-permute-start(bf16[2,256,128]{2,1,0:T(8,128)(2,1)S(1)} %get-tuple-element.14.rest_11_), channel_id=1, source_target_pairs={{6,0},{4,2},{14,6},{12,4},{7,1},{5,3},{15,7},{13,5},{22,16},{20,18... | collective-permute-start | bytes 393224 | tf_op jit(solution)/shard_map/ppermute | solution.py:136
  42.7 0.1 copy.14
  42.8 0.1 collective-permute-start.15
  42.9 7.0 %collective-permute-done.14.rest_9_ = bf16[2,256,128]{2,1,0:T(8,128)(2,1)S(1)} collective-permute-done((bf16[2,256,128]{2,1,0:T(8,128)(2,1)S(1)}, bf16[2,256,128]{2,1,0:T(8,128)(2,1)S(1)}, u32[]{:S(2)}, u32[]{:S(2)}) %collective-permute-start.14) | collective-permute-done | bytes 131104 | tf_op jit(solution)/shard_map/ppermute | solution.py:136
  49.9 1.6 %shard_map.81 = bf16[2,256,128]{2,1,0:T(8,128)(2,1)S(1)} custom-call(s32[4]{0:T(128)S(1)} %pad_add_fusion.where_ref, bf16[2,2,256,256]{3,2,1,0:T(8,128)(2,1)S(1)} %shard_map.77.inv_ref, f32[256,256]{1,0:T(8,128)S(1)} %bitcast.28, f32[256,128]{1,0:T(8,128)S(1)} %collective-permute-done.mate_rhs_ref, bf16[4,256,256]{2,1,0:T(8,128)(2,1)S(1)} %fusion.1.own_ref.w_own_ref, ...), custom_call_target="tpu_custom_call" | custom-call | tf_op jit(solution)/shard_map/pallas_call | solution.py:121
  51.5 16.3 %all_to_all.10 = bf16[8,128,128]{2,1,0:T(8,128)(2,1)S(1)} all-to-all(bf16[8,128,128]{2,1,0:T(8,128)(2,1)S(1)} %bitcast.33), channel_id=1, replica_groups=mesh['z'=4,'yh'=2,'yl'=2,'xp'=2,'xq'=2,'col'=2] {'z','yh'}, dimensions={0} | all-to-all | bytes 524288 | tf_op jit(solution)/shard_map/all_to_all | solution.py:201
  67.8 0.0 collective-permute-done.15.z_other_ref
  67.8 0.2 broadcast_in_dim.34
  68.0 18.0 %all_to_all.11.x_ref = bf16[32,128,128]{2,1,0:T(8,128)(2,1)S(1)} all-to-all(bf16[32,128,128]{2,1,0:T(8,128)(2,1)S(1)} %broadcast_in_dim.34), channel_id=1, replica_groups=mesh['z'=4,'yh'=2,'yl'=2,'xp'=2,'xq'=2,'col'=2] {'z','yl','xp','xq'}, dimensions={0} | all-to-all | bytes 2097152 | tf_op jit(solution)/shard_map/all_to_all | solution.py:206
  86.0 2.1 %shard_map.82 = (f32[256,256]{1,0:T(8,128)}, f32[256,256]{1,0:T(8,128)}) custom-call(s32[4]{0:T(128)S(1)} %pad_add_fusion.where_ref, bf16[32,128,128]{2,1,0:T(8,128)(2,1)S(1)} %all_to_all.11.x_ref, bf16[4,256,256]{2,1,0:T(8,128)(2,1)S(1)} %fusion.1.own_ref.w_own_ref, bf16[1,256,256]{2,1,0:T(8,128)(2,1)S(1)} %collective-permute-done.1.rest_0_.other3_ref, ...), custom_call_target="tpu_custom_call" | custom-call | tf_op jit(solution)/shard_map/pallas_call | solution.py:121
  (11 shorter events, 0.1 us)
Async XLA Ops:
  0.6 5.2 %copy-start = (f32[1,1,256,256]{3,2,1,0:T(8,128)S(1)}, f32[1,1,256,256]{3,2,1,0:T(8,128)}, u32[]{:S(2)}) copy-start(f32[1,1,256,256]{3,2,1,0:T(8,128)} %param.11) | copy-start | bytes 786436
  0.6 9.6 %copy-start.1 = (f32[4,2,256,256]{3,2,1,0:T(8,128)S(1)}, f32[4,2,256,256]{3,2,1,0:T(8,128)}, u32[]{:S(2)}) copy-start(f32[4,2,256,256]{3,2,1,0:T(8,128)} %inv_ref.1) | copy-start | bytes 6291460
  3.7 6.6 %collective-permute-start.2 = (bf16[1,256,256]{2,1,0:T(8,128)(2,1)}, bf16[1,256,256]{2,1,0:T(8,128)(2,1)S(1)}, u32[]{:S(2)}, u32[]{:S(2)}) collective-permute-start(bf16[1,256,256]{2,1,0:T(8,128)(2,1)} %get-tuple-element.21), channel_id=1, source_target_pairs={{0,2},{2,0},{1,3},{3,1},{4,6},{6,4},{5,7},{7,5},{8,10},{10,8},{9,1... | collective-permute-start | bytes 393224 | tf_op jit(solution)/shard_map/ppermute | solution.py:159
  5.3 16.7 %collective-permute-start.8 = (bf16[2,256,256]{2,1,0:T(8,128)(2,1)S(1)}, bf16[2,256,256]{2,1,0:T(8,128)(2,1)S(1)}, u32[]{:S(2)}, u32[]{:S(2)}) collective-permute-start(bf16[2,256,256]{2,1,0:T(8,128)(2,1)S(1)} %slice.30), channel_id=1, source_target_pairs={{0,2},{2,0},{1,3},{3,1},{4,6},{6,4},{5,7},{7,5},{8,10},{10,8},{9,1... | collective-permute-start | bytes 786440 | tf_op jit(solution)/shard_map/ppermute | solution.py:168
  5.8 12.9 %copy-start.3 = (bf16[1,256,256]{2,1,0:T(8,128)(2,1)S(1)}, bf16[1,256,256]{2,1,0:T(8,128)(2,1)}, u32[]{:S(2)}) copy-start(bf16[1,256,256]{2,1,0:T(8,128)(2,1)} %get-tuple-element.20) | copy-start | bytes 393220
  5.9 12.8 %collective-permute-start = (f32[256,128]{1,0:T(8,128)S(1)}, f32[256,128]{1,0:T(8,128)S(1)}, u32[]{:S(2)}, u32[]{:S(2)}) collective-permute-start(f32[256,128]{1,0:T(8,128)S(1)} %slice_select_fusion), channel_id=1, source_target_pairs={{0,2},{2,0},{1,3},{3,1},{4,6},{6,4},{5,7},{7,5},{8,10},{10,8},{9,1... | collective-permute-start | bytes 393224 | tf_op jit(solution)/shard_map/ppermute | solution.py:161
  7.6 12.6 %collective-permute-start.5 = (bf16[1,256,256]{2,1,0:T(8,128)(2,1)}, bf16[1,256,256]{2,1,0:T(8,128)(2,1)S(1)}, u32[]{:S(2)}, u32[]{:S(2)}) collective-permute-start(bf16[1,256,256]{2,1,0:T(8,128)(2,1)} %get-tuple-element.20), channel_id=1, source_target_pairs={{0,2},{2,0},{1,3},{3,1},{4,6},{6,4},{5,7},{7,5},{8,10},{10,8},{9,1... | collective-permute-start | bytes 393224 | tf_op jit(solution)/shard_map/ppermute | solution.py:163
  8.0 12.2 %collective-permute-start.1 = (bf16[1,256,256]{2,1,0:T(8,128)(2,1)}, bf16[1,256,256]{2,1,0:T(8,128)(2,1)S(1)}, u32[]{:S(2)}, u32[]{:S(2)}) collective-permute-start(bf16[1,256,256]{2,1,0:T(8,128)(2,1)} %get-tuple-element.21), channel_id=1, source_target_pairs={{0,1},{1,0},{2,3},{3,2},{4,5},{5,4},{6,7},{7,6},{8,9},{9,8},{10,11... | collective-permute-start | bytes 393224 | tf_op jit(solution)/shard_map/ppermute | solution.py:160
  10.2 10.5 %collective-permute-start.3 = (bf16[1,256,256]{2,1,0:T(8,128)(2,1)S(1)}, bf16[1,256,256]{2,1,0:T(8,128)(2,1)S(1)}, u32[]{:S(2)}, u32[]{:S(2)}) collective-permute-start(bf16[1,256,256]{2,1,0:T(8,128)(2,1)S(1)} %collective-permute-done.2.rest_1_), channel_id=1, source_target_pairs={{0,1},{1,0},{2,3},{3,2},{4,5},{5,4},{6,7},{7,6},{8,9},{9,8},{10,11... | collective-permute-start | bytes 393224 | tf_op jit(solution)/shard_map/ppermute | solution.py:162
  18.7 3.4 %collective-permute-start.4 = (bf16[1,256,256]{2,1,0:T(8,128)(2,1)S(1)}, bf16[1,256,256]{2,1,0:T(8,128)(2,1)S(1)}, u32[]{:S(2)}, u32[]{:S(2)}) collective-permute-start(bf16[1,256,256]{2,1,0:T(8,128)(2,1)S(1)} %copy-done.3), channel_id=1, source_target_pairs={{0,1},{1,0},{2,3},{3,2},{4,5},{5,4},{6,7},{7,6},{8,9},{9,8},{10,11... | collective-permute-start | bytes 393224 | tf_op jit(solution)/shard_map/ppermute | solution.py:164
  20.2 15.1 %collective-permute-start.7 = (bf16[2,256,256]{2,1,0:T(8,128)(2,1)S(1)}, bf16[2,256,256]{2,1,0:T(8,128)(2,1)S(1)}, u32[]{:S(2)}, u32[]{:S(2)}) collective-permute-start(bf16[2,256,256]{2,1,0:T(8,128)(2,1)S(1)} %slice.30), channel_id=1, source_target_pairs={{0,1},{1,0},{2,3},{3,2},{4,5},{5,4},{6,7},{7,6},{8,9},{9,8},{10,11... | collective-permute-start | bytes 786440 | tf_op jit(solution)/shard_map/ppermute | solution.py:169
  20.2 2.6 %collective-permute-start.6 = (bf16[1,256,256]{2,1,0:T(8,128)(2,1)S(1)}, bf16[1,256,256]{2,1,0:T(8,128)(2,1)S(1)}, u32[]{:S(2)}, u32[]{:S(2)}) collective-permute-start(bf16[1,256,256]{2,1,0:T(8,128)(2,1)S(1)} %collective-permute-done.5.rest_4_), channel_id=1, source_target_pairs={{0,1},{1,0},{2,3},{3,2},{4,5},{5,4},{6,7},{7,6},{8,9},{9,8},{10,11... | collective-permute-start | bytes 393224 | tf_op jit(solution)/shard_map/ppermute | solution.py:170
  21.3 1.5 %collective-permute-start.11 = (bf16[2,256,128]{2,1,0:T(8,128)(2,1)S(1)}, bf16[2,256,128]{2,1,0:T(8,128)(2,1)S(1)}, u32[]{:S(2)}, u32[]{:S(2)}) collective-permute-start(bf16[2,256,128]{2,1,0:T(8,128)(2,1)S(1)} %shard_map.78.rest_7_), channel_id=1, source_target_pairs={{14,8},{12,10},{6,14},{4,12},{15,9},{13,11},{7,15},{5,13},{30,24},... | collective-permute-start | bytes 393224 | tf_op jit(solution)/shard_map/ppermute | solution.py:136
  22.0 13.3 %collective-permute-start.9 = (bf16[2,256,256]{2,1,0:T(8,128)(2,1)S(1)}, bf16[2,256,256]{2,1,0:T(8,128)(2,1)S(1)}, u32[]{:S(2)}, u32[]{:S(2)}) collective-permute-start(bf16[2,256,256]{2,1,0:T(8,128)(2,1)S(1)} %collective-permute-done.8.rest_7_), channel_id=1, source_target_pairs={{0,1},{1,0},{2,3},{3,2},{4,5},{5,4},{6,7},{7,6},{8,9},{9,8},{10,11... | collective-permute-start | bytes 786440 | tf_op jit(solution)/shard_map/ppermute | solution.py:171
  22.1 13.2 %collective-permute-start.10 = (bf16[2,256,128]{2,1,0:T(8,128)(2,1)S(1)}, bf16[2,256,128]{2,1,0:T(8,128)(2,1)S(1)}, u32[]{:S(2)}, u32[]{:S(2)}) collective-permute-start(bf16[2,256,128]{2,1,0:T(8,128)(2,1)S(1)} %shard_map.78.rest_7_), channel_id=1, source_target_pairs={{14,6},{12,4},{15,7},{13,5},{30,22},{28,20},{31,23},{29,21},{46,38... | collective-permute-start | bytes 393224 | tf_op jit(solution)/shard_map/ppermute | solution.py:136
  23.4 19.3 %copy-start.2 = (bf16[1,1,256,4,1,256]{5,3,4,2,1,0:T(4,128)(2,1)S(1)}, bf16[1,1,256,4,1,256]{5,3,4,2,1,0:T(4,128)(2,1)}, u32[]{:S(2)}) copy-start(bf16[1,1,256,4,1,256]{5,3,4,2,1,0:T(4,128)(2,1)} %param.8) | copy-start | bytes 1572868
  23.4 17.0 %collective-permute-start.13 = (bf16[2,256,128]{2,1,0:T(8,128)(2,1)S(1)}, bf16[2,256,128]{2,1,0:T(8,128)(2,1)S(1)}, u32[]{:S(2)}, u32[]{:S(2)}) collective-permute-start(bf16[2,256,128]{2,1,0:T(8,128)(2,1)S(1)} %shard_map.79.rest_13_), channel_id=1, source_target_pairs={{8,0},{10,2},{9,1},{11,3},{24,16},{26,18},{25,17},{27,19},{40,32},... | collective-permute-start | bytes 393224 | tf_op jit(solution)/shard_map/ppermute | solution.py:136
  24.8 15.6 %collective-permute-start.12 = (bf16[2,256,128]{2,1,0:T(8,128)(2,1)S(1)}, bf16[2,256,128]{2,1,0:T(8,128)(2,1)S(1)}, u32[]{:S(2)}, u32[]{:S(2)}) collective-permute-start(bf16[2,256,128]{2,1,0:T(8,128)(2,1)S(1)} %shard_map.79.rest_13_), channel_id=1, source_target_pairs={{8,6},{10,4},{14,0},{12,2},{0,8},{2,10},{6,14},{4,12},{9,7},{11,5}... | collective-permute-start | bytes 393224 | tf_op jit(solution)/shard_map/ppermute | solution.py:136
  41.4 8.5 %collective-permute-start.14 = (bf16[2,256,128]{2,1,0:T(8,128)(2,1)S(1)}, bf16[2,256,128]{2,1,0:T(8,128)(2,1)S(1)}, u32[]{:S(2)}, u32[]{:S(2)}) collective-permute-start(bf16[2,256,128]{2,1,0:T(8,128)(2,1)S(1)} %get-tuple-element.14.rest_11_), channel_id=1, source_target_pairs={{6,0},{4,2},{14,6},{12,4},{7,1},{5,3},{15,7},{13,5},{22,16},{20,18... | collective-permute-start | bytes 393224 | tf_op jit(solution)/shard_map/ppermute | solution.py:136
  42.8 25.0 %collective-permute-start.15 = (bf16[4,256,256]{2,1,0:T(8,128)(2,1)S(1)}, bf16[4,256,256]{2,1,0:T(8,128)(2,1)S(1)}, u32[]{:S(2)}, u32[]{:S(2)}) collective-permute-start(bf16[4,256,256]{2,1,0:T(8,128)(2,1)S(1)} %bitcast.30), channel_id=1, source_target_pairs={{0,1},{1,0},{2,3},{3,2},{4,5},{5,4},{6,7},{7,6},{8,9},{9,8},{10,11... | collective-permute-start | bytes 1572872 | tf_op jit(solution)/shard_map/ppermute | solution.py:172

commit v9 on v3

--- a/solution.py
+++ b/solution.py
@@ -12,8 +12,9 @@
 HALF = STEPS // 2
 NB = 256
 WIDE = NB // 2
-GROUPS = 8
+DEPTH = 4
 ROWS = ("z", "yh", "yl", "xp", "xq")
+PLANE = ("yh", "yl", "xp", "xq")
 FLIP = [(0, 1), (1, 0)]
 
 
@@ -103,11 +104,7 @@
         yl, xp = b // 2, b % 2
         own, other = w_own_ref[b], (other01_ref[b] if b < 2 else (other2_ref, other3_ref)[b - 2][0])
         for w, z, p in ((own, z_own_ref, parity), (other, z_other_ref, 1 - parity)):
-            columns = []
-            for half in range(2):
-                at = [(((4 * p + i) * 2 + yl) * 2 + xp) * 2 + (half ^ xp) for i in range(4)]
-                columns.append(jnp.concatenate([x_ref[n] for n in at], 0))
-            x = jnp.concatenate(columns, 1)
+            x = jnp.concatenate([x_ref[((2 * p + yl) * 2 + xp) * 2 + (half ^ xp)] for half in range(2)], 1)
             pending = pending - dot(w, x)
             image = image + dot(z[b], x)
     pending_ref[...] = pending
@@ -196,12 +193,13 @@
     x0 = solve(0, [(1, e)], [], acc, x1)
 
     spread = lax.all_to_all(
-        x0.reshape(GROUPS, 2 * NB // GROUPS, WIDE), ("z", "yh"), 0, 0, tiled=True
-    )[GROUPS - 1]
+        jnp.broadcast_to(x0[None], (DEPTH, *x0.shape)).reshape(2 * DEPTH, *x0.shape[1:]),
+        ("z", "yh"), 0, 0, tiled=True,
+    )[2 * DEPTH - 1]
     spread, other_z = lax.optimization_barrier((spread, other_z))
-    count = lax.axis_size(ROWS)
+    count = lax.axis_size(PLANE)
     every = lax.all_to_all(
-        jnp.broadcast_to(spread[None], (count, *spread.shape)), ROWS, 0, 0, tiled=True
+        jnp.broadcast_to(spread[None], (count, *spread.shape)), PLANE, 0, 0, tiled=True
     )
 
     out = jax.ShapeDtypeStruct((NB, NB), jnp.float32)

time: 89.2 us -> 90.8 us (1.018)
  blocking collectives: 36.5 us -> 18 us
  waiting for transfers between devices: 31.1 us -> 41.6 us
  starting transfers between devices: 10.6 us -> 17.7 us
  local copies, waits for them, and re-layouts: 1.09 us -> 2.57 us
  Pallas kernels: 6.4 us -> 7.31 us
    all_to_all x2 -> x1, blocking collectives: 36.5 us -> 18 us  [local(): lax.all_to_all(jnp.broadcast_to(spread[None], (count, *spread.shape)), PL...]
    all_to_all x0 -> x1, waiting for transfers between devices: none -> 10.7 us  [local(): lax.all_to_all(jnp.broadcast_to(x0[None], (DEPTH, *x0.shape)).reshape(2 *...]
    all_to_all x0 -> x1, starting transfers between devices: none -> 7.65 us  [local(): lax.all_to_all(jnp.broadcast_to(x0[None], (DEPTH, *x0.shape)).reshape(2 *...]
    ppermute x1, waiting for transfers between devices: 2.24 us -> 0.97 us  [local(): mate3 = lax.ppermute(own3, 'xq', FLIP)]
    ppermute x1, waiting for transfers between devices: 0.9 us -> 2.02 us  [local(): mate2 = lax.ppermute(own[2:3], 'xq', FLIP)]
    pallas_call x6, Pallas kernels: 6.4 us -> 7.31 us  [call(): pl.pallas_call(kernel, out_shape=outs, in_specs=[smem if a.dtype == jnp.i...]
  transfers between devices with their start and end apart: 16 -> 17, of which waited for: 5 -> 6; matrix products, arithmetic and copies ran while one was open for 0% -> 1% of each run, Pallas kernels for 5% -> 2%
where the time goes in v9:
time: 90.8 us; the launch traced here: 90.4 us
  waiting for transfers between devices  41.6 us (46%)
  blocking collectives  18 us (20%)
  starting transfers between devices  17.7 us (19%)
  Pallas kernels  7.31 us (8%)
  local copies, waits for them, and re-layouts  2.57 us (3%)
  between operations  1.66 us (2%)
  other arithmetic  1.56 us (2%)
    ppermute x5, waiting for transfers between devices, to_pairs(): return lax.ppermute(a, ('yl', 'xp', 'xq'), sends)  20 us
    all_to_all x1, blocking collectives, local(): lax.all_to_all(jnp.broadcast_to(spread[None], (count, *spread.shape)), PL...  18 us
    all_to_all x1, waiting for transfers between devices, local(): lax.all_to_all(jnp.broadcast_to(x0[None], (DEPTH, *x0.shape)).reshape(2 *...  10.7 us
    ppermute x1, waiting for transfers between devices, local(): lax.ppermute(jnp.where(lower_half, rhs[:, WIDE:], rhs[:, :WIDE]), 'xq', F...  7.96 us
    all_to_all x1, starting transfers between devices, local(): lax.all_to_all(jnp.broadcast_to(x0[None], (DEPTH, *x0.shape)).reshape(2 *...  7.65 us
    pallas_call x6, Pallas kernels, call(): pl.pallas_call(kernel, out_shape=outs, in_specs=[smem if a.dtype == jnp.i...  7.31 us
    ppermute x5, starting transfers between devices, to_pairs(): return lax.ppermute(a, ('yl', 'xp', 'xq'), sends)  5.21 us
    ppermute x1, waiting for transfers between devices, local(): mate2 = lax.ppermute(own[2:3], 'xq', FLIP)  2.02 us
  transfers between devices with their start and end apart: 17, of which 6 were waited for; matrix products, arithmetic and copies ran while one was open for 1% of the time, Pallas kernels for 2%

profile of v9, /device:TPU:0, one launch (start us, length us, event | category | flops | bytes accessed | tf_op | source)
XLA Modules:
  0.0 90.4 jit_solution(16036725833103434729)
XLA Ops:
  1.5 1.5 %fusion.1.own_ref.w_own_ref = bf16[4,256,256]{2,1,0:T(8,128)(2,1)S(1)} fusion(bf16[1,1,256,4,1,256]{5,3,4,2,1,0:T(4,128)(2,1)} %param.7, bf16[1,1,256,4,1,256]{5,3,4,2,1,0:T(4,128)(2,1)} %param.6, f32[]{:T(128)S(6)} %copy.15, pred[4]{0:T(512)(128)(4,1)S(1)} %add_compare_fusion), kind=kLoop, calls=%fused_computation.2 | loop fusion | flops 1572864 | bytes 1572872 | tf_op jit(solution)/shard_map/transpose | solution.py:153
  2.9 0.7 fusion.2
  3.6 1.6 %collective-permute-start.2 = (bf16[1,256,256]{2,1,0:T(8,128)(2,1)}, bf16[1,256,256]{2,1,0:T(8,128)(2,1)S(1)}, u32[]{:S(2)}, u32[]{:S(2)}) collective-permute-start(bf16[1,256,256]{2,1,0:T(8,128)(2,1)} %get-tuple-element.21), channel_id=1, source_target_pairs={{0,2},{2,0},{1,3},{3,1},{4,6},{6,4},{5,7},{7,5},{8,10},{10,8},{9,1... | collective-permute-start | bytes 393224 | tf_op jit(solution)/shard_map/ppermute | solution.py:155
  5.2 0.7 slice.30
  5.9 0.4 collective-permute-start.8
  6.4 0.1 pad_add_fusion.where_ref
  6.5 1.7 %collective-permute-start = (f32[256,128]{1,0:T(8,128)S(1)}, f32[256,128]{1,0:T(8,128)S(1)}, u32[]{:S(2)}, u32[]{:S(2)}) collective-permute-start(f32[256,128]{1,0:T(8,128)S(1)} %slice_select_fusion), channel_id=1, source_target_pairs={{0,2},{2,0},{1,3},{3,1},{4,6},{6,4},{5,7},{7,5},{8,10},{10,8},{9,1... | collective-permute-start | bytes 393224 | tf_op jit(solution)/shard_map/ppermute | solution.py:157
  8.1 0.4 collective-permute-start.5
  8.6 0.0 collective-permute-start.1
  8.6 1.0 %collective-permute-done.2.rest_1_ = bf16[1,256,256]{2,1,0:T(8,128)(2,1)S(1)} collective-permute-done((bf16[1,256,256]{2,1,0:T(8,128)(2,1)}, bf16[1,256,256]{2,1,0:T(8,128)(2,1)S(1)}, u32[]{:S(2)}, u32[]{:S(2)}) %collective-permute-start.2) | collective-permute-done | bytes 131104 | tf_op jit(solution)/shard_map/ppermute | solution.py:155
  9.5 0.0 collective-permute-start.3
  9.5 0.6 shard_map.77.inv_ref
  10.2 8.0 %collective-permute-done.mate_rhs_ref = f32[256,128]{1,0:T(8,128)S(1)} collective-permute-done((f32[256,128]{1,0:T(8,128)S(1)}, f32[256,128]{1,0:T(8,128)S(1)}, u32[]{:S(2)}, u32[]{:S(2)}) %collective-permute-start) | collective-permute-done | bytes 131104 | tf_op jit(solution)/shard_map/ppermute | solution.py:157
  18.1 0.0 collective-permute-start.4
  18.1 2.0 %collective-permute-done.5.rest_4_ = bf16[1,256,256]{2,1,0:T(8,128)(2,1)S(1)} collective-permute-done((bf16[1,256,256]{2,1,0:T(8,128)(2,1)S(1)}, bf16[1,256,256]{2,1,0:T(8,128)(2,1)S(1)}, u32[]{:S(2)}, u32[]{:S(2)}) %collective-permute-start.5) | collective-permute-done | bytes 131104 | tf_op jit(solution)/shard_map/ppermute | solution.py:159
  20.2 0.0 collective-permute-start.7
  20.2 0.0 collective-permute-done.1.rest_0_.other3_ref
  20.2 0.5 collective-permute-start.6
  20.7 0.0 collective-permute-done.3.rest_2_
  20.7 0.6 shard_map.78.rest_7_
  21.3 0.7 collective-permute-start.11
  21.9 0.0 collective-permute-done.8.rest_7_
  22.0 0.1 collective-permute-start.9
  22.0 0.0 collective-permute-done.4.rest_3_.other2_ref
  22.1 0.7 collective-permute-start.10
  22.7 0.0 collective-permute-done.6.rest_5_
  22.7 0.0 collective-permute-done.11.rest_6_
  22.8 0.6 shard_map.79.rest_13_
  23.3 1.3 %collective-permute-start.13 = (bf16[2,256,128]{2,1,0:T(8,128)(2,1)S(1)}, bf16[2,256,128]{2,1,0:T(8,128)(2,1)S(1)}, u32[]{:S(2)}, u32[]{:S(2)}) collective-permute-start(bf16[2,256,128]{2,1,0:T(8,128)(2,1)S(1)} %shard_map.79.rest_13_), channel_id=1, source_target_pairs={{8,0},{10,2},{9,1},{11,3},{24,16},{26,18},{25,17},{27,19},{40,32},... | collective-permute-start | bytes 393224 | tf_op jit(solution)/shard_map/ppermute | solution.py:132
  24.6 1.3 %collective-permute-start.12 = (bf16[2,256,128]{2,1,0:T(8,128)(2,1)S(1)}, bf16[2,256,128]{2,1,0:T(8,128)(2,1)S(1)}, u32[]{:S(2)}, u32[]{:S(2)}) collective-permute-start(bf16[2,256,128]{2,1,0:T(8,128)(2,1)S(1)} %shard_map.79.rest_13_), channel_id=1, source_target_pairs={{8,6},{10,4},{14,0},{12,2},{9,7},{11,5},{15,1},{13,3},{24,22},{26,... | collective-permute-start | bytes 393224 | tf_op jit(solution)/shard_map/ppermute | solution.py:132
  25.9 0.0 collective-permute-done.7.rest_6_.other01_ref
  25.9 0.0 collective-permute-done.10.rest_9_
  25.9 0.0 collective-permute-done.9.rest_8_
  26.0 12.8 %collective-permute-done.13.rest_12_ = bf16[2,256,128]{2,1,0:T(8,128)(2,1)S(1)} collective-permute-done((bf16[2,256,128]{2,1,0:T(8,128)(2,1)S(1)}, bf16[2,256,128]{2,1,0:T(8,128)(2,1)S(1)}, u32[]{:S(2)}, u32[]{:S(2)}) %collective-permute-start.13) | collective-permute-done | bytes 131104 | tf_op jit(solution)/shard_map/ppermute | solution.py:132
  38.7 0.0 collective-permute-done.12.rest_10_.rest_11_
  38.7 1.4 %shard_map.80 = (bf16[2,256,128]{2,1,0:T(8,128)(2,1)S(1)}, f32[2,256,128]{2,1,0:T(8,128)S(1)}) custom-call(s32[4]{0:T(128)S(1)} %pad_add_fusion.where_ref, bf16[2,2,256,256]{3,2,1,0:T(8,128)(2,1)S(1)} %shard_map.77.inv_ref, f32[256,256]{1,0:T(8,128)S(1)} %bitcast.26, f32[256,128]{1,0:T(8,128)S(1)} %collective-permute-done.mate_rhs_ref, ...), custom_call_target="tpu_custom_call" | custom-call | tf_op jit(solution)/shard_map/pallas_call | solution.py:117
  40.1 1.3 %collective-permute-start.14 = (bf16[2,256,128]{2,1,0:T(8,128)(2,1)S(1)}, bf16[2,256,128]{2,1,0:T(8,128)(2,1)S(1)}, u32[]{:S(2)}, u32[]{:S(2)}) collective-permute-start(bf16[2,256,128]{2,1,0:T(8,128)(2,1)S(1)} %get-tuple-element.14.rest_11_), channel_id=1, source_target_pairs={{6,0},{4,2},{7,1},{5,3},{22,16},{20,18},{23,17},{21,19},{38,32},{3... | collective-permute-start | bytes 393224 | tf_op jit(solution)/shard_map/ppermute | solution.py:132
  41.4 7.2 %collective-permute-done.14.rest_9_ = bf16[2,256,128]{2,1,0:T(8,128)(2,1)S(1)} collective-permute-done((bf16[2,256,128]{2,1,0:T(8,128)(2,1)S(1)}, bf16[2,256,128]{2,1,0:T(8,128)(2,1)S(1)}, u32[]{:S(2)}, u32[]{:S(2)}) %collective-permute-start.14) | collective-permute-done | bytes 131104 | tf_op jit(solution)/shard_map/ppermute | solution.py:132
  48.6 2.1 %shard_map.81 = bf16[2,256,128]{2,1,0:T(8,128)(2,1)S(1)} custom-call(s32[4]{0:T(128)S(1)} %pad_add_fusion.where_ref, bf16[2,2,256,256]{3,2,1,0:T(8,128)(2,1)S(1)} %shard_map.77.inv_ref, f32[256,256]{1,0:T(8,128)S(1)} %bitcast.27, f32[256,128]{1,0:T(8,128)S(1)} %collective-permute-done.mate_rhs_ref, bf16[4,256,256]{2,1,0:T(8,128)(2,1)S(1)} %fusion.1.own_ref.w_own_ref, ...), custom_call_target="tpu_custom_call" | custom-call | tf_op jit(solution)/shard_map/pallas_call | solution.py:117
  50.7 0.9 broadcast_in_dim.31
  51.6 7.6 %all-to-all-start = ((bf16[8,256,128]{2,1,0:T(8,128)(2,1)}), bf16[8,256,128]{2,1,0:T(8,128)(2,1)S(1)}, u32[]{:S(2)}, u32[]{:S(2)}) async-start(bf16[8,256,128]{2,1,0:T(8,128)(2,1)} %bitcast.7), calls=%async_computation | async-start | bytes 1048576 | tf_op jit(solution)/shard_map/all_to_all | solution.py:195
  59.2 0.1 copy.14
  59.3 0.1 collective-permute-start.15
  59.4 10.7 %all-to-all-done = bf16[8,256,128]{2,1,0:T(8,128)(2,1)S(1)} async-done(((bf16[8,256,128]{2,1,0:T(8,128)(2,1)}), bf16[8,256,128]{2,1,0:T(8,128)(2,1)S(1)}, u32[]{:S(2)}, u32[]{:S(2)}) %all-to-all-start) | async-done | bytes 524320 | tf_op jit(solution)/shard_map/all_to_all | solution.py:195
  70.1 0.0 collective-permute-done.15.z_other_ref
  70.1 0.2 broadcast_in_dim.32
  70.3 18.0 %all_to_all.10.x_ref = bf16[16,256,128]{2,1,0:T(8,128)(2,1)S(1)} all-to-all(bf16[16,256,128]{2,1,0:T(8,128)(2,1)S(1)} %broadcast_in_dim.32), channel_id=1, replica_groups=mesh['z'=4,'yh'=2,'yl'=2,'xp'=2,'xq'=2,'col'=2] {'yh','yl','xp','xq'}, dimensions={0} | all-to-all | bytes 2097152 | tf_op jit(solution)/shard_map/all_to_all | solution.py:201
  88.3 2.1 %shard_map.82 = (f32[256,256]{1,0:T(8,128)}, f32[256,256]{1,0:T(8,128)}) custom-call(s32[4]{0:T(128)S(1)} %pad_add_fusion.where_ref, bf16[16,256,128]{2,1,0:T(8,128)(2,1)S(1)} %all_to_all.10.x_ref, bf16[4,256,256]{2,1,0:T(8,128)(2,1)S(1)} %fusion.1.own_ref.w_own_ref, bf16[1,256,256]{2,1,0:T(8,128)(2,1)S(1)} %collective-permute-done.1.rest_0_.other3_ref, ...), custom_call_target="tpu_custom_call" | custom-call | tf_op jit(solution)/shard_map/pallas_call | solution.py:117
  (10 shorter events, 0.1 us)
Async XLA Ops:
  0.6 5.8 %copy-start = (f32[1,1,256,256]{3,2,1,0:T(8,128)S(1)}, f32[1,1,256,256]{3,2,1,0:T(8,128)}, u32[]{:S(2)}) copy-start(f32[1,1,256,256]{3,2,1,0:T(8,128)} %param.11) | copy-start | bytes 786436
  0.6 8.9 %copy-start.1 = (f32[4,2,256,256]{3,2,1,0:T(8,128)S(1)}, f32[4,2,256,256]{3,2,1,0:T(8,128)}, u32[]{:S(2)}) copy-start(f32[4,2,256,256]{3,2,1,0:T(8,128)} %inv_ref.1) | copy-start | bytes 6291460
  3.6 5.9 %collective-permute-start.2 = (bf16[1,256,256]{2,1,0:T(8,128)(2,1)}, bf16[1,256,256]{2,1,0:T(8,128)(2,1)S(1)}, u32[]{:S(2)}, u32[]{:S(2)}) collective-permute-start(bf16[1,256,256]{2,1,0:T(8,128)(2,1)} %get-tuple-element.21), channel_id=1, source_target_pairs={{0,2},{2,0},{1,3},{3,1},{4,6},{6,4},{5,7},{7,5},{8,10},{10,8},{9,1... | collective-permute-start | bytes 393224 | tf_op jit(solution)/shard_map/ppermute | solution.py:155
  5.9 16.0 %collective-permute-start.8 = (bf16[2,256,256]{2,1,0:T(8,128)(2,1)}, bf16[2,256,256]{2,1,0:T(8,128)(2,1)}, u32[]{:S(2)}, u32[]{:S(2)}) collective-permute-start(bf16[2,256,256]{2,1,0:T(8,128)(2,1)} %slice.30), channel_id=1, source_target_pairs={{0,2},{2,0},{1,3},{3,1},{4,6},{6,4},{5,7},{7,5},{8,10},{10,8},{9,1... | collective-permute-start | bytes 786440 | tf_op jit(solution)/shard_map/ppermute | solution.py:164
  6.5 11.7 %collective-permute-start = (f32[256,128]{1,0:T(8,128)S(1)}, f32[256,128]{1,0:T(8,128)S(1)}, u32[]{:S(2)}, u32[]{:S(2)}) collective-permute-start(f32[256,128]{1,0:T(8,128)S(1)} %slice_select_fusion), channel_id=1, source_target_pairs={{0,2},{2,0},{1,3},{3,1},{4,6},{6,4},{5,7},{7,5},{8,10},{10,8},{9,1... | collective-permute-start | bytes 393224 | tf_op jit(solution)/shard_map/ppermute | solution.py:157
  8.1 12.0 %collective-permute-start.5 = (bf16[1,256,256]{2,1,0:T(8,128)(2,1)S(1)}, bf16[1,256,256]{2,1,0:T(8,128)(2,1)S(1)}, u32[]{:S(2)}, u32[]{:S(2)}) collective-permute-start(bf16[1,256,256]{2,1,0:T(8,128)(2,1)S(1)} %get-tuple-element.20), channel_id=1, source_target_pairs={{0,2},{2,0},{1,3},{3,1},{4,6},{6,4},{5,7},{7,5},{8,10},{10,8},{9,1... | collective-permute-start | bytes 393224 | tf_op jit(solution)/shard_map/ppermute | solution.py:159
  8.6 11.6 %collective-permute-start.1 = (bf16[1,256,256]{2,1,0:T(8,128)(2,1)}, bf16[1,256,256]{2,1,0:T(8,128)(2,1)S(1)}, u32[]{:S(2)}, u32[]{:S(2)}) collective-permute-start(bf16[1,256,256]{2,1,0:T(8,128)(2,1)} %get-tuple-element.21), channel_id=1, source_target_pairs={{0,1},{1,0},{2,3},{3,2},{4,5},{5,4},{6,7},{7,6},{8,9},{9,8},{10,11... | collective-permute-start | bytes 393224 | tf_op jit(solution)/shard_map/ppermute | solution.py:156
  9.5 11.1 %collective-permute-start.3 = (bf16[1,256,256]{2,1,0:T(8,128)(2,1)S(1)}, bf16[1,256,256]{2,1,0:T(8,128)(2,1)S(1)}, u32[]{:S(2)}, u32[]{:S(2)}) collective-permute-start(bf16[1,256,256]{2,1,0:T(8,128)(2,1)S(1)} %collective-permute-done.2.rest_1_), channel_id=1, source_target_pairs={{0,1},{1,0},{2,3},{3,2},{4,5},{5,4},{6,7},{7,6},{8,9},{9,8},{10,11... | collective-permute-start | bytes 393224 | tf_op jit(solution)/shard_map/ppermute | solution.py:158
  18.1 3.9 %collective-permute-start.4 = (bf16[1,256,256]{2,1,0:T(8,128)(2,1)S(1)}, bf16[1,256,256]{2,1,0:T(8,128)(2,1)S(1)}, u32[]{:S(2)}, u32[]{:S(2)}) collective-permute-start(bf16[1,256,256]{2,1,0:T(8,128)(2,1)S(1)} %get-tuple-element.20), channel_id=1, source_target_pairs={{0,1},{1,0},{2,3},{3,2},{4,5},{5,4},{6,7},{7,6},{8,9},{9,8},{10,11... | collective-permute-start | bytes 393224 | tf_op jit(solution)/shard_map/ppermute | solution.py:160
  20.2 5.8 %collective-permute-start.7 = (bf16[2,256,256]{2,1,0:T(8,128)(2,1)}, bf16[2,256,256]{2,1,0:T(8,128)(2,1)S(1)}, u32[]{:S(2)}, u32[]{:S(2)}) collective-permute-start(bf16[2,256,256]{2,1,0:T(8,128)(2,1)} %slice.30), channel_id=1, source_target_pairs={{0,1},{1,0},{2,3},{3,2},{4,5},{5,4},{6,7},{7,6},{8,9},{9,8},{10,11... | collective-permute-start | bytes 786440 | tf_op jit(solution)/shard_map/ppermute | solution.py:165
  20.2 2.6 %collective-permute-start.6 = (bf16[1,256,256]{2,1,0:T(8,128)(2,1)S(1)}, bf16[1,256,256]{2,1,0:T(8,128)(2,1)S(1)}, u32[]{:S(2)}, u32[]{:S(2)}) collective-permute-start(bf16[1,256,256]{2,1,0:T(8,128)(2,1)S(1)} %collective-permute-done.5.rest_4_), channel_id=1, source_target_pairs={{0,1},{1,0},{2,3},{3,2},{4,5},{5,4},{6,7},{7,6},{8,9},{9,8},{10,11... | collective-permute-start | bytes 393224 | tf_op jit(solution)/shard_map/ppermute | solution.py:166
  21.3 1.5 %collective-permute-start.11 = (bf16[2,256,128]{2,1,0:T(8,128)(2,1)S(1)}, bf16[2,256,128]{2,1,0:T(8,128)(2,1)S(1)}, u32[]{:S(2)}, u32[]{:S(2)}) collective-permute-start(bf16[2,256,128]{2,1,0:T(8,128)(2,1)S(1)} %shard_map.78.rest_7_), channel_id=1, source_target_pairs={{14,8},{12,10},{15,9},{13,11},{30,24},{28,26},{31,25},{29,27},{46,... | collective-permute-start | bytes 393224 | tf_op jit(solution)/shard_map/ppermute | solution.py:132
  22.0 4.0 %collective-permute-start.9 = (bf16[2,256,256]{2,1,0:T(8,128)(2,1)}, bf16[2,256,256]{2,1,0:T(8,128)(2,1)S(1)}, u32[]{:S(2)}, u32[]{:S(2)}) collective-permute-start(bf16[2,256,256]{2,1,0:T(8,128)(2,1)} %collective-permute-done.8.rest_7_), channel_id=1, source_target_pairs={{0,1},{1,0},{2,3},{3,2},{4,5},{5,4},{6,7},{7,6},{8,9},{9,8},{10,11... | collective-permute-start | bytes 786440 | tf_op jit(solution)/shard_map/ppermute | solution.py:167
  22.1 3.9 %collective-permute-start.10 = (bf16[2,256,128]{2,1,0:T(8,128)(2,1)S(1)}, bf16[2,256,128]{2,1,0:T(8,128)(2,1)S(1)}, u32[]{:S(2)}, u32[]{:S(2)}) collective-permute-start(bf16[2,256,128]{2,1,0:T(8,128)(2,1)S(1)} %shard_map.78.rest_7_), channel_id=1, source_target_pairs={{14,6},{12,4},{15,7},{13,5},{30,22},{28,20},{31,23},{29,21},{46,38... | collective-permute-start | bytes 393224 | tf_op jit(solution)/shard_map/ppermute | solution.py:132
  23.3 15.4 %collective-permute-start.13 = (bf16[2,256,128]{2,1,0:T(8,128)(2,1)S(1)}, bf16[2,256,128]{2,1,0:T(8,128)(2,1)S(1)}, u32[]{:S(2)}, u32[]{:S(2)}) collective-permute-start(bf16[2,256,128]{2,1,0:T(8,128)(2,1)S(1)} %shard_map.79.rest_13_), channel_id=1, source_target_pairs={{8,0},{10,2},{9,1},{11,3},{24,16},{26,18},{25,17},{27,19},{40,32},... | collective-permute-start | bytes 393224 | tf_op jit(solution)/shard_map/ppermute | solution.py:132
  24.6 14.1 %collective-permute-start.12 = (bf16[2,256,128]{2,1,0:T(8,128)(2,1)S(1)}, bf16[2,256,128]{2,1,0:T(8,128)(2,1)S(1)}, u32[]{:S(2)}, u32[]{:S(2)}) collective-permute-start(bf16[2,256,128]{2,1,0:T(8,128)(2,1)S(1)} %shard_map.79.rest_13_), channel_id=1, source_target_pairs={{8,6},{10,4},{14,0},{12,2},{9,7},{11,5},{15,1},{13,3},{24,22},{26,... | collective-permute-start | bytes 393224 | tf_op jit(solution)/shard_map/ppermute | solution.py:132
  40.1 8.5 %collective-permute-start.14 = (bf16[2,256,128]{2,1,0:T(8,128)(2,1)S(1)}, bf16[2,256,128]{2,1,0:T(8,128)(2,1)S(1)}, u32[]{:S(2)}, u32[]{:S(2)}) collective-permute-start(bf16[2,256,128]{2,1,0:T(8,128)(2,1)S(1)} %get-tuple-element.14.rest_11_), channel_id=1, source_target_pairs={{6,0},{4,2},{7,1},{5,3},{22,16},{20,18},{23,17},{21,19},{38,32},{3... | collective-permute-start | bytes 393224 | tf_op jit(solution)/shard_map/ppermute | solution.py:132
  48.6 10.6 %copy-start.2 = (bf16[1,1,256,4,1,256]{5,3,4,2,1,0:T(4,128)(2,1)S(1)}, bf16[1,1,256,4,1,256]{5,3,4,2,1,0:T(4,128)(2,1)}, u32[]{:S(2)}) copy-start(bf16[1,1,256,4,1,256]{5,3,4,2,1,0:T(4,128)(2,1)} %param.8) | copy-start | bytes 1572868
  51.6 18.5 %all-to-all-start = ((bf16[8,256,128]{2,1,0:T(8,128)(2,1)}), bf16[8,256,128]{2,1,0:T(8,128)(2,1)S(1)}, u32[]{:S(2)}, u32[]{:S(2)}) async-start(bf16[8,256,128]{2,1,0:T(8,128)(2,1)} %bitcast.7), calls=%async_computation | async-start | bytes 1048576 | tf_op jit(solution)/shard_map/all_to_all | solution.py:195
  59.3 10.8 %collective-permute-start.15 = (bf16[4,256,256]{2,1,0:T(8,128)(2,1)S(1)}, bf16[4,256,256]{2,1,0:T(8,128)(2,1)S(1)}, u32[]{:S(2)}, u32[]{:S(2)}) collective-permute-start(bf16[4,256,256]{2,1,0:T(8,128)(2,1)S(1)} %bitcast.29), channel_id=1, source_target_pairs={{0,1},{1,0},{2,3},{3,2},{4,5},{5,4},{6,7},{7,6},{8,9},{9,8},{10,11... | collective-permute-start | bytes 1572872 | tf_op jit(solution)/shard_map/ppermute | solution.py:168

commit v10 on v8

--- a/solution.py
+++ b/solution.py
@@ -34,7 +34,8 @@
 
 def precise(inv_ref, e, b):
     high, low = halves(b)
-    return dot(inv_ref[e, 0], high) + (dot(inv_ref[e, 1], high) + dot(inv_ref[e, 0], low))
+    both = dot(inv_ref[e].reshape(2 * NB, NB), high)
+    return both[:NB] + (both[NB:] + dot(inv_ref[e, 0], low))
 
 
 def pair_kernel(
@@ -57,10 +58,10 @@
     def less(accs, b, x):
         own, other, mate, mate_other = blocks(b)
         mine, theirs = x[parity], x[1 - parity]
-        return (
-            accs[0] - (dot(own, mine) + dot(other, theirs)),
-            accs[1] - (dot(mate, mine) + dot(mate_other, theirs)),
+        step = dot(jnp.concatenate([own, mate], 0), mine) + dot(
+            jnp.concatenate([other, mate_other], 0), theirs
         )
+        return accs[0] - step[:NB], accs[1] - step[NB:]
 
     def fresh():
         return rhs_ref[:, pl.ds(pl.multiple_of(half * WIDE, WIDE), WIDE)], mate_rhs_ref[...]
@@ -187,13 +188,13 @@
         )
 
     x3 = solve(3, [], [], jnp.zeros(shape.shape, shape.dtype))
-    a = to_pairs(x3, [(3, 2), (1, 3)])
+    a = to_pairs(x3, [(3, 2)])
     b = to_pairs(x3, [(3, 1)])
     x2 = solve(2, [(3, a)], [], x3)
-    c = to_pairs(x2, [(2, 1), (3, 0), (0, 2), (1, 3)])
+    c = to_pairs(x2, [(2, 1), (3, 0)])
     d = to_pairs(x2, [(2, 0)])
     x1, acc = solve(1, [(3, b), (2, c)], [(3, c), (2, d)], x2)
-    e = to_pairs(x1, [(1, 0), (3, 1)])
+    e = to_pairs(x1, [(1, 0)])
     x0 = solve(0, [(1, e)], [], acc, x1)
 
     quarters = x0.reshape(DEPTH, 1, 2 * NB // DEPTH, WIDE)

time: 88.3 us -> 87.1 us (0.986)
  starting transfers between devices: 19.4 us -> 10.2 us
  waiting for transfers between devices: 23.7 us -> 31.4 us
    ppermute x5, starting transfers between devices: 14.5 us -> 5.35 us  [to_pairs(): return lax.ppermute(a, ('yl', 'xp', 'xq'), sends)]
    ppermute x5, waiting for transfers between devices: 12.1 us -> 19.9 us  [to_pairs(): return lax.ppermute(a, ('yl', 'xp', 'xq'), sends)]
where the time goes in v10:
time: 87.1 us; the launch traced here: 86.8 us
  blocking collectives  34.2 us (39%)
  waiting for transfers between devices  31.4 us (36%)
  starting transfers between devices  10.2 us (12%)
  Pallas kernels  6.52 us (7%)
  between operations  1.68 us (2%)
  other arithmetic  1.56 us (2%)
  local copies, waits for them, and re-layouts  1.11 us (1%)
    ppermute x5, waiting for transfers between devices, to_pairs(): return lax.ppermute(a, ('yl', 'xp', 'xq'), sends)  19.9 us
    all_to_all x1, blocking collectives, local(): lax.all_to_all(jnp.broadcast_to(spread[None], (count, *spread.shape)), PL...  18 us
    all_to_all x1, blocking collectives, local(): lax.all_to_all(quarters.reshape(2 * DEPTH, *quarters.shape[2:]), ('z', 'y...  16.2 us
    ppermute x1, waiting for transfers between devices, local(): lax.ppermute(jnp.where(lower_half, rhs[:, WIDE:], rhs[:, :WIDE]), 'xq', F...  7.79 us
    pallas_call x6, Pallas kernels, call(): pl.pallas_call(kernel, out_shape=outs, in_specs=[smem if a.dtype == jnp.i...  6.52 us
    ppermute x5, starting transfers between devices, to_pairs(): return lax.ppermute(a, ('yl', 'xp', 'xq'), sends)  5.35 us
    ppermute x1, waiting for transfers between devices, local(): mate3 = lax.ppermute(own3, 'xq', FLIP)  2.24 us
  transfers between devices with their start and end apart: 16, of which 5 were waited for; matrix products, arithmetic and copies ran while one was open for 0% of the time, Pallas kernels for 4%

profile of v10, /device:TPU:0, one launch (start us, length us, event | category | flops | bytes accessed | tf_op | source)
XLA Modules:
  0.0 86.8 jit_solution(9443175628858515259)
XLA Ops:
  0.6 0.0 copy-start
  0.6 0.0 copy-start.1
  1.5 1.5 %fusion.1.own_ref.w_own_ref = bf16[4,256,256]{2,1,0:T(8,128)(2,1)S(1)} fusion(bf16[1,1,256,4,1,256]{5,3,4,2,1,0:T(4,128)(2,1)} %param.7, bf16[1,1,256,4,1,256]{5,3,4,2,1,0:T(4,128)(2,1)} %param.6, f32[]{:T(128)S(6)} %copy.15, pred[4]{0:T(512)(128)(4,1)S(1)} %add_compare_fusion), kind=kLoop, calls=%fused_computation.2 | loop fusion | flops 1572864 | bytes 1572872 | tf_op jit(solution)/shard_map/transpose | solution.py:158
  2.9 0.7 fusion.2
  3.7 1.6 %collective-permute-start.2 = (bf16[1,256,256]{2,1,0:T(8,128)(2,1)}, bf16[1,256,256]{2,1,0:T(8,128)(2,1)S(1)}, u32[]{:S(2)}, u32[]{:S(2)}) collective-permute-start(bf16[1,256,256]{2,1,0:T(8,128)(2,1)} %get-tuple-element.21), channel_id=1, source_target_pairs={{0,2},{2,0},{1,3},{3,1},{4,6},{6,4},{5,7},{7,5},{8,10},{10,8},{9,1... | collective-permute-start | bytes 393224 | tf_op jit(solution)/shard_map/ppermute | solution.py:160
  5.3 0.5 collective-permute-start.8
  5.8 0.1 pad_add_fusion.where_ref
  5.9 1.7 %collective-permute-start = (f32[256,128]{1,0:T(8,128)S(1)}, f32[256,128]{1,0:T(8,128)S(1)}, u32[]{:S(2)}, u32[]{:S(2)}) collective-permute-start(f32[256,128]{1,0:T(8,128)S(1)} %slice_select_fusion), channel_id=1, source_target_pairs={{0,2},{2,0},{1,3},{3,1},{4,6},{6,4},{5,7},{7,5},{8,10},{10,8},{9,1... | collective-permute-start | bytes 393224 | tf_op jit(solution)/shard_map/ppermute | solution.py:162
  7.6 0.4 collective-permute-start.5
  8.0 0.0 collective-permute-start.1
  8.0 2.2 %collective-permute-done.2.rest_1_ = bf16[1,256,256]{2,1,0:T(8,128)(2,1)S(1)} collective-permute-done((bf16[1,256,256]{2,1,0:T(8,128)(2,1)}, bf16[1,256,256]{2,1,0:T(8,128)(2,1)S(1)}, u32[]{:S(2)}, u32[]{:S(2)}) %collective-permute-start.2) | collective-permute-done | bytes 131104 | tf_op jit(solution)/shard_map/ppermute | solution.py:160
  10.2 0.0 collective-permute-start.3
  10.2 0.6 shard_map.77.inv_ref
  10.9 7.8 %collective-permute-done.mate_rhs_ref = f32[256,128]{1,0:T(8,128)S(1)} collective-permute-done((f32[256,128]{1,0:T(8,128)S(1)}, f32[256,128]{1,0:T(8,128)S(1)}, u32[]{:S(2)}, u32[]{:S(2)}) %collective-permute-start) | collective-permute-done | bytes 131104 | tf_op jit(solution)/shard_map/ppermute | solution.py:162
  18.7 0.0 collective-permute-start.4
  18.7 1.5 %collective-permute-done.5.rest_4_ = bf16[1,256,256]{2,1,0:T(8,128)(2,1)S(1)} collective-permute-done((bf16[1,256,256]{2,1,0:T(8,128)(2,1)}, bf16[1,256,256]{2,1,0:T(8,128)(2,1)S(1)}, u32[]{:S(2)}, u32[]{:S(2)}) %collective-permute-start.5) | collective-permute-done | bytes 131104 | tf_op jit(solution)/shard_map/ppermute | solution.py:164
  20.2 0.0 collective-permute-start.7
  20.2 0.0 collective-permute-done.1.rest_0_.other3_ref
  20.2 0.5 collective-permute-start.6
  20.7 0.0 collective-permute-done.3.rest_2_
  20.7 0.6 shard_map.78.rest_7_
  21.3 0.7 collective-permute-start.11
  22.0 0.0 collective-permute-done.8.rest_7_
  22.0 0.1 collective-permute-start.9
  22.1 0.0 collective-permute-done.4.rest_3_.other2_ref
  22.1 0.7 collective-permute-start.10
  22.8 0.0 collective-permute-done.6.rest_5_
  22.8 0.0 collective-permute-done.11.rest_6_
  22.8 0.6 shard_map.79.rest_13_
  23.4 0.0 copy-start.2
  23.4 1.4 %collective-permute-start.13 = (bf16[2,256,128]{2,1,0:T(8,128)(2,1)S(1)}, bf16[2,256,128]{2,1,0:T(8,128)(2,1)S(1)}, u32[]{:S(2)}, u32[]{:S(2)}) collective-permute-start(bf16[2,256,128]{2,1,0:T(8,128)(2,1)S(1)} %shard_map.79.rest_13_), channel_id=1, source_target_pairs={{8,0},{10,2},{9,1},{11,3},{24,16},{26,18},{25,17},{27,19},{40,32},... | collective-permute-start | bytes 393224 | tf_op jit(solution)/shard_map/ppermute | solution.py:137
  24.8 1.3 %collective-permute-start.12 = (bf16[2,256,128]{2,1,0:T(8,128)(2,1)S(1)}, bf16[2,256,128]{2,1,0:T(8,128)(2,1)S(1)}, u32[]{:S(2)}, u32[]{:S(2)}) collective-permute-start(bf16[2,256,128]{2,1,0:T(8,128)(2,1)S(1)} %shard_map.79.rest_13_), channel_id=1, source_target_pairs={{8,6},{10,4},{14,0},{12,2},{9,7},{11,5},{15,1},{13,3},{24,22},{26,... | collective-permute-start | bytes 393224 | tf_op jit(solution)/shard_map/ppermute | solution.py:137
  26.1 0.0 collective-permute-done.7.rest_6_.other01_ref
  26.1 0.0 collective-permute-done.10.rest_9_
  26.1 0.0 collective-permute-done.9.rest_8_
  26.1 12.9 %collective-permute-done.13.rest_12_ = bf16[2,256,128]{2,1,0:T(8,128)(2,1)S(1)} collective-permute-done((bf16[2,256,128]{2,1,0:T(8,128)(2,1)S(1)}, bf16[2,256,128]{2,1,0:T(8,128)(2,1)S(1)}, u32[]{:S(2)}, u32[]{:S(2)}) %collective-permute-start.13) | collective-permute-done | bytes 131104 | tf_op jit(solution)/shard_map/ppermute | solution.py:137
  39.0 0.0 collective-permute-done.12.rest_10_.rest_11_
  39.0 1.0 %shard_map.80 = (bf16[2,256,128]{2,1,0:T(8,128)(2,1)S(1)}, f32[2,256,128]{2,1,0:T(8,128)S(1)}) custom-call(s32[4]{0:T(128)S(1)} %pad_add_fusion.where_ref, bf16[2,2,256,256]{3,2,1,0:T(8,128)(2,1)S(1)} %shard_map.77.inv_ref, f32[256,256]{1,0:T(8,128)S(1)} %bitcast.27, f32[256,128]{1,0:T(8,128)S(1)} %collective-permute-done.mate_rhs_ref, ...), custom_call_target="tpu_custom_call" | custom-call | tf_op jit(solution)/shard_map/pallas_call | solution.py:122
  40.0 1.3 %collective-permute-start.14 = (bf16[2,256,128]{2,1,0:T(8,128)(2,1)S(1)}, bf16[2,256,128]{2,1,0:T(8,128)(2,1)S(1)}, u32[]{:S(2)}, u32[]{:S(2)}) collective-permute-start(bf16[2,256,128]{2,1,0:T(8,128)(2,1)S(1)} %get-tuple-element.14.rest_11_), channel_id=1, source_target_pairs={{6,0},{4,2},{7,1},{5,3},{22,16},{20,18},{23,17},{21,19},{38,32},{3... | collective-permute-start | bytes 393224 | tf_op jit(solution)/shard_map/ppermute | solution.py:137
  41.3 0.1 copy.14
  41.4 0.1 collective-permute-start.15
  41.5 7.0 %collective-permute-done.14.rest_9_ = bf16[2,256,128]{2,1,0:T(8,128)(2,1)S(1)} collective-permute-done((bf16[2,256,128]{2,1,0:T(8,128)(2,1)S(1)}, bf16[2,256,128]{2,1,0:T(8,128)(2,1)S(1)}, u32[]{:S(2)}, u32[]{:S(2)}) %collective-permute-start.14) | collective-permute-done | bytes 131104 | tf_op jit(solution)/shard_map/ppermute | solution.py:137
  48.5 1.7 %shard_map.81 = bf16[2,256,128]{2,1,0:T(8,128)(2,1)S(1)} custom-call(s32[4]{0:T(128)S(1)} %pad_add_fusion.where_ref, bf16[2,2,256,256]{3,2,1,0:T(8,128)(2,1)S(1)} %shard_map.77.inv_ref, f32[256,256]{1,0:T(8,128)S(1)} %bitcast.28, f32[256,128]{1,0:T(8,128)S(1)} %collective-permute-done.mate_rhs_ref, bf16[4,256,256]{2,1,0:T(8,128)(2,1)S(1)} %fusion.1.own_ref.w_own_ref, ...), custom_call_target="tpu_custom_call" | custom-call | tf_op jit(solution)/shard_map/pallas_call | solution.py:122
  50.2 16.2 %all_to_all.10 = bf16[8,128,128]{2,1,0:T(8,128)(2,1)S(1)} all-to-all(bf16[8,128,128]{2,1,0:T(8,128)(2,1)S(1)} %bitcast.33), channel_id=1, replica_groups=mesh['z'=4,'yh'=2,'yl'=2,'xp'=2,'xq'=2,'col'=2] {'z','yh'}, dimensions={0} | all-to-all | bytes 524288 | tf_op jit(solution)/shard_map/all_to_all | solution.py:202
  66.5 0.0 collective-permute-done.15.z_other_ref
  66.5 0.2 broadcast_in_dim.34
  66.7 18.0 %all_to_all.11.x_ref = bf16[32,128,128]{2,1,0:T(8,128)(2,1)S(1)} all-to-all(bf16[32,128,128]{2,1,0:T(8,128)(2,1)S(1)} %broadcast_in_dim.34), channel_id=1, replica_groups=mesh['z'=4,'yh'=2,'yl'=2,'xp'=2,'xq'=2,'col'=2] {'z','yl','xp','xq'}, dimensions={0} | all-to-all | bytes 2097152 | tf_op jit(solution)/shard_map/all_to_all | solution.py:207
  84.7 2.1 %shard_map.82 = (f32[256,256]{1,0:T(8,128)}, f32[256,256]{1,0:T(8,128)}) custom-call(s32[4]{0:T(128)S(1)} %pad_add_fusion.where_ref, bf16[32,128,128]{2,1,0:T(8,128)(2,1)S(1)} %all_to_all.11.x_ref, bf16[4,256,256]{2,1,0:T(8,128)(2,1)S(1)} %fusion.1.own_ref.w_own_ref, bf16[1,256,256]{2,1,0:T(8,128)(2,1)S(1)} %collective-permute-done.1.rest_0_.other3_ref, ...), custom_call_target="tpu_custom_call" | custom-call | tf_op jit(solution)/shard_map/pallas_call | solution.py:122
  (11 shorter events, 0.1 us)
Async XLA Ops:
  0.6 5.2 %copy-start = (f32[1,1,256,256]{3,2,1,0:T(8,128)S(1)}, f32[1,1,256,256]{3,2,1,0:T(8,128)}, u32[]{:S(2)}) copy-start(f32[1,1,256,256]{3,2,1,0:T(8,128)} %param.11) | copy-start | bytes 786436
  0.6 9.6 %copy-start.1 = (f32[4,2,256,256]{3,2,1,0:T(8,128)S(1)}, f32[4,2,256,256]{3,2,1,0:T(8,128)}, u32[]{:S(2)}) copy-start(f32[4,2,256,256]{3,2,1,0:T(8,128)} %inv_ref.1) | copy-start | bytes 6291460
  3.7 6.6 %collective-permute-start.2 = (bf16[1,256,256]{2,1,0:T(8,128)(2,1)}, bf16[1,256,256]{2,1,0:T(8,128)(2,1)S(1)}, u32[]{:S(2)}, u32[]{:S(2)}) collective-permute-start(bf16[1,256,256]{2,1,0:T(8,128)(2,1)} %get-tuple-element.21), channel_id=1, source_target_pairs={{0,2},{2,0},{1,3},{3,1},{4,6},{6,4},{5,7},{7,5},{8,10},{10,8},{9,1... | collective-permute-start | bytes 393224 | tf_op jit(solution)/shard_map/ppermute | solution.py:160
  5.3 16.7 %collective-permute-start.8 = (bf16[2,256,256]{2,1,0:T(8,128)(2,1)S(1)}, bf16[2,256,256]{2,1,0:T(8,128)(2,1)S(1)}, u32[]{:S(2)}, u32[]{:S(2)}) collective-permute-start(bf16[2,256,256]{2,1,0:T(8,128)(2,1)S(1)} %slice.30), channel_id=1, source_target_pairs={{0,2},{2,0},{1,3},{3,1},{4,6},{6,4},{5,7},{7,5},{8,10},{10,8},{9,1... | collective-permute-start | bytes 786440 | tf_op jit(solution)/shard_map/ppermute | solution.py:169
  5.8 12.9 %copy-start.3 = (bf16[1,256,256]{2,1,0:T(8,128)(2,1)S(1)}, bf16[1,256,256]{2,1,0:T(8,128)(2,1)}, u32[]{:S(2)}) copy-start(bf16[1,256,256]{2,1,0:T(8,128)(2,1)} %get-tuple-element.20) | copy-start | bytes 393220
  5.9 12.8 %collective-permute-start = (f32[256,128]{1,0:T(8,128)S(1)}, f32[256,128]{1,0:T(8,128)S(1)}, u32[]{:S(2)}, u32[]{:S(2)}) collective-permute-start(f32[256,128]{1,0:T(8,128)S(1)} %slice_select_fusion), channel_id=1, source_target_pairs={{0,2},{2,0},{1,3},{3,1},{4,6},{6,4},{5,7},{7,5},{8,10},{10,8},{9,1... | collective-permute-start | bytes 393224 | tf_op jit(solution)/shard_map/ppermute | solution.py:162
  7.6 12.6 %collective-permute-start.5 = (bf16[1,256,256]{2,1,0:T(8,128)(2,1)}, bf16[1,256,256]{2,1,0:T(8,128)(2,1)S(1)}, u32[]{:S(2)}, u32[]{:S(2)}) collective-permute-start(bf16[1,256,256]{2,1,0:T(8,128)(2,1)} %get-tuple-element.20), channel_id=1, source_target_pairs={{0,2},{2,0},{1,3},{3,1},{4,6},{6,4},{5,7},{7,5},{8,10},{10,8},{9,1... | collective-permute-start | bytes 393224 | tf_op jit(solution)/shard_map/ppermute | solution.py:164
  8.0 12.2 %collective-permute-start.1 = (bf16[1,256,256]{2,1,0:T(8,128)(2,1)}, bf16[1,256,256]{2,1,0:T(8,128)(2,1)S(1)}, u32[]{:S(2)}, u32[]{:S(2)}) collective-permute-start(bf16[1,256,256]{2,1,0:T(8,128)(2,1)} %get-tuple-element.21), channel_id=1, source_target_pairs={{0,1},{1,0},{2,3},{3,2},{4,5},{5,4},{6,7},{7,6},{8,9},{9,8},{10,11... | collective-permute-start | bytes 393224 | tf_op jit(solution)/shard_map/ppermute | solution.py:161
  10.2 10.5 %collective-permute-start.3 = (bf16[1,256,256]{2,1,0:T(8,128)(2,1)S(1)}, bf16[1,256,256]{2,1,0:T(8,128)(2,1)S(1)}, u32[]{:S(2)}, u32[]{:S(2)}) collective-permute-start(bf16[1,256,256]{2,1,0:T(8,128)(2,1)S(1)} %collective-permute-done.2.rest_1_), channel_id=1, source_target_pairs={{0,1},{1,0},{2,3},{3,2},{4,5},{5,4},{6,7},{7,6},{8,9},{9,8},{10,11... | collective-permute-start | bytes 393224 | tf_op jit(solution)/shard_map/ppermute | solution.py:163
  18.7 3.4 %collective-permute-start.4 = (bf16[1,256,256]{2,1,0:T(8,128)(2,1)S(1)}, bf16[1,256,256]{2,1,0:T(8,128)(2,1)S(1)}, u32[]{:S(2)}, u32[]{:S(2)}) collective-permute-start(bf16[1,256,256]{2,1,0:T(8,128)(2,1)S(1)} %copy-done.3), channel_id=1, source_target_pairs={{0,1},{1,0},{2,3},{3,2},{4,5},{5,4},{6,7},{7,6},{8,9},{9,8},{10,11... | collective-permute-start | bytes 393224 | tf_op jit(solution)/shard_map/ppermute | solution.py:165
  20.2 5.9 %collective-permute-start.7 = (bf16[2,256,256]{2,1,0:T(8,128)(2,1)S(1)}, bf16[2,256,256]{2,1,0:T(8,128)(2,1)S(1)}, u32[]{:S(2)}, u32[]{:S(2)}) collective-permute-start(bf16[2,256,256]{2,1,0:T(8,128)(2,1)S(1)} %slice.30), channel_id=1, source_target_pairs={{0,1},{1,0},{2,3},{3,2},{4,5},{5,4},{6,7},{7,6},{8,9},{9,8},{10,11... | collective-permute-start | bytes 786440 | tf_op jit(solution)/shard_map/ppermute | solution.py:170
  20.2 2.6 %collective-permute-start.6 = (bf16[1,256,256]{2,1,0:T(8,128)(2,1)S(1)}, bf16[1,256,256]{2,1,0:T(8,128)(2,1)S(1)}, u32[]{:S(2)}, u32[]{:S(2)}) collective-permute-start(bf16[1,256,256]{2,1,0:T(8,128)(2,1)S(1)} %collective-permute-done.5.rest_4_), channel_id=1, source_target_pairs={{0,1},{1,0},{2,3},{3,2},{4,5},{5,4},{6,7},{7,6},{8,9},{9,8},{10,11... | collective-permute-start | bytes 393224 | tf_op jit(solution)/shard_map/ppermute | solution.py:171
  21.3 1.5 %collective-permute-start.11 = (bf16[2,256,128]{2,1,0:T(8,128)(2,1)S(1)}, bf16[2,256,128]{2,1,0:T(8,128)(2,1)S(1)}, u32[]{:S(2)}, u32[]{:S(2)}) collective-permute-start(bf16[2,256,128]{2,1,0:T(8,128)(2,1)S(1)} %shard_map.78.rest_7_), channel_id=1, source_target_pairs={{14,8},{12,10},{15,9},{13,11},{30,24},{28,26},{31,25},{29,27},{46,... | collective-permute-start | bytes 393224 | tf_op jit(solution)/shard_map/ppermute | solution.py:137
  22.0 4.1 %collective-permute-start.9 = (bf16[2,256,256]{2,1,0:T(8,128)(2,1)S(1)}, bf16[2,256,256]{2,1,0:T(8,128)(2,1)S(1)}, u32[]{:S(2)}, u32[]{:S(2)}) collective-permute-start(bf16[2,256,256]{2,1,0:T(8,128)(2,1)S(1)} %collective-permute-done.8.rest_7_), channel_id=1, source_target_pairs={{0,1},{1,0},{2,3},{3,2},{4,5},{5,4},{6,7},{7,6},{8,9},{9,8},{10,11... | collective-permute-start | bytes 786440 | tf_op jit(solution)/shard_map/ppermute | solution.py:172
  22.1 4.0 %collective-permute-start.10 = (bf16[2,256,128]{2,1,0:T(8,128)(2,1)S(1)}, bf16[2,256,128]{2,1,0:T(8,128)(2,1)S(1)}, u32[]{:S(2)}, u32[]{:S(2)}) collective-permute-start(bf16[2,256,128]{2,1,0:T(8,128)(2,1)S(1)} %shard_map.78.rest_7_), channel_id=1, source_target_pairs={{14,6},{12,4},{15,7},{13,5},{30,22},{28,20},{31,23},{29,21},{46,38... | collective-permute-start | bytes 393224 | tf_op jit(solution)/shard_map/ppermute | solution.py:137
  23.4 17.9 %copy-start.2 = (bf16[1,1,256,4,1,256]{5,3,4,2,1,0:T(4,128)(2,1)S(1)}, bf16[1,1,256,4,1,256]{5,3,4,2,1,0:T(4,128)(2,1)}, u32[]{:S(2)}) copy-start(bf16[1,1,256,4,1,256]{5,3,4,2,1,0:T(4,128)(2,1)} %param.8) | copy-start | bytes 1572868
  23.4 15.6 %collective-permute-start.13 = (bf16[2,256,128]{2,1,0:T(8,128)(2,1)S(1)}, bf16[2,256,128]{2,1,0:T(8,128)(2,1)S(1)}, u32[]{:S(2)}, u32[]{:S(2)}) collective-permute-start(bf16[2,256,128]{2,1,0:T(8,128)(2,1)S(1)} %shard_map.79.rest_13_), channel_id=1, source_target_pairs={{8,0},{10,2},{9,1},{11,3},{24,16},{26,18},{25,17},{27,19},{40,32},... | collective-permute-start | bytes 393224 | tf_op jit(solution)/shard_map/ppermute | solution.py:137
  24.8 14.2 %collective-permute-start.12 = (bf16[2,256,128]{2,1,0:T(8,128)(2,1)S(1)}, bf16[2,256,128]{2,1,0:T(8,128)(2,1)S(1)}, u32[]{:S(2)}, u32[]{:S(2)}) collective-permute-start(bf16[2,256,128]{2,1,0:T(8,128)(2,1)S(1)} %shard_map.79.rest_13_), channel_id=1, source_target_pairs={{8,6},{10,4},{14,0},{12,2},{9,7},{11,5},{15,1},{13,3},{24,22},{26,... | collective-permute-start | bytes 393224 | tf_op jit(solution)/shard_map/ppermute | solution.py:137
  40.0 8.5 %collective-permute-start.14 = (bf16[2,256,128]{2,1,0:T(8,128)(2,1)S(1)}, bf16[2,256,128]{2,1,0:T(8,128)(2,1)S(1)}, u32[]{:S(2)}, u32[]{:S(2)}) collective-permute-start(bf16[2,256,128]{2,1,0:T(8,128)(2,1)S(1)} %get-tuple-element.14.rest_11_), channel_id=1, source_target_pairs={{6,0},{4,2},{7,1},{5,3},{22,16},{20,18},{23,17},{21,19},{38,32},{3... | collective-permute-start | bytes 393224 | tf_op jit(solution)/shard_map/ppermute | solution.py:137
  41.4 25.1 %collective-permute-start.15 = (bf16[4,256,256]{2,1,0:T(8,128)(2,1)S(1)}, bf16[4,256,256]{2,1,0:T(8,128)(2,1)S(1)}, u32[]{:S(2)}, u32[]{:S(2)}) collective-permute-start(bf16[4,256,256]{2,1,0:T(8,128)(2,1)S(1)} %bitcast.30), channel_id=1, source_target_pairs={{0,1},{1,0},{2,3},{3,2},{4,5},{5,4},{6,7},{7,6},{8,9},{9,8},{10,11... | collective-permute-start | bytes 1572872 | tf_op jit(solution)/shard_map/ppermute | solution.py:173

commit v11 on v8

--- a/solution.py
+++ b/solution.py
@@ -187,13 +187,13 @@
         )
 
     x3 = solve(3, [], [], jnp.zeros(shape.shape, shape.dtype))
-    a = to_pairs(x3, [(3, 2), (1, 3)])
+    a = to_pairs(x3, [(3, 2)])
     b = to_pairs(x3, [(3, 1)])
     x2 = solve(2, [(3, a)], [], x3)
-    c = to_pairs(x2, [(2, 1), (3, 0), (0, 2), (1, 3)])
+    c = to_pairs(x2, [(2, 1), (3, 0)])
     d = to_pairs(x2, [(2, 0)])
     x1, acc = solve(1, [(3, b), (2, c)], [(3, c), (2, d)], x2)
-    e = to_pairs(x1, [(1, 0), (3, 1)])
+    e = to_pairs(x1, [(1, 0)])
     x0 = solve(0, [(1, e)], [], acc, x1)
 
     quarters = x0.reshape(DEPTH, 1, 2 * NB // DEPTH, WIDE)

time: 88.3 us -> 86.8 us (0.983)
  starting transfers between devices: 19.4 us -> 10.2 us
  waiting for transfers between devices: 23.7 us -> 31.4 us
    ppermute x5, starting transfers between devices: 14.5 us -> 5.35 us  [to_pairs(): return lax.ppermute(a, ('yl', 'xp', 'xq'), sends)]
    ppermute x5, waiting for transfers between devices: 12.1 us -> 19.8 us  [to_pairs(): return lax.ppermute(a, ('yl', 'xp', 'xq'), sends)]
where the time goes in v11:
time: 86.8 us; the launch traced here: 86.6 us
  blocking collectives  34.2 us (39%)
  waiting for transfers between devices  31.4 us (36%)
  starting transfers between devices  10.2 us (12%)
  Pallas kernels  6.39 us (7%)
  between operations  1.68 us (2%)
  other arithmetic  1.56 us (2%)
  local copies, waits for them, and re-layouts  1.11 us (1%)
    ppermute x5, waiting for transfers between devices, to_pairs(): return lax.ppermute(a, ('yl', 'xp', 'xq'), sends)  19.8 us
    all_to_all x1, blocking collectives, local(): lax.all_to_all(jnp.broadcast_to(spread[None], (count, *spread.shape)), PL...  18 us
    all_to_all x1, blocking collectives, local(): lax.all_to_all(quarters.reshape(2 * DEPTH, *quarters.shape[2:]), ('z', 'y...  16.2 us
    ppermute x1, waiting for transfers between devices, local(): lax.ppermute(jnp.where(lower_half, rhs[:, WIDE:], rhs[:, :WIDE]), 'xq', F...  7.79 us
    pallas_call x6, Pallas kernels, call(): pl.pallas_call(kernel, out_shape=outs, in_specs=[smem if a.dtype == jnp.i...  6.39 us
    ppermute x5, starting transfers between devices, to_pairs(): return lax.ppermute(a, ('yl', 'xp', 'xq'), sends)  5.35 us
    ppermute x1, waiting for transfers between devices, local(): mate3 = lax.ppermute(own3, 'xq', FLIP)  2.24 us
  transfers between devices with their start and end apart: 16, of which 5 were waited for; matrix products, arithmetic and copies ran while one was open for 0% of the time, Pallas kernels for 4%

profile of v11, /device:TPU:0, one launch (start us, length us, event | category | flops | bytes accessed | tf_op | source)
XLA Modules:
  0.0 86.6 jit_solution(14338196625713786281)
XLA Ops:
  0.6 0.0 copy-start
  0.6 0.0 copy-start.1
  1.5 1.5 %fusion.1.own_ref.w_own_ref = bf16[4,256,256]{2,1,0:T(8,128)(2,1)S(1)} fusion(bf16[1,1,256,4,1,256]{5,3,4,2,1,0:T(4,128)(2,1)} %param.7, bf16[1,1,256,4,1,256]{5,3,4,2,1,0:T(4,128)(2,1)} %param.6, f32[]{:T(128)S(6)} %copy.15, pred[4]{0:T(512)(128)(4,1)S(1)} %add_compare_fusion), kind=kLoop, calls=%fused_computation.2 | loop fusion | flops 1572864 | bytes 1572872 | tf_op jit(solution)/shard_map/transpose | solution.py:157
  2.9 0.7 fusion.2
  3.7 1.6 %collective-permute-start.2 = (bf16[1,256,256]{2,1,0:T(8,128)(2,1)}, bf16[1,256,256]{2,1,0:T(8,128)(2,1)S(1)}, u32[]{:S(2)}, u32[]{:S(2)}) collective-permute-start(bf16[1,256,256]{2,1,0:T(8,128)(2,1)} %get-tuple-element.21), channel_id=1, source_target_pairs={{0,2},{2,0},{1,3},{3,1},{4,6},{6,4},{5,7},{7,5},{8,10},{10,8},{9,1... | collective-permute-start | bytes 393224 | tf_op jit(solution)/shard_map/ppermute | solution.py:159
  5.3 0.5 collective-permute-start.8
  5.8 0.1 pad_add_fusion.where_ref
  5.9 1.7 %collective-permute-start = (f32[256,128]{1,0:T(8,128)S(1)}, f32[256,128]{1,0:T(8,128)S(1)}, u32[]{:S(2)}, u32[]{:S(2)}) collective-permute-start(f32[256,128]{1,0:T(8,128)S(1)} %slice_select_fusion), channel_id=1, source_target_pairs={{0,2},{2,0},{1,3},{3,1},{4,6},{6,4},{5,7},{7,5},{8,10},{10,8},{9,1... | collective-permute-start | bytes 393224 | tf_op jit(solution)/shard_map/ppermute | solution.py:161
  7.6 0.4 collective-permute-start.5
  8.0 0.0 collective-permute-start.1
  8.0 2.2 %collective-permute-done.2.rest_1_ = bf16[1,256,256]{2,1,0:T(8,128)(2,1)S(1)} collective-permute-done((bf16[1,256,256]{2,1,0:T(8,128)(2,1)}, bf16[1,256,256]{2,1,0:T(8,128)(2,1)S(1)}, u32[]{:S(2)}, u32[]{:S(2)}) %collective-permute-start.2) | collective-permute-done | bytes 131104 | tf_op jit(solution)/shard_map/ppermute | solution.py:159
  10.2 0.0 collective-permute-start.3
  10.2 0.6 shard_map.77.inv_ref
  10.9 7.8 %collective-permute-done.mate_rhs_ref = f32[256,128]{1,0:T(8,128)S(1)} collective-permute-done((f32[256,128]{1,0:T(8,128)S(1)}, f32[256,128]{1,0:T(8,128)S(1)}, u32[]{:S(2)}, u32[]{:S(2)}) %collective-permute-start) | collective-permute-done | bytes 131104 | tf_op jit(solution)/shard_map/ppermute | solution.py:161
  18.7 0.0 collective-permute-start.4
  18.7 1.5 %collective-permute-done.5.rest_4_ = bf16[1,256,256]{2,1,0:T(8,128)(2,1)S(1)} collective-permute-done((bf16[1,256,256]{2,1,0:T(8,128)(2,1)}, bf16[1,256,256]{2,1,0:T(8,128)(2,1)S(1)}, u32[]{:S(2)}, u32[]{:S(2)}) %collective-permute-start.5) | collective-permute-done | bytes 131104 | tf_op jit(solution)/shard_map/ppermute | solution.py:163
  20.2 0.0 collective-permute-start.7
  20.2 0.0 collective-permute-done.1.rest_0_.other3_ref
  20.2 0.5 collective-permute-start.6
  20.7 0.0 collective-permute-done.3.rest_2_
  20.7 0.6 shard_map.78.rest_7_
  21.3 0.7 collective-permute-start.11
  22.0 0.0 collective-permute-done.8.rest_7_
  22.0 0.1 collective-permute-start.9
  22.1 0.0 collective-permute-done.4.rest_3_.other2_ref
  22.1 0.7 collective-permute-start.10
  22.8 0.0 collective-permute-done.6.rest_5_
  22.8 0.0 collective-permute-done.11.rest_6_
  22.8 0.6 shard_map.79.rest_13_
  23.4 0.0 copy-start.2
  23.4 1.4 %collective-permute-start.13 = (bf16[2,256,128]{2,1,0:T(8,128)(2,1)S(1)}, bf16[2,256,128]{2,1,0:T(8,128)(2,1)S(1)}, u32[]{:S(2)}, u32[]{:S(2)}) collective-permute-start(bf16[2,256,128]{2,1,0:T(8,128)(2,1)S(1)} %shard_map.79.rest_13_), channel_id=1, source_target_pairs={{8,0},{10,2},{9,1},{11,3},{24,16},{26,18},{25,17},{27,19},{40,32},... | collective-permute-start | bytes 393224 | tf_op jit(solution)/shard_map/ppermute | solution.py:136
  24.8 1.3 %collective-permute-start.12 = (bf16[2,256,128]{2,1,0:T(8,128)(2,1)S(1)}, bf16[2,256,128]{2,1,0:T(8,128)(2,1)S(1)}, u32[]{:S(2)}, u32[]{:S(2)}) collective-permute-start(bf16[2,256,128]{2,1,0:T(8,128)(2,1)S(1)} %shard_map.79.rest_13_), channel_id=1, source_target_pairs={{8,6},{10,4},{14,0},{12,2},{9,7},{11,5},{15,1},{13,3},{24,22},{26,... | collective-permute-start | bytes 393224 | tf_op jit(solution)/shard_map/ppermute | solution.py:136
  26.1 0.0 collective-permute-done.7.rest_6_.other01_ref
  26.1 0.0 collective-permute-done.10.rest_9_
  26.1 0.0 collective-permute-done.9.rest_8_
  26.1 12.8 %collective-permute-done.13.rest_12_ = bf16[2,256,128]{2,1,0:T(8,128)(2,1)S(1)} collective-permute-done((bf16[2,256,128]{2,1,0:T(8,128)(2,1)S(1)}, bf16[2,256,128]{2,1,0:T(8,128)(2,1)S(1)}, u32[]{:S(2)}, u32[]{:S(2)}) %collective-permute-start.13) | collective-permute-done | bytes 131104 | tf_op jit(solution)/shard_map/ppermute | solution.py:136
  38.9 0.0 collective-permute-done.12.rest_10_.rest_11_
  38.9 1.0 %shard_map.80 = (bf16[2,256,128]{2,1,0:T(8,128)(2,1)S(1)}, f32[2,256,128]{2,1,0:T(8,128)S(1)}) custom-call(s32[4]{0:T(128)S(1)} %pad_add_fusion.where_ref, bf16[2,2,256,256]{3,2,1,0:T(8,128)(2,1)S(1)} %shard_map.77.inv_ref, f32[256,256]{1,0:T(8,128)S(1)} %bitcast.27, f32[256,128]{1,0:T(8,128)S(1)} %collective-permute-done.mate_rhs_ref, ...), custom_call_target="tpu_custom_call" | custom-call | tf_op jit(solution)/shard_map/pallas_call | solution.py:121
  39.9 1.3 %collective-permute-start.14 = (bf16[2,256,128]{2,1,0:T(8,128)(2,1)S(1)}, bf16[2,256,128]{2,1,0:T(8,128)(2,1)S(1)}, u32[]{:S(2)}, u32[]{:S(2)}) collective-permute-start(bf16[2,256,128]{2,1,0:T(8,128)(2,1)S(1)} %get-tuple-element.14.rest_11_), channel_id=1, source_target_pairs={{6,0},{4,2},{7,1},{5,3},{22,16},{20,18},{23,17},{21,19},{38,32},{3... | collective-permute-start | bytes 393224 | tf_op jit(solution)/shard_map/ppermute | solution.py:136
  41.2 0.1 copy.14
  41.3 0.1 collective-permute-start.15
  41.4 7.0 %collective-permute-done.14.rest_9_ = bf16[2,256,128]{2,1,0:T(8,128)(2,1)S(1)} collective-permute-done((bf16[2,256,128]{2,1,0:T(8,128)(2,1)S(1)}, bf16[2,256,128]{2,1,0:T(8,128)(2,1)S(1)}, u32[]{:S(2)}, u32[]{:S(2)}) %collective-permute-start.14) | collective-permute-done | bytes 131104 | tf_op jit(solution)/shard_map/ppermute | solution.py:136
  48.4 1.6 %shard_map.81 = bf16[2,256,128]{2,1,0:T(8,128)(2,1)S(1)} custom-call(s32[4]{0:T(128)S(1)} %pad_add_fusion.where_ref, bf16[2,2,256,256]{3,2,1,0:T(8,128)(2,1)S(1)} %shard_map.77.inv_ref, f32[256,256]{1,0:T(8,128)S(1)} %bitcast.28, f32[256,128]{1,0:T(8,128)S(1)} %collective-permute-done.mate_rhs_ref, bf16[4,256,256]{2,1,0:T(8,128)(2,1)S(1)} %fusion.1.own_ref.w_own_ref, ...), custom_call_target="tpu_custom_call" | custom-call | tf_op jit(solution)/shard_map/pallas_call | solution.py:121
  50.0 16.2 %all_to_all.10 = bf16[8,128,128]{2,1,0:T(8,128)(2,1)S(1)} all-to-all(bf16[8,128,128]{2,1,0:T(8,128)(2,1)S(1)} %bitcast.33), channel_id=1, replica_groups=mesh['z'=4,'yh'=2,'yl'=2,'xp'=2,'xq'=2,'col'=2] {'z','yh'}, dimensions={0} | all-to-all | bytes 524288 | tf_op jit(solution)/shard_map/all_to_all | solution.py:201
  66.3 0.0 collective-permute-done.15.z_other_ref
  66.3 0.2 broadcast_in_dim.34
  66.5 18.0 %all_to_all.11.x_ref = bf16[32,128,128]{2,1,0:T(8,128)(2,1)S(1)} all-to-all(bf16[32,128,128]{2,1,0:T(8,128)(2,1)S(1)} %broadcast_in_dim.34), channel_id=1, replica_groups=mesh['z'=4,'yh'=2,'yl'=2,'xp'=2,'xq'=2,'col'=2] {'z','yl','xp','xq'}, dimensions={0} | all-to-all | bytes 2097152 | tf_op jit(solution)/shard_map/all_to_all | solution.py:206
  84.5 2.1 %shard_map.82 = (f32[256,256]{1,0:T(8,128)}, f32[256,256]{1,0:T(8,128)}) custom-call(s32[4]{0:T(128)S(1)} %pad_add_fusion.where_ref, bf16[32,128,128]{2,1,0:T(8,128)(2,1)S(1)} %all_to_all.11.x_ref, bf16[4,256,256]{2,1,0:T(8,128)(2,1)S(1)} %fusion.1.own_ref.w_own_ref, bf16[1,256,256]{2,1,0:T(8,128)(2,1)S(1)} %collective-permute-done.1.rest_0_.other3_ref, ...), custom_call_target="tpu_custom_call" | custom-call | tf_op jit(solution)/shard_map/pallas_call | solution.py:121
  (11 shorter events, 0.1 us)
Async XLA Ops:
  0.6 5.2 %copy-start = (f32[1,1,256,256]{3,2,1,0:T(8,128)S(1)}, f32[1,1,256,256]{3,2,1,0:T(8,128)}, u32[]{:S(2)}) copy-start(f32[1,1,256,256]{3,2,1,0:T(8,128)} %param.11) | copy-start | bytes 786436
  0.6 9.6 %copy-start.1 = (f32[4,2,256,256]{3,2,1,0:T(8,128)S(1)}, f32[4,2,256,256]{3,2,1,0:T(8,128)}, u32[]{:S(2)}) copy-start(f32[4,2,256,256]{3,2,1,0:T(8,128)} %inv_ref.1) | copy-start | bytes 6291460
  3.7 6.6 %collective-permute-start.2 = (bf16[1,256,256]{2,1,0:T(8,128)(2,1)}, bf16[1,256,256]{2,1,0:T(8,128)(2,1)S(1)}, u32[]{:S(2)}, u32[]{:S(2)}) collective-permute-start(bf16[1,256,256]{2,1,0:T(8,128)(2,1)} %get-tuple-element.21), channel_id=1, source_target_pairs={{0,2},{2,0},{1,3},{3,1},{4,6},{6,4},{5,7},{7,5},{8,10},{10,8},{9,1... | collective-permute-start | bytes 393224 | tf_op jit(solution)/shard_map/ppermute | solution.py:159
  5.3 16.7 %collective-permute-start.8 = (bf16[2,256,256]{2,1,0:T(8,128)(2,1)S(1)}, bf16[2,256,256]{2,1,0:T(8,128)(2,1)S(1)}, u32[]{:S(2)}, u32[]{:S(2)}) collective-permute-start(bf16[2,256,256]{2,1,0:T(8,128)(2,1)S(1)} %slice.30), channel_id=1, source_target_pairs={{0,2},{2,0},{1,3},{3,1},{4,6},{6,4},{5,7},{7,5},{8,10},{10,8},{9,1... | collective-permute-start | bytes 786440 | tf_op jit(solution)/shard_map/ppermute | solution.py:168
  5.8 12.9 %copy-start.3 = (bf16[1,256,256]{2,1,0:T(8,128)(2,1)S(1)}, bf16[1,256,256]{2,1,0:T(8,128)(2,1)}, u32[]{:S(2)}) copy-start(bf16[1,256,256]{2,1,0:T(8,128)(2,1)} %get-tuple-element.20) | copy-start | bytes 393220
  5.9 12.8 %collective-permute-start = (f32[256,128]{1,0:T(8,128)S(1)}, f32[256,128]{1,0:T(8,128)S(1)}, u32[]{:S(2)}, u32[]{:S(2)}) collective-permute-start(f32[256,128]{1,0:T(8,128)S(1)} %slice_select_fusion), channel_id=1, source_target_pairs={{0,2},{2,0},{1,3},{3,1},{4,6},{6,4},{5,7},{7,5},{8,10},{10,8},{9,1... | collective-permute-start | bytes 393224 | tf_op jit(solution)/shard_map/ppermute | solution.py:161
  7.6 12.6 %collective-permute-start.5 = (bf16[1,256,256]{2,1,0:T(8,128)(2,1)}, bf16[1,256,256]{2,1,0:T(8,128)(2,1)S(1)}, u32[]{:S(2)}, u32[]{:S(2)}) collective-permute-start(bf16[1,256,256]{2,1,0:T(8,128)(2,1)} %get-tuple-element.20), channel_id=1, source_target_pairs={{0,2},{2,0},{1,3},{3,1},{4,6},{6,4},{5,7},{7,5},{8,10},{10,8},{9,1... | collective-permute-start | bytes 393224 | tf_op jit(solution)/shard_map/ppermute | solution.py:163
  8.0 12.2 %collective-permute-start.1 = (bf16[1,256,256]{2,1,0:T(8,128)(2,1)}, bf16[1,256,256]{2,1,0:T(8,128)(2,1)S(1)}, u32[]{:S(2)}, u32[]{:S(2)}) collective-permute-start(bf16[1,256,256]{2,1,0:T(8,128)(2,1)} %get-tuple-element.21), channel_id=1, source_target_pairs={{0,1},{1,0},{2,3},{3,2},{4,5},{5,4},{6,7},{7,6},{8,9},{9,8},{10,11... | collective-permute-start | bytes 393224 | tf_op jit(solution)/shard_map/ppermute | solution.py:160
  10.2 10.5 %collective-permute-start.3 = (bf16[1,256,256]{2,1,0:T(8,128)(2,1)S(1)}, bf16[1,256,256]{2,1,0:T(8,128)(2,1)S(1)}, u32[]{:S(2)}, u32[]{:S(2)}) collective-permute-start(bf16[1,256,256]{2,1,0:T(8,128)(2,1)S(1)} %collective-permute-done.2.rest_1_), channel_id=1, source_target_pairs={{0,1},{1,0},{2,3},{3,2},{4,5},{5,4},{6,7},{7,6},{8,9},{9,8},{10,11... | collective-permute-start | bytes 393224 | tf_op jit(solution)/shard_map/ppermute | solution.py:162
  18.7 3.4 %collective-permute-start.4 = (bf16[1,256,256]{2,1,0:T(8,128)(2,1)S(1)}, bf16[1,256,256]{2,1,0:T(8,128)(2,1)S(1)}, u32[]{:S(2)}, u32[]{:S(2)}) collective-permute-start(bf16[1,256,256]{2,1,0:T(8,128)(2,1)S(1)} %copy-done.3), channel_id=1, source_target_pairs={{0,1},{1,0},{2,3},{3,2},{4,5},{5,4},{6,7},{7,6},{8,9},{9,8},{10,11... | collective-permute-start | bytes 393224 | tf_op jit(solution)/shard_map/ppermute | solution.py:164
  20.2 5.9 %collective-permute-start.7 = (bf16[2,256,256]{2,1,0:T(8,128)(2,1)S(1)}, bf16[2,256,256]{2,1,0:T(8,128)(2,1)S(1)}, u32[]{:S(2)}, u32[]{:S(2)}) collective-permute-start(bf16[2,256,256]{2,1,0:T(8,128)(2,1)S(1)} %slice.30), channel_id=1, source_target_pairs={{0,1},{1,0},{2,3},{3,2},{4,5},{5,4},{6,7},{7,6},{8,9},{9,8},{10,11... | collective-permute-start | bytes 786440 | tf_op jit(solution)/shard_map/ppermute | solution.py:169
  20.2 2.6 %collective-permute-start.6 = (bf16[1,256,256]{2,1,0:T(8,128)(2,1)S(1)}, bf16[1,256,256]{2,1,0:T(8,128)(2,1)S(1)}, u32[]{:S(2)}, u32[]{:S(2)}) collective-permute-start(bf16[1,256,256]{2,1,0:T(8,128)(2,1)S(1)} %collective-permute-done.5.rest_4_), channel_id=1, source_target_pairs={{0,1},{1,0},{2,3},{3,2},{4,5},{5,4},{6,7},{7,6},{8,9},{9,8},{10,11... | collective-permute-start | bytes 393224 | tf_op jit(solution)/shard_map/ppermute | solution.py:170
  21.3 1.5 %collective-permute-start.11 = (bf16[2,256,128]{2,1,0:T(8,128)(2,1)S(1)}, bf16[2,256,128]{2,1,0:T(8,128)(2,1)S(1)}, u32[]{:S(2)}, u32[]{:S(2)}) collective-permute-start(bf16[2,256,128]{2,1,0:T(8,128)(2,1)S(1)} %shard_map.78.rest_7_), channel_id=1, source_target_pairs={{14,8},{12,10},{15,9},{13,11},{30,24},{28,26},{31,25},{29,27},{46,... | collective-permute-start | bytes 393224 | tf_op jit(solution)/shard_map/ppermute | solution.py:136
  22.0 4.1 %collective-permute-start.9 = (bf16[2,256,256]{2,1,0:T(8,128)(2,1)S(1)}, bf16[2,256,256]{2,1,0:T(8,128)(2,1)S(1)}, u32[]{:S(2)}, u32[]{:S(2)}) collective-permute-start(bf16[2,256,256]{2,1,0:T(8,128)(2,1)S(1)} %collective-permute-done.8.rest_7_), channel_id=1, source_target_pairs={{0,1},{1,0},{2,3},{3,2},{4,5},{5,4},{6,7},{7,6},{8,9},{9,8},{10,11... | collective-permute-start | bytes 786440 | tf_op jit(solution)/shard_map/ppermute | solution.py:171
  22.1 4.0 %collective-permute-start.10 = (bf16[2,256,128]{2,1,0:T(8,128)(2,1)S(1)}, bf16[2,256,128]{2,1,0:T(8,128)(2,1)S(1)}, u32[]{:S(2)}, u32[]{:S(2)}) collective-permute-start(bf16[2,256,128]{2,1,0:T(8,128)(2,1)S(1)} %shard_map.78.rest_7_), channel_id=1, source_target_pairs={{14,6},{12,4},{15,7},{13,5},{30,22},{28,20},{31,23},{29,21},{46,38... | collective-permute-start | bytes 393224 | tf_op jit(solution)/shard_map/ppermute | solution.py:136
  23.4 17.8 %copy-start.2 = (bf16[1,1,256,4,1,256]{5,3,4,2,1,0:T(4,128)(2,1)S(1)}, bf16[1,1,256,4,1,256]{5,3,4,2,1,0:T(4,128)(2,1)}, u32[]{:S(2)}) copy-start(bf16[1,1,256,4,1,256]{5,3,4,2,1,0:T(4,128)(2,1)} %param.8) | copy-start | bytes 1572868
  23.4 15.5 %collective-permute-start.13 = (bf16[2,256,128]{2,1,0:T(8,128)(2,1)S(1)}, bf16[2,256,128]{2,1,0:T(8,128)(2,1)S(1)}, u32[]{:S(2)}, u32[]{:S(2)}) collective-permute-start(bf16[2,256,128]{2,1,0:T(8,128)(2,1)S(1)} %shard_map.79.rest_13_), channel_id=1, source_target_pairs={{8,0},{10,2},{9,1},{11,3},{24,16},{26,18},{25,17},{27,19},{40,32},... | collective-permute-start | bytes 393224 | tf_op jit(solution)/shard_map/ppermute | solution.py:136
  24.8 14.1 %collective-permute-start.12 = (bf16[2,256,128]{2,1,0:T(8,128)(2,1)S(1)}, bf16[2,256,128]{2,1,0:T(8,128)(2,1)S(1)}, u32[]{:S(2)}, u32[]{:S(2)}) collective-permute-start(bf16[2,256,128]{2,1,0:T(8,128)(2,1)S(1)} %shard_map.79.rest_13_), channel_id=1, source_target_pairs={{8,6},{10,4},{14,0},{12,2},{9,7},{11,5},{15,1},{13,3},{24,22},{26,... | collective-permute-start | bytes 393224 | tf_op jit(solution)/shard_map/ppermute | solution.py:136
  39.9 8.5 %collective-permute-start.14 = (bf16[2,256,128]{2,1,0:T(8,128)(2,1)S(1)}, bf16[2,256,128]{2,1,0:T(8,128)(2,1)S(1)}, u32[]{:S(2)}, u32[]{:S(2)}) collective-permute-start(bf16[2,256,128]{2,1,0:T(8,128)(2,1)S(1)} %get-tuple-element.14.rest_11_), channel_id=1, source_target_pairs={{6,0},{4,2},{7,1},{5,3},{22,16},{20,18},{23,17},{21,19},{38,32},{3... | collective-permute-start | bytes 393224 | tf_op jit(solution)/shard_map/ppermute | solution.py:136
  41.3 25.0 %collective-permute-start.15 = (bf16[4,256,256]{2,1,0:T(8,128)(2,1)S(1)}, bf16[4,256,256]{2,1,0:T(8,128)(2,1)S(1)}, u32[]{:S(2)}, u32[]{:S(2)}) collective-permute-start(bf16[4,256,256]{2,1,0:T(8,128)(2,1)S(1)} %bitcast.30), channel_id=1, source_target_pairs={{0,1},{1,0},{2,3},{3,2},{4,5},{5,4},{6,7},{7,6},{8,9},{9,8},{10,11... | collective-permute-start | bytes 1572872 | tf_op jit(solution)/shard_map/ppermute | solution.py:172
